TPU v7x, 256 devices: a whole 4x4x8 slice. The times are simulated.
256 devices in a mesh: dp: 8 (over z), section: 2 (over core), space: 16 (over y, x).
Axes of the slice: x: 4, y: 4, z: 8, core: 2. Of those that a mesh axis runs over, the one named last changes fastest.
Arguments:
- latents: bfloat16 [32, 96, 192, 320], P('dp', 'space'), parts along dimension 0, may hold values from -16 to 16
- kernels: bfloat16 [2, 3, 3, 320, 320], P('section'), may hold values from -0.109375 to 0.109375
- norm_gain: float32 [2, 320], P('section'), may hold values from 0.25 to 1.75
- norm_bias: float32 [2, 320], P('section'), may hold values from -3 to 3
- conv_bias: float32 [2, 320], P('section'), may hold values from -3 to 3
Outputs:
- skips: bfloat16 [2, 32, 96, 192, 320], P('section', 'dp', 'space'), parts along dimension 1
There are 8 independent parts, one for each index of `dp`. A program takes and returns all parts, laid end to end along the dimension named above; an argument that names none is the same for every part. Nothing has to cross between parts.
All inputs are finite; a program needn't handle non-finite values.
Results may differ from a plain program's by a relative error of at most 0.01.
Values may be sent and summed in bfloat16 or wider, within the bound.
No kernel may reach another device: no remote copies, remote signals or barrier semaphores. Data moves between devices by JAX's collectives and lax.ppermute only.
A program may use at most 128 MiB of HBM per device.

v0:
```python
import jax
import jax.numpy as jnp
from jax import lax
from jax.sharding import PartitionSpec as P

GROUPS = 32


def sent_to_all(array, axis):
    copies = jnp.broadcast_to(array, (lax.axis_size(axis), *array.shape))
    return lax.all_to_all(copies, axis, split_axis=0, concat_axis=0, tiled=True)


def of_everyone(array, axis):
    return sent_to_all(array, axis).sum(axis=0)


def together(arrays, axis):
    flat, at, gathered = (jnp.concatenate([a.reshape(-1) for a in arrays]), 0, [])
    total = of_everyone(flat, axis)
    for a in arrays:
        gathered.append(total[at : at + a.size].reshape(a.shape))
        at += a.size
    return tuple(gathered)


def padded_2(array, sides, width):
    for axis, dim in sides:
        size, length = (lax.axis_size(axis), array.shape[dim])
        up = [(i, (i + 1) % size) for i in range(size - 1)]
        down = [(j, i) for i, j in up]
        last = lax.slice_in_dim(array, length - width, length, axis=dim)
        initial = lax.slice_in_dim(array, 0, width, axis=dim)
        before = lax.ppermute(last, axis, up)
        after = lax.ppermute(initial, axis, down)
        array = jnp.concatenate([before, array, after], axis=dim)
    return array


def group_moments(inputs):
    batch_count, local_rows, columns, channels = inputs.shape
    members = local_rows * lax.axis_size("space") * columns * (channels // GROUPS)
    values = inputs.astype(jnp.float32).reshape(
        batch_count, local_rows * columns, GROUPS, channels // GROUPS
    )
    totals, squares = together(
        (jnp.sum(values, axis=(1, 3)), jnp.sum(values * values, axis=(1, 3))), "space"
    )
    group_mean = totals / members
    group_var = jnp.maximum(squares / members - group_mean * group_mean, 0.0)
    return (group_mean, lax.rsqrt(group_var + 1e-05))


def apply_layer(inputs, kernel, norm_gain, norm_shift, shift_bias, residual):
    batch_count, local_rows, columns, channels = inputs.shape
    group_mean, inv_spread = group_moments(inputs)
    padded = padded_2(inputs, (("space", 1),), 1)
    values = padded.astype(jnp.float32).reshape(
        batch_count, local_rows + 2, columns, GROUPS, channels // GROUPS
    )
    scaled = (values - group_mean[:, None, None, :, None]) * inv_spread[:, None, None, :, None]
    scaled = scaled.reshape(batch_count, local_rows + 2, columns, channels) * norm_gain + norm_shift
    activated = jax.nn.silu(scaled)
    space_index = lax.axis_index("space")
    row_place = lax.broadcasted_iota(jnp.int32, (1, local_rows + 2, 1, 1), 1)
    outside = jnp.logical_or(
        jnp.logical_and(space_index == 0, row_place == 0),
        jnp.logical_and(space_index == lax.axis_size("space") - 1, row_place == local_rows + 1),
    )
    normed = jnp.where(outside, 0.0, activated).astype(jnp.bfloat16)
    convolved = lax.conv_general_dilated(
        normed,
        kernel,
        (1, 1),
        ((0, 0), (1, 1)),
        dimension_numbers=("NHWC", "HWIO", "NHWC"),
        preferred_element_type=jnp.float32,
    )
    return (residual + convolved + shift_bias).astype(jnp.bfloat16)


def on_device(latents, kernels, norm_gain, norm_bias, conv_bias):
    section_count = lax.axis_size("section")
    section_index = lax.axis_index("section")
    sample_count = latents.shape[0]
    per_section = sample_count // section_count
    own = lax.dynamic_slice_in_dim(latents, section_index * per_section, per_section, 0)
    all_kernels, all_gains, all_shifts, all_biases = (
        lax.all_gather(kernels, "section", axis=0, tiled=True),
        lax.all_gather(norm_gain.astype(jnp.bfloat16), "section", axis=0, tiled=True).astype(
            norm_gain.dtype
        ),
        lax.all_gather(norm_bias.astype(jnp.bfloat16), "section", axis=0, tiled=True).astype(
            norm_bias.dtype
        ),
        lax.all_gather(conv_bias.astype(jnp.bfloat16), "section", axis=0, tiled=True).astype(
            conv_bias.dtype
        ),
    )
    first = apply_layer(
        own,
        all_kernels[0],
        all_gains[0],
        all_shifts[0],
        all_biases[0],
        jnp.zeros(own.shape, jnp.float32),
    )
    second = apply_layer(
        first, all_kernels[1], all_gains[1], all_shifts[1], all_biases[1], own.astype(jnp.float32)
    )
    stacked = jnp.stack([first, second])
    return lax.all_to_all(stacked, "section", split_axis=0, concat_axis=1, tiled=True)


def solution(mesh):
    return jax.shard_map(
        on_device,
        mesh=mesh,
        in_specs=(
            P("dp", "space", None, None),
            P("section", None, None, None, None),
            P("section", None),
            P("section", None),
            P("section", None),
        ),
        out_specs=P("section", "dp", "space", None, None),
        check_vma=False,
    )
```

profile of v0, /device:TPU:1, one launch (start us, length us, event | category | flops | bytes accessed | tf_op | source)
XLA Modules:
  0.0 147.8 jit_solution(6580711174692724752)
XLA Ops:
  6.5 0.7 all-gather.5.cloned.1.call-update
  7.3 1.3 copy-done
  8.5 0.2 constant_dynamic-slice_fusion
  8.7 1.2 copy-done.2
  10.0 1.4 convert_reduce_fusion
  11.7 0.1 reduce_sum.69
  12.0 0.6 broadcast_in_dim.28
  12.7 7.6 %all-to-all-start = ((f32[16,1,128]{2,1,0:T(1,128)}), f32[16,1,128]{2,1,0:T(1,128)S(1)}, u32[]{:S(2)}, u32[]{:S(2)}) async-start(f32[16,1,128]{2,1,0:T(1,128)} %broadcast_in_dim.28), calls=%async_computation | async-start | bytes 16384 | tf_op jit(solution)/shard_map/all_to_all | solution.py:11
  20.3 2.6 %copy.102 = bf16[2,6,192,320]{3,1,2,0:T(8,128)(2,1)S(1)} copy(bf16[2,6,192,320]{3,2,1,0:T(8,128)(2,1)} %copy-done.2) | data formatting | bytes 2949120
  22.9 0.8 fusion.20
  23.7 0.8 copy.77
  24.4 3.3 %collective-permute-start = (bf16[2,1,192,320]{3,2,1,0:T(8,128)(2,1)}, bf16[2,1,192,320]{3,2,1,0:T(8,128)(2,1)S(1)}, u32[]{:S(2)}, u32[]{:S(2)}) collective-permute-start(bf16[2,1,192,320]{3,2,1,0:T(8,128)(2,1)} %copy.77), channel_id=1, source_target_pairs={{0,1},{1,2},{2,3},{3,4},{4,5},{5,6},{6,7},{7,8},{8,9},{9,10},{10,1... | collective-permute-start | bytes 737288 | tf_op jit(solution)/shard_map/ppermute | solution.py:34
  27.8 1.3 collective-permute-start.1
  29.1 3.0 %all-gather = bf16[2,1,320]{2,1,0:T(2,128)(2,1)S(1)} all-gather(bf16[1,1,320]{2,1,0:T(2,128)(2,1)S(1)} %convert_bitcast_fusion.2), channel_id=1, replica_groups=mesh['dp'=8,'section'=2,'space'=16] {'section'}, dimensions={0}, use_global_device_ids=true | all-gather | bytes 1920 | tf_op jit(solution)/shard_map/all_gather | solution.py:90
  32.1 1.9 %all-gather.1 = bf16[2,1,320]{2,1,0:T(2,128)(2,1)S(1)} all-gather(bf16[1,1,320]{2,1,0:T(2,128)(2,1)S(1)} %convert_bitcast_fusion.1), channel_id=1, replica_groups=mesh['dp'=8,'section'=2,'space'=16] {'section'}, dimensions={0}, use_global_device_ids=true | all-gather | bytes 1920 | tf_op jit(solution)/shard_map/all_gather | solution.py:93
  34.0 0.7 convert_bitcast_fusion
  34.7 2.0 %all-gather.2 = bf16[2,1,320]{2,1,0:T(2,128)(2,1)S(1)} all-gather(bf16[1,1,320]{2,1,0:T(2,128)(2,1)S(1)} %convert_bitcast_fusion), channel_id=1, replica_groups=mesh['dp'=8,'section'=2,'space'=16] {'section'}, dimensions={0}, use_global_device_ids=true | all-gather | bytes 1920 | tf_op jit(solution)/shard_map/all_gather | solution.py:96
  36.7 0.6 slice_reduce_fusion.4
  37.3 0.6 slice_reduce_fusion.3
  37.9 0.6 slice_reduce_fusion.2
  38.5 0.6 and_or_fusion
  39.4 0.1 mul.82
  39.6 0.1 sub.41
  39.7 0.5 copy.79
  40.2 1.4 copy.80
  41.6 4.4 %fusion.13 = bf16[8,2,192,320]{3,0,2,1:T(8,128)(2,1)S(1)} fusion(bf16[2,1,192,320]{3,1,2,0:T(2,128)(2,1)S(1)} %copy.80, bf16[2,6,192,320]{3,1,2,0:T(8,128)(2,1)S(1)} %copy.102, bf16[2,1,192,320]{3,1,2,0:T(2,128)(2,1)S(1)} %copy.79, f32[320]{0:T(512)} %get-tuple-element.12, f32[320]{0:T(512)} %get-tuple-element.10, f32[2,320]{1,0:T(2,128)S(1)} %mul.82, ...), kind=kLoop, calls=%fused_computation.24 | loop fusion | flops 15728640 | bytes 3939848 | tf_op jit(solution)/shard_map/convert_element_type | solution.py:70
  46.0 0.3 pad
  46.3 1.8 %fusion.5 = bf16[8,2,8,27,320]{4,0,3,2,1:T(8,128)(2,1)} fusion(bf16[8,2,7,2,320]{4,0,3,2,1:T(8,128)(2,1)S(1)} %slice.120, bf16[8,2,8,25,320]{4,0,3,2,1:T(8,128)(2,1)S(1)} %bitcast.67), kind=kLoop, calls=%fused_computation.16 | loop fusion | flops 6635520 | bytes 4403200 | tf_op jit(solution)/shard_map/conv_general_dilated | solution.py:71
  48.1 11.4 %convert_multiply_fusion.1 = (f32[6,16,25,320]{3,1,2,0:T(8,128)}, bf16[6,16,25,320]{3,1,2,0:T(8,128)(2,1)S(1)}) fusion(f32[320]{0:T(512)S(1)} %copy-done.7, bf16[2,3,3,320,320]{4,3,2,1,0:T(8,128)(2,1)} %all-gather.5.cloned.1.call-done, bf16[8,2,8,27,320]{4,0,3,2,1:T(8,128)(2,1)} %fusion.5, pred[16,25]{0,1:T(8,128)(4,1)S(1)} %copy-done.10), kind=kOutput, calls=%fused_computation.32 | convolution fusion | flops 4427520000 | bytes 9475728 | tf_op jit(solution)/shard_map/conv_general_dilated | solution.py:71
  59.5 2.8 %copy.91 = f32[6,16,25,320]{3,2,1,0:T(8,128)} copy(bf16[6,16,25,320]{3,1,2,0:T(8,128)(2,1)S(1)} %get-tuple-element.24) | data formatting | bytes 4608000 | tf_op jit(solution)/shard_map/convert_element_type | solution.py:43
  62.3 2.0 %copy.98 = bf16[6,16,25,320]{3,0,2,1:T(8,128)(2,1)} copy(bf16[6,16,25,320]{3,1,2,0:T(8,128)(2,1)S(1)} %get-tuple-element.24) | data formatting | bytes 3072000 | tf_op jit(solution)/shard_map/convert_element_type | solution.py:79
  64.3 4.8 %reshape.176 = f32[6,2,200,320]{3,2,1,0:T(8,128)} reshape(f32[6,16,25,320]{3,2,1,0:T(8,128)} %copy.91) | data formatting | bytes 6144000 | tf_op jit(solution)/shard_map/convert_element_type | solution.py:43
  69.1 2.3 %slice_reduce_fusion.1 = f32[2,320]{1,0:T(2,128)S(1)} fusion(f32[6,2,200,320]{3,2,1,0:T(8,128)} %reshape.176), kind=kLoop, calls=%fused_computation.15 | loop fusion | flops 736640 | bytes 2951680 | tf_op jit(solution)/shard_map/reduce_sum | solution.py:47
  71.4 0.1 reduce_sum.90
  71.7 5.4 %copy.92 = f32[6,16,25,320]{3,2,1,0:T(8,128)} copy(f32[6,16,25,320]{3,1,2,0:T(8,128)} %get-tuple-element.23) | data formatting | bytes 6144000 | tf_op jit(solution)/shard_map/mul | solution.py:47
  77.1 4.8 %reshape.178 = f32[6,2,200,320]{3,2,1,0:T(8,128)} reshape(f32[6,16,25,320]{3,2,1,0:T(8,128)} %copy.92) | data formatting | bytes 6144000 | tf_op jit(solution)/shard_map/mul | solution.py:47
  81.9 2.4 %slice_reduce_fusion = f32[2,320]{1,0:T(2,128)S(1)} fusion(f32[6,2,200,320]{3,2,1,0:T(8,128)} %reshape.178), kind=kLoop, calls=%fused_computation.14 | loop fusion | flops 736640 | bytes 2951680 | tf_op jit(solution)/shard_map/reduce_sum | solution.py:47
  84.7 0.6 broadcast_in_dim.29
  85.3 7.7 %all-to-all-start.1 = ((f32[16,1,128]{2,1,0:T(1,128)}), f32[16,1,128]{2,1,0:T(1,128)S(1)}, u32[]{:S(2)}, u32[]{:S(2)}) async-start(f32[16,1,128]{2,1,0:T(1,128)} %broadcast_in_dim.29), calls=%async_computation.1 | async-start | bytes 16384 | tf_op jit(solution)/shard_map/all_to_all | solution.py:11
  93.0 2.6 %slice_bitcast_fusion.5 = (bf16[1,2,6,192,320]{4,2,3,1,0:T(8,128)(2,1)}, bf16[2,6,192,320]{3,1,2,0:T(8,128)(2,1)}) fusion(bf16[6,2,200,320]{3,0,2,1:T(8,128)(2,1)S(1)} %bitcast.68), kind=kLoop, calls=%fused_computation.29 | loop fusion | bytes 4423680 | tf_op jit(solution)/shard_map/stack | solution.py:111
  95.7 0.2 reshape.172
  95.9 0.8 slice_bitcast_fusion.12
  96.6 3.5 %collective-permute-start.2 = (bf16[2,1,192,320]{3,2,1,0:T(8,128)(2,1)}, bf16[2,1,192,320]{3,2,1,0:T(8,128)(2,1)S(1)}, u32[]{:S(2)}, u32[]{:S(2)}) collective-permute-start(bf16[2,1,192,320]{3,2,1,0:T(8,128)(2,1)} %slice_bitcast_fusion.12), channel_id=1, source_target_pairs={{0,1},{1,2},{2,3},{3,4},{4,5},{5,6},{6,7},{7,8},{8,9},{9,10},{10,1... | collective-permute-start | bytes 737288 | tf_op jit(solution)/shard_map/ppermute | solution.py:34
  100.2 0.2 reshape.174
  100.4 0.8 slice_bitcast_fusion.11
  101.1 1.3 collective-permute-start.3
  102.8 0.1 mul.92
  103.0 0.1 sub.46
  103.1 2.6 %collective-permute-done.2 = bf16[2,1,192,320]{3,2,1,0:T(8,128)(2,1)S(1)} collective-permute-done((bf16[2,1,192,320]{3,2,1,0:T(8,128)(2,1)}, bf16[2,1,192,320]{3,2,1,0:T(8,128)(2,1)S(1)}, u32[]{:S(2)}, u32[]{:S(2)}) %collective-permute-start.2) | collective-permute-done | bytes 245792 | tf_op jit(solution)/shard_map/ppermute | solution.py:34
  105.7 0.5 copy.89
  106.1 4.6 %collective-permute-done.3 = bf16[2,1,192,320]{3,2,1,0:T(8,128)(2,1)} collective-permute-done((bf16[2,1,192,320]{3,2,1,0:T(8,128)(2,1)}, bf16[2,1,192,320]{3,2,1,0:T(8,128)(2,1)}, u32[]{:S(2)}, u32[]{:S(2)}) %collective-permute-start.3) | collective-permute-done | bytes 245792 | tf_op jit(solution)/shard_map/ppermute | solution.py:35
  110.7 1.4 copy.90
  112.2 4.5 %fusion.14 = bf16[8,2,192,320]{3,0,2,1:T(8,128)(2,1)S(1)} fusion(bf16[2,1,192,320]{3,1,2,0:T(2,128)(2,1)S(1)} %copy.90, bf16[2,6,192,320]{3,1,2,0:T(8,128)(2,1)S(1)} %copy-done.6, bf16[2,1,192,320]{3,1,2,0:T(2,128)(2,1)S(1)} %copy.89, f32[320]{0:T(512)} %get-tuple-element.11, f32[320]{0:T(512)S(1)} %get-tuple-element.9, f32[2,320]{1,0:T(2,128)S(1)} %mul.92, ...), kind=kLoop, calls=%fused_computation.25 | loop fusion | flops 15728640 | bytes 3939848 | tf_op jit(solution)/shard_map/convert_element_type | solution.py:70
  116.7 0.3 pad.2
  117.0 0.3 fusion.6
  117.3 0.3 slice-done.1
  117.7 7.7 %broadcast_select_fusion = f32[6,16,25,320]{3,1,2,0:T(8,128)S(1)} fusion(pred[16,25]{0,1:T(8,128)(4,1)S(1)} %copy-done.11, bf16[2,3,3,320,320]{4,3,2,1,0:T(8,128)(2,1)S(1)} %bitcast.72, bf16[8,2,8,27,320]{4,0,3,2,1:T(8,128)(2,1)S(1)} %fusion.6), kind=kOutput, calls=%fused_computation.31 | convolution fusion | flops 4424448000 | bytes 7942144 | tf_op jit(solution)/shard_map/conv_general_dilated | solution.py:71
  125.4 1.2 copy.99
  126.6 0.3 copy-done.3
  126.9 1.6 %fusion.15 = bf16[1,2,6,192,320]{4,2,3,1,0:T(8,128)(2,1)S(1)} fusion(f32[6,2,200,320]{3,0,2,1:T(8,128)S(1)} %bitcast.62, f32[320]{0:T(512)S(1)} %get-tuple-element.7, bf16[2,6,192,320]{3,2,1,0:T(8,128)(2,1)S(1)} %copy-done.3), kind=kLoop, calls=%fused_computation.26 | loop fusion | flops 2949120 | bytes 5899520 | tf_op jit(solution)/shard_map/stack | solution.py:111
  128.5 1.4 pad_maximum_fusion
  130.0 0.6 copy.97
  130.6 8.5 %all_to_all.24 = bf16[2,2,6,192,320]{4,3,2,1,0:T(8,128)(2,1)S(1)} all-to-all(bf16[2,2,6,192,320]{4,3,2,1,0:T(8,128)(2,1)S(1)} %copy.97), channel_id=1, replica_groups=mesh['dp'=8,'section'=2,'space'=16] {'section'}, dimensions={0} | all-to-all | bytes 5898240 | tf_op jit(solution)/shard_map/all_to_all | solution.py:112
  139.1 1.8 %copy.121 = bf16[1,4,6,192,320]{4,3,2,1,0:T(8,128)(2,1)} copy(bf16[1,4,6,192,320]{4,3,2,1,0:T(8,128)(2,1)S(1)} %bitcast.63) | data formatting | bytes 5898240
  (68 shorter events, 2.4 us)
Async XLA Ops:
  6.5 2.0 %copy-start = (bf16[4,6,192,320]{3,2,1,0:T(8,128)(2,1)S(1)}, bf16[4,6,192,320]{3,2,1,0:T(8,128)(2,1)}, u32[]{:S(2)}) copy-start(bf16[4,6,192,320]{3,2,1,0:T(8,128)(2,1)} %param.5) | copy-start | bytes 8847364
  6.5 41.6 %all-gather.5.cloned.1.call-start = ((), (), s32[]{:S(2)}) async-start(), calls=%async_computation.3 | async-start | bytes 6635520 | tf_op jit(solution)/shard_map/all_gather | solution.py:89
  8.7 1.2 copy-start.2
  12.7 26.4 %all-to-all-start = ((f32[16,1,128]{2,1,0:T(1,128)}), f32[16,1,128]{2,1,0:T(1,128)S(1)}, u32[]{:S(2)}, u32[]{:S(2)}) async-start(f32[16,1,128]{2,1,0:T(1,128)} %broadcast_in_dim.28), calls=%async_computation | async-start | bytes 16384 | tf_op jit(solution)/shard_map/all_to_all | solution.py:11
  20.2 8.8 %copy-start.8 = (f32[1,320]{1,0:T(1,128)S(1)}, f32[1,320]{1,0:T(1,128)}, u32[]{:S(2)}) copy-start(f32[1,320]{1,0:T(1,128)} %param.7) | copy-start | bytes 3844
  20.3 11.9 %copy-start.9 = (f32[1,320]{1,0:T(1,128)S(1)}, f32[1,320]{1,0:T(1,128)}, u32[]{:S(2)}) copy-start(f32[1,320]{1,0:T(1,128)} %param.8) | copy-start | bytes 3844
  24.4 15.3 %collective-permute-start = (bf16[2,1,192,320]{3,2,1,0:T(8,128)(2,1)}, bf16[2,1,192,320]{3,2,1,0:T(8,128)(2,1)S(1)}, u32[]{:S(2)}, u32[]{:S(2)}) collective-permute-start(bf16[2,1,192,320]{3,2,1,0:T(8,128)(2,1)} %copy.77), channel_id=1, source_target_pairs={{0,1},{1,2},{2,3},{3,4},{4,5},{5,6},{6,7},{7,8},{8,9},{9,10},{10,1... | collective-permute-start | bytes 737288 | tf_op jit(solution)/shard_map/ppermute | solution.py:34
  27.8 12.4 %collective-permute-start.1 = (bf16[2,1,192,320]{3,2,1,0:T(8,128)(2,1)S(1)}, bf16[2,1,192,320]{3,2,1,0:T(8,128)(2,1)}, u32[]{:S(2)}, u32[]{:S(2)}) collective-permute-start(bf16[2,1,192,320]{3,2,1,0:T(8,128)(2,1)S(1)} %copy.78), channel_id=1, source_target_pairs={{1,0},{2,1},{3,2},{4,3},{5,4},{6,5},{7,6},{8,7},{9,8},{10,9},{11,1... | collective-permute-start | bytes 737288 | tf_op jit(solution)/shard_map/ppermute | solution.py:35
  46.3 1.8 %copy-start.7 = (f32[320]{0:T(512)S(1)}, f32[320]{0:T(512)}, u32[]{:S(2)}) copy-start(f32[320]{0:T(512)} %get-tuple-element.8) | copy-start | bytes 3844
  46.3 1.8 %copy-start.10 = (pred[16,25]{0,1:T(8,128)(4,1)S(1)}, pred[16,25]{0,1:T(8,128)(4,1)}, u32[]{:S(2)}) copy-start(pred[16,25]{0,1:T(8,128)(4,1)} %constant.48) | copy-start | bytes 1204
  81.9 11.1 %copy-start.4 = (bf16[6,16,25,320]{3,0,2,1:T(8,128)(2,1)S(1)}, bf16[6,16,25,320]{3,0,2,1:T(8,128)(2,1)}, u32[]{:S(2)}) copy-start(bf16[6,16,25,320]{3,0,2,1:T(8,128)(2,1)} %copy.98) | copy-start | bytes 4608004
  85.3 17.1 %all-to-all-start.1 = ((f32[16,1,128]{2,1,0:T(1,128)}), f32[16,1,128]{2,1,0:T(1,128)S(1)}, u32[]{:S(2)}, u32[]{:S(2)}) async-start(f32[16,1,128]{2,1,0:T(1,128)} %broadcast_in_dim.29), calls=%async_computation.1 | async-start | bytes 16384 | tf_op jit(solution)/shard_map/all_to_all | solution.py:11
  95.6 16.5 %copy-start.6 = (bf16[2,6,192,320]{3,1,2,0:T(8,128)(2,1)S(1)}, bf16[2,6,192,320]{3,1,2,0:T(8,128)(2,1)}, u32[]{:S(2)}) copy-start(bf16[2,6,192,320]{3,1,2,0:T(8,128)(2,1)} %get-tuple-element.14) | copy-start | bytes 4423684
  96.6 9.0 %collective-permute-start.2 = (bf16[2,1,192,320]{3,2,1,0:T(8,128)(2,1)}, bf16[2,1,192,320]{3,2,1,0:T(8,128)(2,1)S(1)}, u32[]{:S(2)}, u32[]{:S(2)}) collective-permute-start(bf16[2,1,192,320]{3,2,1,0:T(8,128)(2,1)} %slice_bitcast_fusion.12), channel_id=1, source_target_pairs={{0,1},{1,2},{2,3},{3,4},{4,5},{5,6},{6,7},{7,8},{8,9},{9,10},{10,1... | collective-permute-start | bytes 737288 | tf_op jit(solution)/shard_map/ppermute | solution.py:34
  101.1 9.6 %collective-permute-start.3 = (bf16[2,1,192,320]{3,2,1,0:T(8,128)(2,1)}, bf16[2,1,192,320]{3,2,1,0:T(8,128)(2,1)}, u32[]{:S(2)}, u32[]{:S(2)}) collective-permute-start(bf16[2,1,192,320]{3,2,1,0:T(8,128)(2,1)} %slice_bitcast_fusion.11), channel_id=1, source_target_pairs={{1,0},{2,1},{3,2},{4,3},{5,4},{6,5},{7,6},{8,7},{9,8},{10,9},{11,1... | collective-permute-start | bytes 737288 | tf_op jit(solution)/shard_map/ppermute | solution.py:35
  112.1 5.1 %slice-start = ((s8[4423680]{0:T(1024)(128)(4,1)}), s8[4194304]{0:T(1024)(128)(4,1)S(1)}, s32[]{:S(2)}) async-start(s8[4423680]{0:T(1024)(128)(4,1)} %bitcast.71), calls=%async_computation.4 | async-start | bytes 8388608
  116.7 0.9 slice-start.1
  117.0 0.7 copy-start.11
  125.4 1.5 copy-start.3
  126.9 1.7 %copy-start.5 = (bf16[1,2,6,192,320]{4,2,3,1,0:T(8,128)(2,1)S(1)}, bf16[1,2,6,192,320]{4,2,3,1,0:T(8,128)(2,1)}, u32[]{:S(2)}) copy-start(bf16[1,2,6,192,320]{4,2,3,1,0:T(8,128)(2,1)} %get-tuple-element.13) | copy-start | bytes 4423684
  130.6 10.3 %copy-start.1 = (bf16[4,6,192,320]{3,2,1,0:T(8,128)(2,1)S(1)}, bf16[4,6,192,320]{3,2,1,0:T(8,128)(2,1)}, u32[]{:S(2)}) copy-start(bf16[4,6,192,320]{3,2,1,0:T(8,128)(2,1)} %param.5) | copy-start | bytes 8847364
Sparse Core Ops, SparseCore 0:
  9.1 23.8 all-gather.4
where the time goes:
time: 150 us; the launch traced here: 148 us
  local copies, waits for them, and re-layouts  44.9 us (30%)
  starting transfers between devices  24.6 us (16%)
  other arithmetic  22.1 us (15%)
  matrix products  19.1 us (13%)
  blocking collectives  15.4 us (10%)
  between operations  13.8 us (9%)
  waiting for transfers between devices  7.89 us (5%)
    conv_general_dilated x2, matrix products, apply_layer(): lax.conv_general_dilated(normed, kernel, (1, 1), ((0, 0), (1, 1)), dimens...  19.1 us
    all_to_all x2, starting transfers between devices, sent_to_all(): return lax.all_to_all(copies, axis, split_axis=0, concat_axis=0, tiled=True)  15.3 us
    mul x2, local copies, waits for them, and re-layouts, group_moments(): values * values  10.2 us
    convert_element_type x2, other arithmetic, apply_layer(): normed = jnp.where(outside, 0.0, activated).astype(jnp.bfloat16)  8.89 us
    all_to_all x1, blocking collectives, on_device(): lax.all_to_all(stacked, 'section', split_axis=0, concat_axis=1, tiled=True)  8.51 us
    unnamed x30, local copies, waits for them, and re-layouts  7.69 us
    convert_element_type x2, local copies, waits for them, and re-layouts, group_moments(): inputs.astype(jnp.float32)  7.6 us
    ppermute x2, starting transfers between devices, padded_2(): before = lax.ppermute(last, axis, up)  6.76 us
  transfers between devices with their start and end apart: 7, of which 2 were waited for; matrix products, arithmetic and copies ran while one was open for 17% of the time, Pallas kernels for 0%

commit v1 on v0

v1 whole, which is shorter than its diff:
```python
import jax
import jax.numpy as jnp
from jax import lax
from jax.experimental import pallas as pl
from jax.experimental.pallas import tpu as pltpu
from jax.sharding import PartitionSpec as P

GROUPS = 32
F32 = jnp.float32
BF16 = jnp.bfloat16
ANY = pl.BlockSpec(memory_space=pl.ANY)
VM = pl.BlockSpec(memory_space=pltpu.VMEM)


def one_hot(shape, channel_dim, per_group):
    channel = lax.broadcasted_iota(jnp.int32, shape, channel_dim)
    group = lax.broadcasted_iota(jnp.int32, shape, 1 - channel_dim)
    low = group * per_group
    return jnp.where((channel >= low) & (channel < low + per_group), 1.0, 0.0).astype(BF16)


def exact_dot(values, selector):
    high = values.astype(BF16)
    rest = values - high.astype(F32)
    middle = rest.astype(BF16)
    low = (rest - middle.astype(F32)).astype(BF16)
    return (
        jnp.dot(high, selector, preferred_element_type=F32)
        + jnp.dot(middle, selector, preferred_element_type=F32)
        + jnp.dot(low, selector, preferred_element_type=F32)
    )


def send_group_sums(sums, stats_out, per_group):
    channels = sums.shape[1]
    grouped = exact_dot(sums, one_hot((channels, 128), 0, per_group))
    for i in range(stats_out.shape[0]):
        stats_out[i] = grouped


def fold_rows(block):
    return block.reshape(block.shape[0] // 8, 8, block.shape[1]).sum(axis=0)


def stats_kernel(x_any, stats_out, ha_out, hb_out, x_buf, sem, sem_out):
    n, rows, cols, ch = x_buf.shape
    sec = lax.axis_index("section")
    even = lax.axis_index("space") % 2 == 0
    loads = []
    for s in range(n):
        cp = pltpu.make_async_copy(x_any.at[sec * n + s], x_buf.at[s], sem.at[s])
        cp.start()
        loads.append(cp)
    total = []
    row_a = jnp.where(even, rows - 1, 0)
    sends = []
    for s in range(n):
        loads[s].wait()
        for k, (dst, row) in enumerate(((ha_out, row_a), (hb_out, rows - 1 - row_a))):
            cp = pltpu.make_async_copy(x_buf.at[s, row], dst.at[s], sem_out.at[2 * s + k])
            cp.start()
            sends.append(cp)

        def step(r, carry):
            acc, sq = carry
            v = x_buf[s, r].astype(F32)
            return acc + fold_rows(v), sq + fold_rows(v * v)

        zero = jnp.zeros((8, ch), F32)
        acc, sq = lax.fori_loop(0, rows, step, (zero, zero))
        total += [acc.sum(axis=0, keepdims=True), sq.sum(axis=0, keepdims=True)]
    sums = jnp.concatenate(total + [jnp.zeros((8 - len(total), ch), F32)], axis=0)
    send_group_sums(sums, stats_out, ch // GROUPS)
    for cp in sends:
        cp.wait()


def weight_kernel(own_ref, other_ref, w0_ref, w1_ref):
    sec = lax.axis_index("section")

    def lay_out(src, dst):
        ch = src.shape[-1]
        rem = ch - 256
        for dr in range(3):
            for dc in range(3):
                dst[dr * 256 : dr * 256 + 256, dc * 256 : dc * 256 + 256] = src[0, dr, dc, 0:256, 0:256]
                dst[768 + dr * rem : 768 + dr * rem + rem, dc * 256 : dc * 256 + 256] = src[
                    0, dr, dc, 256:ch, 0:256
                ]
            right = [src[0, dr, dc, :, 256:ch].astype(F32) for dc in range(3)]
            right = jnp.concatenate(right + [jnp.zeros((ch, 256 - 3 * rem), F32)], axis=1).astype(BF16)
            dst[dr * 256 : dr * 256 + 256, 768:1024] = right[0:256]
            dst[768 + dr * rem : 768 + dr * rem + rem, 768:1024] = right[256:ch]
        dst[768 + 3 * rem : 1024, :] = jnp.zeros((256 - 3 * rem, 1024), BF16)

    @pl.when(sec == 0)
    def _():
        lay_out(own_ref, w0_ref)
        lay_out(other_ref, w1_ref)

    @pl.when(sec != 0)
    def _():
        lay_out(other_ref, w0_ref)
        lay_out(own_ref, w1_ref)


def conv_kernel(index, members, n_space, chunk_rows, *refs):
    if index == 0:
        (x_any, ra_any, rb_any, stats_ref, own_p, other_p, w_ref,
         y_out, stats_out, ha_out, hb_out,
         x_buf, xm, xr, rem_buf, z_buf, y_buf, sem) = refs
    else:
        (x_any, ra_any, rb_any, stats_ref, own_p, other_p, w_ref, lat_any, first_other,
         y_out, full_out,
         x_buf, xm, xr, rem_buf, z_buf, y_buf, lat_buf, sem) = refs
    n, padded_rows, cols, ch = x_buf.shape
    rows = padded_rows - 2
    rem = ch - 256
    sec = lax.axis_index("section")
    space = lax.axis_index("space")
    even = space % 2 == 0
    slot_a = jnp.where(even, rows + 1, 0)
    loads = []
    for s in range(n):
        src = x_any.at[sec * n + s] if index == 0 else x_any.at[s]
        group = [
            pltpu.make_async_copy(ra_any.at[s], x_buf.at[s, slot_a], sem.at[0, s]),
            pltpu.make_async_copy(rb_any.at[s], x_buf.at[s, rows + 1 - slot_a], sem.at[1, s]),
            pltpu.make_async_copy(src, x_buf.at[s, pl.ds(1, rows)], sem.at[2, s]),
        ]
        if index == 1:
            group.append(pltpu.make_async_copy(lat_any.at[sec * n + s], lat_buf.at[s], sem.at[3, s]))
        for cp in group:
            cp.start()
        loads.append(group)
    if index == 1:
        keep_own = pltpu.make_async_copy(x_any, full_out.at[pl.ds(0, n)], sem.at[5, 0])
        keep_other = pltpu.make_async_copy(first_other, full_out.at[pl.ds(n, n)], sem.at[5, 1])

        @pl.when(sec == 0)
        def _():
            keep_own.start()
            keep_other.start()

    params = jnp.where(sec == index, own_p[...], other_p[...])
    gain, shift, bias = params[0:1], params[1:2], params[2:3]
    total = stats_ref[0]
    for i in range(1, n_space):
        total = total + stats_ref[i]
    packed = []
    for s in range(n):
        mean = total[2 * s : 2 * s + 1] * (1.0 / members)
        var = jnp.maximum(total[2 * s + 1 : 2 * s + 2] * (1.0 / members) - mean * mean, 0.0)
        packed += [mean, lax.rsqrt(var + 1e-05)]
    packed = jnp.concatenate(packed + [jnp.zeros((8 - 2 * n, 128), F32)], axis=0)
    spread = exact_dot(packed, one_hot((128, ch), 1, ch // GROUPS))

    if index == 0:
        acc = [[jnp.zeros((8, ch), F32) for _ in range(2)] for _ in range(n)]
    stores = []
    for s in range(n):
        for cp in loads[s]:
            cp.wait()
        half_a = 0.5 * (spread[2 * s + 1 : 2 * s + 2] * gain)
        half_b = 0.5 * shift - spread[2 * s : 2 * s + 1] * half_a
        for j in range(padded_rows):
            half = x_buf[s, j].astype(F32) * half_a + half_b
            y = half + half * jnp.tanh(half)
            if j == 0:
                y = jnp.where(space == 0, 0.0, y)
            if j == padded_rows - 1:
                y = jnp.where(space == n_space - 1, 0.0, y)
            xm[s, pl.ds(j * cols, cols), :] = y[:, 0:256].astype(BF16)
            rem_buf[j] = y[:, 256:ch]
            if j >= 2:
                parts = [rem_buf[j - 2], rem_buf[j - 1], rem_buf[j], jnp.zeros((cols, 256 - 3 * rem), F32)]
                xr[s, pl.ds((j - 2) * cols, cols), :] = jnp.concatenate(parts, axis=1).astype(BF16)
        for r0 in range(0, rows, chunk_rows):
            m = chunk_rows * cols
            lhs = jnp.concatenate(
                [xm[s, pl.ds((r0 + dr) * cols, m), :] for dr in range(3)] + [xr[s, pl.ds(r0 * cols, m), :]],
                axis=1,
            )
            slot = (r0 // chunk_rows) % 2
            z_buf[slot] = jnp.dot(lhs, w_ref[...], preferred_element_type=F32)
            first_slab = lax.broadcasted_iota(jnp.int32, (8, 256), 0) == 0
            last_slab = lax.broadcasted_iota(jnp.int32, (8, 256), 0) == 7
            for r in range(chunk_rows):
                at = pl.ds(r * cols, cols)

                def down(z, width):
                    moved = pltpu.roll(z, 1, 0)
                    head = jnp.where(first_slab[:, :width], 0.0, moved[0:8])
                    return jnp.concatenate([head, moved[8:]], axis=0)

                def up(z, width):
                    moved = pltpu.roll(z, cols - 1, 0)
                    tail = jnp.where(last_slab[:, :width], 0.0, moved[cols - 8 :])
                    return jnp.concatenate([moved[: cols - 8], tail], axis=0)

                main = z_buf[slot, at, 256:512] + down(z_buf[slot, at, 0:256], 256) + up(z_buf[slot, at, 512:768], 256)
                left = z_buf[slot, at, 768:896]
                right = z_buf[slot, at, 896:1024]
                side = down(left, 128) + pltpu.roll(left, 64, 1) + up(right, 128)
                out = jnp.concatenate([main, side[:, 0:rem]], axis=1) + bias
                if index == 1:
                    out = out + lat_buf[s, r0 + r].astype(F32)
                rounded = out.astype(BF16)
                y_buf[s, r0 + r] = rounded
                if index == 0:
                    back = rounded.astype(F32)
                    acc[s][0] = acc[s][0] + fold_rows(back)
                    acc[s][1] = acc[s][1] + fold_rows(back * back)
        cp = pltpu.make_async_copy(y_buf.at[s], y_out.at[s], sem.at[4, s])
        cp.start()
        stores.append(cp)
        if index == 0:
            for k, (dst, row) in enumerate(((ha_out, slot_a), (hb_out, rows + 1 - slot_a))):
                cp = pltpu.make_async_copy(
                    y_buf.at[s, jnp.clip(row - 1, 0, rows - 1)], dst.at[s], sem.at[5 + k, s]
                )
                cp.start()
                stores.append(cp)
        else:
            keep_new = pltpu.make_async_copy(y_buf.at[s], full_out.at[n + s], sem.at[6, s])

            @pl.when(sec != 0)
            def _():
                keep_new.start()

    if index == 0:
        rows_out = []
        for s in range(n):
            rows_out += [v.sum(axis=0, keepdims=True) for v in acc[s]]
        sums = jnp.concatenate(rows_out + [jnp.zeros((8 - 2 * n, ch), F32)], axis=0)
        send_group_sums(sums, stats_out, ch // GROUPS)
    for cp in stores:
        cp.wait()
    if index == 1:

        @pl.when(sec == 0)
        def _():
            keep_own.wait()
            keep_other.wait()

        @pl.when(sec != 0)
        def _():
            for s in range(n):
                pltpu.make_async_copy(y_buf.at[s], full_out.at[n + s], sem.at[6, s]).wait()


def finish_kernel(full_in, second_other, full_out, sem):
    n = second_other.shape[0]
    cp = pltpu.make_async_copy(second_other, full_out.at[pl.ds(0, n)], sem)

    @pl.when(lax.axis_index("section") != 0)
    def _():
        cp.start()
        cp.wait()


def swap(array):
    return lax.ppermute(array, "section", [(0, 1), (1, 0)])


def on_device(latents, kernels, norm_gain, norm_bias, conv_bias):
    samples, rows, cols, ch = latents.shape
    n = samples // lax.axis_size("section")
    n_space = lax.axis_size("space")
    members = rows * n_space * cols * (ch // GROUPS)
    pairs_a = [(i, i ^ 1) for i in range(n_space)]
    pairs_b = [(i, (i - 1) % n_space if i % 2 == 0 else (i + 1) % n_space) for i in range(n_space)]
    shape = jax.ShapeDtypeStruct
    stats_shape = shape((n_space, 8, 128), F32)
    edge_shape = shape((n, cols, ch), BF16)
    part_shape = shape((n, rows, cols, ch), BF16)
    limit = pltpu.CompilerParams(vmem_limit_bytes=40 * 1024 * 1024)

    own_p = jnp.concatenate([norm_gain, norm_bias, conv_bias], axis=0)
    other_p = swap(own_p)
    other_k = swap(kernels)

    stats, ha, hb = pl.pallas_call(
        stats_kernel,
        out_shape=(stats_shape, edge_shape, edge_shape),
        in_specs=[ANY],
        out_specs=(VM, ANY, ANY),
        scratch_shapes=[
            pltpu.VMEM((n, rows, cols, ch), BF16),
            pltpu.SemaphoreType.DMA((n,)),
            pltpu.SemaphoreType.DMA((2 * n,)),
        ],
        compiler_params=limit,
        name="stats",
    )(latents)
    ra = lax.ppermute(ha, "space", pairs_a)
    rb = lax.ppermute(hb, "space", pairs_b)
    stats = lax.all_to_all(stats, "space", split_axis=0, concat_axis=0, tiled=True)

    w_shape = shape((1024, 1024), BF16)
    w0, w1 = pl.pallas_call(
        weight_kernel,
        out_shape=(w_shape, w_shape),
        in_specs=[VM, VM],
        out_specs=(VM, VM),
        compiler_params=limit,
        name="weights",
    )(kernels, other_k)

    chunk_rows = 2

    def conv(index, operands, out_shape, out_specs, extra):
        body = lambda *refs: conv_kernel(index, members, n_space, chunk_rows, *refs)
        return pl.pallas_call(
            body,
            out_shape=out_shape,
            in_specs=[ANY, ANY, ANY, VM, VM, VM, VM] + [ANY] * (len(operands) - 7),
            out_specs=out_specs,
            scratch_shapes=[
                pltpu.VMEM((n, rows + 2, cols, ch), BF16),
                pltpu.VMEM((n, (rows + 2) * cols, 256), BF16),
                pltpu.VMEM((n, rows * cols, 256), BF16),
                pltpu.VMEM((rows + 2, cols, ch - 256), F32),
                pltpu.VMEM((2, chunk_rows * cols, 1024), F32),
                pltpu.VMEM((n, rows, cols, ch), BF16),
                *extra,
                pltpu.SemaphoreType.DMA((7, n)),
            ],
            compiler_params=limit,
            name="conv%d" % index,
        )(*operands)

    first, stats, ha, hb = conv(
        0,
        (latents, ra, rb, stats, own_p, other_p, w0),
        (part_shape, stats_shape, edge_shape, edge_shape),
        (ANY, VM, ANY, ANY),
        (),
    )
    ra = lax.ppermute(ha, "space", pairs_a)
    rb = lax.ppermute(hb, "space", pairs_b)
    first_other = swap(first)
    stats = lax.all_to_all(stats, "space", split_axis=0, concat_axis=0, tiled=True)
    full_shape = shape((samples, rows, cols, ch), BF16)
    second, full = conv(
        1,
        (first, ra, rb, stats, own_p, other_p, w1, latents, first_other),
        (part_shape, full_shape),
        (ANY, ANY),
        (pltpu.VMEM((n, rows, cols, ch), BF16),),
    )
    second_other = swap(second)
    full = pl.pallas_call(
        finish_kernel,
        out_shape=full_shape,
        in_specs=[ANY, ANY],
        out_specs=ANY,
        scratch_shapes=[pltpu.SemaphoreType.DMA],
        input_output_aliases={0: 0},
        name="finish",
    )(full, second_other)
    return full[None]


def solution(mesh):
    return jax.shard_map(
        on_device,
        mesh=mesh,
        in_specs=(
            P("dp", "space", None, None),
            P("section", None, None, None, None),
            P("section", None),
            P("section", None),
            P("section", None),
        ),
        out_specs=P("section", "dp", "space", None, None),
        check_vma=False,
    )
```

time: 150 us -> 119 us (0.79); the launches traced: 148 us -> 119 us
  Pallas kernels: 0 us -> 77.3 us
  local copies, waits for them, and re-layouts: 44.9 us -> 9.44 us
  other arithmetic: 22.1 us -> 0.01 us
  matrix products: 19.1 us -> 0 us
  between operations: 13.8 us -> 0.31 us
  blocking collectives: 15.4 us -> 9.5 us
  starting transfers between devices: 24.6 us -> 18.8 us
  waiting for transfers between devices: 7.89 us -> 3.34 us
    pallas_call x0 -> x5, Pallas kernels: none -> 77.3 us  [the longest x1 54.7 us: on_device(): pl.pallas_call(finish_kernel, out_shape=full_shape, in_specs=[ANY, ANY],...]
    conv_general_dilated x2 -> x0, matrix products: 19.1 us -> none  [apply_layer(): lax.conv_general_dilated(normed, kernel, (1, 1), ((0, 0), (1, 1)), dimens...]
    all_to_all x2 -> x1, starting transfers between devices: 15.3 us -> 4.15 us  [on_device(): lax.all_to_all(stats, 'space', split_axis=0, concat_axis=0, tiled=True)]
    mul x6 -> x0, local copies, waits for them, and re-layouts: 10.6 us -> none  [the longest x2 10.2 us: group_moments(): values * values]
    convert_element_type x10 -> x0, local copies, waits for them, and re-layouts: 10.6 us -> none  [the longest x2 7.6 us: group_moments(): inputs.astype(jnp.float32)]
    convert_element_type x5 -> x0, other arithmetic: 8.9 us -> none  [the longest x2 8.89 us: apply_layer(): normed = jnp.where(outside, 0.0, activated).astype(jnp.bfloat16)]
    all_gather x3 -> x0, blocking collectives: 6.85 us -> none  [the longest x1 3 us: on_device(): lax.all_gather(norm_gain.astype(jnp.bfloat16), 'section', axis=0, tiled=T...]
    reduce_sum x9 -> x0, other arithmetic: 6.49 us -> none  [the longest x4 3.87 us: group_moments(): jnp.sum(values, axis=(1, 3))]
  transfers between devices with their start and end apart: 7 -> 9, of which waited for: 2 -> 1; matrix products, arithmetic and copies ran while one was open for 17% -> 0% of each run, Pallas kernels for 0% -> 4%
where the time goes in v1:
time: 119 us
  Pallas kernels  77.3 us (65%)
  starting transfers between devices  18.8 us (16%)
  blocking collectives  9.5 us (8%)
  local copies, waits for them, and re-layouts  9.44 us (8%)
  waiting for transfers between devices  3.34 us (3%)
    pallas_call x1, Pallas kernels, on_device(): pl.pallas_call(finish_kernel, out_shape=full_shape, in_specs=[ANY, ANY],...  54.7 us
    pallas_call x2, Pallas kernels, conv(): pl.pallas_call(body, out_shape=out_shape, in_specs=[ANY, ANY, ANY, VM, VM...  18.4 us
    all_to_all x1, blocking collectives, on_device(): lax.all_to_all(stats, 'space', split_axis=0, concat_axis=0, tiled=True)  9.5 us
    unnamed x22, local copies, waits for them, and re-layouts  9.44 us
    ppermute x2, starting transfers between devices, on_device(): rb = lax.ppermute(hb, 'space', pairs_b)  7.73 us
    ppermute x4, starting transfers between devices, swap(): return lax.ppermute(array, 'section', [(0, 1), (1, 0)])  6.14 us
    all_to_all x1, starting transfers between devices, on_device(): lax.all_to_all(stats, 'space', split_axis=0, concat_axis=0, tiled=True)  4.15 us
    ppermute x4, waiting for transfers between devices, swap(): return lax.ppermute(array, 'section', [(0, 1), (1, 0)])  3.33 us
  transfers between devices with their start and end apart: 9, of which 1 were waited for; matrix products, arithmetic and copies ran while one was open for 0% of the time, Pallas kernels for 4%

profile of v1, /device:TPU:1, one launch (start us, length us, event | category | flops | bytes accessed | tf_op | source)
XLA Modules:
  0.0 118.7 jit_solution(4521468020158757581)
XLA Ops:
  0.0 3.2 %collective-permute-start.3 = (bf16[1,3,3,320,320]{4,3,2,1,0:T(8,128)(2,1)}, bf16[1,3,3,320,320]{4,3,2,1,0:T(8,128)(2,1)}, u32[]{:S(2)}, u32[]{:S(2)}) collective-permute-start(bf16[1,3,3,320,320]{4,3,2,1,0:T(8,128)(2,1)} %own_ref.1), channel_id=1, source_target_pairs={{0,16},{16,0},{1,17},{17,1},{2,18},{18,2},{3,19},{19,3},{4,20},{20... | collective-permute-start | bytes 5529608 | tf_op jit(solution)/shard_map/ppermute | solution.py:263
  3.2 0.0 copy-start
  3.2 2.0 %copy-done = bf16[4,6,192,320]{3,2,1,0:T(8,128)(2,1)S(1)} copy-done((bf16[4,6,192,320]{3,2,1,0:T(8,128)(2,1)S(1)}, bf16[4,6,192,320]{3,2,1,0:T(8,128)(2,1)}, u32[]{:S(2)}) %copy-start) | copy-done | bytes 2949144
  5.2 0.0 copy-start.8
  5.2 0.0 copy-start.9
  5.2 0.0 copy-start.10
  5.2 2.0 %stats.1 = (f32[16,8,128]{2,1,0:T(8,128)}, bf16[2,192,320]{2,1,0:T(8,128)(2,1)}, bf16[2,192,320]{2,1,0:T(8,128)(2,1)}) custom-call(bf16[4,6,192,320]{3,2,1,0:T(8,128)(2,1)S(1)} %copy-done), custom_call_target="tpu_custom_call" | custom-call | tf_op jit(solution)/shard_map/stats/pallas_call | solution.py:283
  7.2 0.1 collective-permute-start
  7.4 3.8 %collective-permute-start.1 = (bf16[2,192,320]{2,1,0:T(8,128)(2,1)}, bf16[2,192,320]{2,1,0:T(8,128)(2,1)}, u32[]{:S(2)}, u32[]{:S(2)}) collective-permute-start(bf16[2,192,320]{2,1,0:T(8,128)(2,1)} %get-tuple-element.17), channel_id=1, source_target_pairs={{0,15},{1,2},{2,1},{3,4},{4,3},{5,6},{6,5},{7,8},{8,7},{9,10},{10,... | collective-permute-start | bytes 737288 | tf_op jit(solution)/shard_map/ppermute | solution.py:297
  11.1 4.1 %all-to-all-start = ((f32[16,8,128]{2,1,0:T(8,128)}), f32[16,8,128]{2,1,0:T(8,128)}, u32[]{:S(2)}, u32[]{:S(2)}) async-start(f32[16,8,128]{2,1,0:T(8,128)} %get-tuple-element.18), calls=%async_computation | async-start | bytes 131072 | tf_op jit(solution)/shard_map/all_to_all | solution.py:298
  15.3 0.0 copy-done.8
  15.3 0.0 copy-done.9
  15.3 0.0 copy-done.10
  15.3 0.0 copy-start.1
  15.3 0.7 collective-permute-start.2
  16.0 0.0 collective-permute-done.3.other_ref
  16.0 0.0 copy-start.2
  16.0 2.0 %copy-done.2 = bf16[1,3,3,320,320]{4,3,2,1,0:T(8,128)(2,1)S(1)} copy-done((bf16[1,3,3,320,320]{4,3,2,1,0:T(8,128)(2,1)S(1)}, bf16[1,3,3,320,320]{4,3,2,1,0:T(8,128)(2,1)}, u32[]{:S(2)}) %copy-start.2) | copy-done | bytes 1843224
  17.9 2.2 %weights.1 = (bf16[1024,1024]{1,0:T(8,128)(2,1)S(1)}, bf16[1024,1024]{1,0:T(8,128)(2,1)S(1)}) custom-call(bf16[1,3,3,320,320]{4,3,2,1,0:T(8,128)(2,1)S(1)} %copy-done.2, bf16[1,3,3,320,320]{4,3,2,1,0:T(8,128)(2,1)} %collective-permute-done.3.other_ref), custom_call_target="tpu_custom_call" | custom-call | tf_op jit(solution)/shard_map/weights/pallas_call | solution.py:301
  20.1 0.0 copy-start.3
  20.2 1.3 %copy-done.3 = bf16[1024,1024]{1,0:T(8,128)(2,1)} copy-done((bf16[1024,1024]{1,0:T(8,128)(2,1)}, bf16[1024,1024]{1,0:T(8,128)(2,1)S(1)}, u32[]{:S(2)}) %copy-start.3) | copy-done | bytes 2097176
  21.5 0.0 copy-start.5
  21.5 1.3 %copy-done.5 = bf16[1024,1024]{1,0:T(8,128)(2,1)} copy-done((bf16[1024,1024]{1,0:T(8,128)(2,1)}, bf16[1024,1024]{1,0:T(8,128)(2,1)S(1)}, u32[]{:S(2)}) %copy-start.5) | copy-done | bytes 2097176
  22.8 0.0 collective-permute-done.2.refs_5_
  22.8 0.0 all-to-all-done.refs_3_
  22.8 0.0 collective-permute-done.refs_1_
  22.8 0.0 collective-permute-done.1.refs_2_
  22.8 0.0 copy-done.1
  22.8 0.0 copy-start.4
  22.9 1.6 %copy-done.4 = bf16[1024,1024]{1,0:T(8,128)(2,1)S(1)} copy-done((bf16[1024,1024]{1,0:T(8,128)(2,1)S(1)}, bf16[1024,1024]{1,0:T(8,128)(2,1)}, u32[]{:S(2)}) %copy-start.4) | copy-done | bytes 2097176
  24.4 0.0 copy-start.6
  24.4 9.4 %conv0.1 = (bf16[2,6,192,320]{3,2,1,0:T(8,128)(2,1)S(1)}, f32[16,8,128]{2,1,0:T(8,128)S(1)}, bf16[2,192,320]{2,1,0:T(8,128)(2,1)S(1)}, bf16[2,192,320]{2,1,0:T(8,128)(2,1)S(1)}) custom-call(bf16[4,6,192,320]{3,2,1,0:T(8,128)(2,1)S(1)} %copy-done.1, bf16[2,192,320]{2,1,0:T(8,128)(2,1)} %collective-permute-done.refs_1_, ...), custom_call_target="tpu_custom_call" | custom-call | tf_op jit(solution)/shard_map/conv0/pallas_call | solution.py:314
  33.9 0.7 collective-permute-start.6
  34.6 0.7 collective-permute-start.4
  35.3 4.0 %collective-permute-start.5 = (bf16[2,192,320]{2,1,0:T(8,128)(2,1)S(1)}, bf16[2,192,320]{2,1,0:T(8,128)(2,1)S(1)}, u32[]{:S(2)}, u32[]{:S(2)}) collective-permute-start(bf16[2,192,320]{2,1,0:T(8,128)(2,1)S(1)} %get-tuple-element.22), channel_id=1, source_target_pairs={{0,15},{1,2},{2,1},{3,4},{4,3},{5,6},{6,5},{7,8},{8,7},{9,10},{10,... | collective-permute-start | bytes 737288 | tf_op jit(solution)/shard_map/ppermute | solution.py:341
  39.3 9.5 %all_to_all.10.refs_3_ = f32[16,8,128]{2,1,0:T(8,128)S(1)} all-to-all(f32[16,8,128]{2,1,0:T(8,128)S(1)} %get-tuple-element.23), channel_id=1, replica_groups=mesh['dp'=8,'section'=2,'space'=16] {'space'}, dimensions={0} | all-to-all | bytes 131072 | tf_op jit(solution)/shard_map/all_to_all | solution.py:343
  48.8 0.0 collective-permute-done.4.refs_1_
  48.8 0.0 collective-permute-done.5.refs_2_
  48.8 0.0 collective-permute-done.6.refs_8_
  48.8 0.0 copy-done.6
  48.8 8.9 %conv1.1 = (bf16[2,6,192,320]{3,2,1,0:T(8,128)(2,1)S(1)}, bf16[4,6,192,320]{3,2,1,0:T(8,128)(2,1)}) custom-call(bf16[2,6,192,320]{3,2,1,0:T(8,128)(2,1)S(1)} %get-tuple-element.20.refs_0_, bf16[2,192,320]{2,1,0:T(8,128)(2,1)S(1)} %collective-permute-done.4.refs_1_, bf16[2,192,320]{2,1,0:T(8,128)(2,1)S(1)} %collective-permute-done.5.refs_2_, ...), custom_call_target="tpu_custom_call" | custom-call | tf_op jit(solution)/shard_map/conv1/pallas_call | solution.py:314
  57.8 1.6 %collective-permute-start.7 = (bf16[2,6,192,320]{3,2,1,0:T(8,128)(2,1)S(1)}, bf16[2,6,192,320]{3,2,1,0:T(8,128)(2,1)S(1)}, u32[]{:S(2)}, u32[]{:S(2)}) collective-permute-start(bf16[2,6,192,320]{3,2,1,0:T(8,128)(2,1)S(1)} %get-tuple-element.26), channel_id=1, source_target_pairs={{0,16},{16,0},{1,17},{17,1},{2,18},{18,2},{3,19},{19,3},{4,20},{20... | collective-permute-start | bytes 4423688 | tf_op jit(solution)/shard_map/ppermute | solution.py:263
  59.3 3.3 %collective-permute-done.7.second_other = bf16[2,6,192,320]{3,2,1,0:T(8,128)(2,1)S(1)} collective-permute-done((bf16[2,6,192,320]{3,2,1,0:T(8,128)(2,1)S(1)}, bf16[2,6,192,320]{3,2,1,0:T(8,128)(2,1)S(1)}, u32[]{:S(2)}, u32[]{:S(2)}) %collective-permute-start.7) | collective-permute-done | bytes 1474592 | tf_op jit(solution)/shard_map/ppermute | solution.py:263
  62.6 0.0 copy-start.7
  62.6 1.2 %copy-done.7 = bf16[2,6,192,320]{3,2,1,0:T(8,128)(2,1)} copy-done((bf16[2,6,192,320]{3,2,1,0:T(8,128)(2,1)}, bf16[2,6,192,320]{3,2,1,0:T(8,128)(2,1)S(1)}, u32[]{:S(2)}) %copy-start.7) | copy-done | bytes 1474584
  63.9 54.7 %finish.1 = bf16[4,6,192,320]{3,2,1,0:T(8,128)(2,1)} custom-call(bf16[4,6,192,320]{3,2,1,0:T(8,128)(2,1)} %get-tuple-element.25.full_in, bf16[2,6,192,320]{3,2,1,0:T(8,128)(2,1)} %copy-done.7), custom_call_target="tpu_custom_call", output_to_operand_aliasing={{}: (0, {})} | custom-call | tf_op jit(solution)/shard_map/finish/pallas_call | solution.py:353
  (1 shorter events, 0.0 us)
Async XLA Ops:
  0.0 16.0 %collective-permute-start.3 = (bf16[1,3,3,320,320]{4,3,2,1,0:T(8,128)(2,1)}, bf16[1,3,3,320,320]{4,3,2,1,0:T(8,128)(2,1)}, u32[]{:S(2)}, u32[]{:S(2)}) collective-permute-start(bf16[1,3,3,320,320]{4,3,2,1,0:T(8,128)(2,1)} %own_ref.1), channel_id=1, source_target_pairs={{0,16},{16,0},{1,17},{17,1},{2,18},{18,2},{3,19},{19,3},{4,20},{20... | collective-permute-start | bytes 5529608 | tf_op jit(solution)/shard_map/ppermute | solution.py:263
  3.2 2.0 %copy-start = (bf16[4,6,192,320]{3,2,1,0:T(8,128)(2,1)S(1)}, bf16[4,6,192,320]{3,2,1,0:T(8,128)(2,1)}, u32[]{:S(2)}) copy-start(bf16[4,6,192,320]{3,2,1,0:T(8,128)(2,1)} %refs_7_.1) | copy-start | bytes 8847364
  5.2 10.1 %copy-start.8 = (f32[1,320]{1,0:T(1,128)S(1)}, f32[1,320]{1,0:T(1,128)}, u32[]{:S(2)}) copy-start(f32[1,320]{1,0:T(1,128)} %param.9) | copy-start | bytes 3844
  5.2 10.1 %copy-start.9 = (f32[1,320]{1,0:T(1,128)S(1)}, f32[1,320]{1,0:T(1,128)}, u32[]{:S(2)}) copy-start(f32[1,320]{1,0:T(1,128)} %param.8) | copy-start | bytes 3844
  5.2 10.1 %copy-start.10 = (f32[1,320]{1,0:T(1,128)S(1)}, f32[1,320]{1,0:T(1,128)}, u32[]{:S(2)}) copy-start(f32[1,320]{1,0:T(1,128)} %param.7) | copy-start | bytes 3844
  7.2 15.6 %collective-permute-start = (bf16[2,192,320]{2,1,0:T(8,128)(2,1)}, bf16[2,192,320]{2,1,0:T(8,128)(2,1)}, u32[]{:S(2)}, u32[]{:S(2)}) collective-permute-start(bf16[2,192,320]{2,1,0:T(8,128)(2,1)} %get-tuple-element.16), channel_id=1, source_target_pairs={{0,1},{1,0},{2,3},{3,2},{4,5},{5,4},{6,7},{7,6},{8,9},{9,8},{10,11... | collective-permute-start | bytes 737288 | tf_op jit(solution)/shard_map/ppermute | solution.py:296
  7.4 15.5 %collective-permute-start.1 = (bf16[2,192,320]{2,1,0:T(8,128)(2,1)}, bf16[2,192,320]{2,1,0:T(8,128)(2,1)}, u32[]{:S(2)}, u32[]{:S(2)}) collective-permute-start(bf16[2,192,320]{2,1,0:T(8,128)(2,1)} %get-tuple-element.17), channel_id=1, source_target_pairs={{0,15},{1,2},{2,1},{3,4},{4,3},{5,6},{6,5},{7,8},{8,7},{9,10},{10,... | collective-permute-start | bytes 737288 | tf_op jit(solution)/shard_map/ppermute | solution.py:297
  11.1 11.7 %all-to-all-start = ((f32[16,8,128]{2,1,0:T(8,128)}), f32[16,8,128]{2,1,0:T(8,128)}, u32[]{:S(2)}, u32[]{:S(2)}) async-start(f32[16,8,128]{2,1,0:T(8,128)} %get-tuple-element.18), calls=%async_computation | async-start | bytes 131072 | tf_op jit(solution)/shard_map/all_to_all | solution.py:298
  15.3 7.5 %copy-start.1 = (bf16[4,6,192,320]{3,2,1,0:T(8,128)(2,1)S(1)}, bf16[4,6,192,320]{3,2,1,0:T(8,128)(2,1)}, u32[]{:S(2)}) copy-start(bf16[4,6,192,320]{3,2,1,0:T(8,128)(2,1)} %refs_7_.1) | copy-start | bytes 8847364
  15.3 7.5 %collective-permute-start.2 = (f32[3,320]{1,0:T(4,128)S(1)}, f32[3,320]{1,0:T(4,128)S(1)}, u32[]{:S(2)}, u32[]{:S(2)}) collective-permute-start(f32[3,320]{1,0:T(4,128)S(1)} %pad_maximum_fusion.refs_4_), channel_id=1, source_target_pairs={{0,16},{16,0},{1,17},{17,1},{2,18},{18,2},{3,19},{19,3},{4,20},{20... | collective-permute-start | bytes 11528 | tf_op jit(solution)/shard_map/ppermute | solution.py:263
  16.0 2.0 %copy-start.2 = (bf16[1,3,3,320,320]{4,3,2,1,0:T(8,128)(2,1)S(1)}, bf16[1,3,3,320,320]{4,3,2,1,0:T(8,128)(2,1)}, u32[]{:S(2)}) copy-start(bf16[1,3,3,320,320]{4,3,2,1,0:T(8,128)(2,1)} %own_ref.1) | copy-start | bytes 5529604
  20.1 1.3 %copy-start.3 = (bf16[1024,1024]{1,0:T(8,128)(2,1)}, bf16[1024,1024]{1,0:T(8,128)(2,1)S(1)}, u32[]{:S(2)}) copy-start(bf16[1024,1024]{1,0:T(8,128)(2,1)S(1)} %get-tuple-element.19.refs_6_) | copy-start | bytes 6291460
  21.5 1.3 %copy-start.5 = (bf16[1024,1024]{1,0:T(8,128)(2,1)}, bf16[1024,1024]{1,0:T(8,128)(2,1)S(1)}, u32[]{:S(2)}) copy-start(bf16[1024,1024]{1,0:T(8,128)(2,1)S(1)} %get-tuple-element.24.refs_6_) | copy-start | bytes 6291460
  22.8 1.6 %copy-start.4 = (bf16[1024,1024]{1,0:T(8,128)(2,1)S(1)}, bf16[1024,1024]{1,0:T(8,128)(2,1)}, u32[]{:S(2)}) copy-start(bf16[1024,1024]{1,0:T(8,128)(2,1)} %copy-done.3) | copy-start | bytes 6291460
  24.4 24.4 %copy-start.6 = (bf16[1024,1024]{1,0:T(8,128)(2,1)S(1)}, bf16[1024,1024]{1,0:T(8,128)(2,1)}, u32[]{:S(2)}) copy-start(bf16[1024,1024]{1,0:T(8,128)(2,1)} %copy-done.5) | copy-start | bytes 6291460
  33.9 14.9 %collective-permute-start.6 = (bf16[2,6,192,320]{3,2,1,0:T(8,128)(2,1)S(1)}, bf16[2,6,192,320]{3,2,1,0:T(8,128)(2,1)S(1)}, u32[]{:S(2)}, u32[]{:S(2)}) collective-permute-start(bf16[2,6,192,320]{3,2,1,0:T(8,128)(2,1)S(1)} %get-tuple-element.20.refs_0_), channel_id=1, source_target_pairs={{0,16},{16,0},{1,17},{17,1},{2,18},{18,2},{3,19},{19,3},{4,20},{20... | collective-permute-start | bytes 4423688 | tf_op jit(solution)/shard_map/ppermute | solution.py:263
  34.6 14.2 %collective-permute-start.4 = (bf16[2,192,320]{2,1,0:T(8,128)(2,1)S(1)}, bf16[2,192,320]{2,1,0:T(8,128)(2,1)S(1)}, u32[]{:S(2)}, u32[]{:S(2)}) collective-permute-start(bf16[2,192,320]{2,1,0:T(8,128)(2,1)S(1)} %get-tuple-element.21), channel_id=1, source_target_pairs={{0,1},{1,0},{2,3},{3,2},{4,5},{5,4},{6,7},{7,6},{8,9},{9,8},{10,11... | collective-permute-start | bytes 737288 | tf_op jit(solution)/shard_map/ppermute | solution.py:340
  35.3 13.5 %collective-permute-start.5 = (bf16[2,192,320]{2,1,0:T(8,128)(2,1)S(1)}, bf16[2,192,320]{2,1,0:T(8,128)(2,1)S(1)}, u32[]{:S(2)}, u32[]{:S(2)}) collective-permute-start(bf16[2,192,320]{2,1,0:T(8,128)(2,1)S(1)} %get-tuple-element.22), channel_id=1, source_target_pairs={{0,15},{1,2},{2,1},{3,4},{4,3},{5,6},{6,5},{7,8},{8,7},{9,10},{10,... | collective-permute-start | bytes 737288 | tf_op jit(solution)/shard_map/ppermute | solution.py:341
  57.8 4.9 %collective-permute-start.7 = (bf16[2,6,192,320]{3,2,1,0:T(8,128)(2,1)S(1)}, bf16[2,6,192,320]{3,2,1,0:T(8,128)(2,1)S(1)}, u32[]{:S(2)}, u32[]{:S(2)}) collective-permute-start(bf16[2,6,192,320]{3,2,1,0:T(8,128)(2,1)S(1)} %get-tuple-element.26), channel_id=1, source_target_pairs={{0,16},{16,0},{1,17},{17,1},{2,18},{18,2},{3,19},{19,3},{4,20},{20... | collective-permute-start | bytes 4423688 | tf_op jit(solution)/shard_map/ppermute | solution.py:263
  62.6 1.2 %copy-start.7 = (bf16[2,6,192,320]{3,2,1,0:T(8,128)(2,1)}, bf16[2,6,192,320]{3,2,1,0:T(8,128)(2,1)S(1)}, u32[]{:S(2)}) copy-start(bf16[2,6,192,320]{3,2,1,0:T(8,128)(2,1)S(1)} %collective-permute-done.7.second_other) | copy-start | bytes 4423684

commit v2 on v1

v2 whole, which is shorter than its diff:
```python
import jax
import jax.numpy as jnp
from jax import lax
from jax.experimental import pallas as pl
from jax.experimental.pallas import tpu as pltpu
from jax.sharding import PartitionSpec as P

GROUPS = 32
F32 = jnp.float32
BF16 = jnp.bfloat16
ANY = pl.BlockSpec(memory_space=pl.ANY)
VM = pl.BlockSpec(memory_space=pltpu.VMEM)
HBM = pl.BlockSpec(memory_space=pltpu.HBM)


def one_hot(shape, channel_dim, per_group):
    channel = lax.broadcasted_iota(jnp.int32, shape, channel_dim)
    group = lax.broadcasted_iota(jnp.int32, shape, 1 - channel_dim)
    low = group * per_group
    return jnp.where((channel >= low) & (channel < low + per_group), 1.0, 0.0).astype(BF16)


def exact_dot(values, selector):
    high = values.astype(BF16)
    rest = values - high.astype(F32)
    middle = rest.astype(BF16)
    low = (rest - middle.astype(F32)).astype(BF16)
    return (
        jnp.dot(high, selector, preferred_element_type=F32)
        + jnp.dot(middle, selector, preferred_element_type=F32)
        + jnp.dot(low, selector, preferred_element_type=F32)
    )


def send_group_sums(sums, stats_out, per_group):
    channels = sums.shape[1]
    grouped = exact_dot(sums, one_hot((channels, 128), 0, per_group))
    for i in range(stats_out.shape[0]):
        stats_out[i] = grouped


def fold_rows(block):
    return block.reshape(block.shape[0] // 8, 8, block.shape[1]).sum(axis=0)


def stats_kernel(x_any, stats_out, ha_out, hb_out, x_buf, sem):
    n, rows, cols, ch = x_buf.shape
    sec = lax.axis_index("section")
    even = lax.axis_index("space") % 2 == 0
    loads = []
    for s in range(n):
        cp = pltpu.make_async_copy(x_any.at[sec * n + s], x_buf.at[s], sem.at[s])
        cp.start()
        loads.append(cp)
    total = []
    row_a = jnp.where(even, rows - 1, 0)
    for s in range(n):
        loads[s].wait()
        ha_out[s] = x_buf[s, row_a]
        hb_out[s] = x_buf[s, rows - 1 - row_a]

        def step(r, carry):
            acc, sq = carry
            v = x_buf[s, r].astype(F32)
            return acc + fold_rows(v), sq + fold_rows(v * v)

        zero = jnp.zeros((8, ch), F32)
        acc, sq = lax.fori_loop(0, rows, step, (zero, zero))
        total += [acc.sum(axis=0, keepdims=True), sq.sum(axis=0, keepdims=True)]
    sums = jnp.concatenate(total + [jnp.zeros((8 - len(total), ch), F32)], axis=0)
    send_group_sums(sums, stats_out, ch // GROUPS)


def lay_out_right(src, right_ref):
    ch = src.shape[-1]
    rem = ch - 256
    for dr in range(3):
        right = [src[0, dr, dc, :, 256:ch].astype(F32) for dc in range(3)]
        right = jnp.concatenate(right + [jnp.zeros((ch, 256 - 3 * rem), F32)], axis=1).astype(BF16)
        right_ref[dr * 256 : dr * 256 + 256, :] = right[0:256]
        right_ref[768 + dr * rem : 768 + dr * rem + rem, :] = right[256:ch]
    right_ref[768 + 3 * rem : 1024, :] = jnp.zeros((256 - 3 * rem, 256), BF16)


def kernel_columns(src, dc):
    ch = src.shape[-1]
    parts = [src[0, dr, dc, 0:256, 0:256] for dr in range(3)] + [src[0, dr, dc, 256:ch, 0:256] for dr in range(3)]
    return jnp.concatenate(parts + [jnp.zeros((1024 - 3 * ch, 256), BF16)], axis=0)


def conv_kernel(index, members, n_space, chunk_rows, *refs):
    if index == 0:
        (lat_hbm, ra_ref, rb_ref, stats_ref, own_p, other_p, own_k, other_k,
         y_out, stats_out, ha_out, hb_out,
         lat_buf, w_buf, right_buf, xm, xr, rem_buf, z_buf, sem) = refs
        x_ref = lat_buf
    else:
        (lat_hbm, ra_ref, rb_ref, stats_ref, own_p, other_p, own_k, other_k, x_ref, first_other,
         y_out, full_out,
         lat_buf, w_buf, right_buf, xm, xr, rem_buf, z_buf, sem) = refs
    n, rows, cols, ch = lat_buf.shape
    padded_rows = rows + 2
    rem = ch - 256
    sec = lax.axis_index("section")
    space = lax.axis_index("space")
    even = space % 2 == 0
    lat_loads = [
        pltpu.make_async_copy(lat_hbm.at[sec * n + s], lat_buf.at[s], sem.at[2, s]) for s in range(n)
    ]
    if index == 0:
        for cp in lat_loads:
            cp.start()

    @pl.when(sec == index)
    def _():
        pltpu.make_async_copy(own_k, w_buf, sem.at[3, 0]).start()

    @pl.when(sec != index)
    def _():
        pltpu.make_async_copy(other_k, w_buf, sem.at[3, 0]).start()

    if index == 1:
        for cp in lat_loads:
            cp.start()
    if index == 1:
        keep_own = pltpu.make_async_copy(x_ref, full_out.at[pl.ds(0, n)], sem.at[0, 0])
        keep_other = pltpu.make_async_copy(first_other, full_out.at[pl.ds(n, n)], sem.at[0, 1])

        @pl.when(sec == 0)
        def _():
            keep_own.start()
            keep_other.start()

    params = jnp.where(sec == index, own_p[...], other_p[...])
    gain, shift, bias = params[0:1], params[1:2], params[2:3]
    total = stats_ref[0]
    for i in range(1, n_space):
        total = total + stats_ref[i]
    packed = []
    for s in range(n):
        mean = total[2 * s : 2 * s + 1] * (1.0 / members)
        var = jnp.maximum(total[2 * s + 1 : 2 * s + 2] * (1.0 / members) - mean * mean, 0.0)
        packed += [mean, lax.rsqrt(var + 1e-05)]
    packed = jnp.concatenate(packed + [jnp.zeros((8 - 2 * n, 128), F32)], axis=0)
    spread = exact_dot(packed, one_hot((128, ch), 1, ch // GROUPS))

    if index == 0:
        acc = [[jnp.zeros((8, ch), F32) for _ in range(2)] for _ in range(n)]
    row_a = jnp.where(even, rows - 1, 0)
    for s in range(n):
        if index == 0:
            lat_loads[s].wait()
        half_a = 0.5 * (spread[2 * s + 1 : 2 * s + 2] * gain)
        half_b = 0.5 * shift - spread[2 * s : 2 * s + 1] * half_a
        for j in range(padded_rows):
            if j == 0:
                source = jnp.where(even, rb_ref[s], ra_ref[s])
            elif j == padded_rows - 1:
                source = jnp.where(even, ra_ref[s], rb_ref[s])
            else:
                source = x_ref[s, j - 1]
            half = source.astype(F32) * half_a + half_b
            y = half + half * jnp.tanh(half)
            if j == 0:
                y = jnp.where(space == 0, 0.0, y)
            if j == padded_rows - 1:
                y = jnp.where(space == n_space - 1, 0.0, y)
            xm[s, pl.ds(j * cols, cols), :] = y[:, 0:256].astype(BF16)
            rem_buf[j] = y[:, 256:ch]
            if j >= 2:
                parts = [rem_buf[j - 2], rem_buf[j - 1], rem_buf[j], jnp.zeros((cols, 256 - 3 * rem), F32)]
                xr[s, pl.ds((j - 2) * cols, cols), :] = jnp.concatenate(parts, axis=1).astype(BF16)
        if s == 0:
            pltpu.make_async_copy(own_k, w_buf, sem.at[3, 0]).wait()
            lay_out_right(w_buf, right_buf)
        if index == 1:
            lat_loads[s].wait()
        for r0 in range(0, rows, chunk_rows):
            m = chunk_rows * cols
            lhs = jnp.concatenate(
                [xm[s, pl.ds((r0 + dr) * cols, m), :] for dr in range(3)] + [xr[s, pl.ds(r0 * cols, m), :]],
                axis=1,
            )
            slot = (r0 // chunk_rows) % 2
            for dc in range(3):
                z_buf[slot, :, dc * 256 : dc * 256 + 256] = jnp.dot(
                    lhs, kernel_columns(w_buf, dc), preferred_element_type=F32
                )
            z_buf[slot, :, 768:1024] = jnp.dot(lhs, right_buf[...], preferred_element_type=F32)
            first_slab = lax.broadcasted_iota(jnp.int32, (8, 256), 0) == 0
            last_slab = lax.broadcasted_iota(jnp.int32, (8, 256), 0) == 7
            for r in range(chunk_rows):
                at = pl.ds(r * cols, cols)

                def down(z, width):
                    moved = pltpu.roll(z, 1, 0)
                    head = jnp.where(first_slab[:, :width], 0.0, moved[0:8])
                    return jnp.concatenate([head, moved[8:]], axis=0)

                def up(z, width):
                    moved = pltpu.roll(z, cols - 1, 0)
                    tail = jnp.where(last_slab[:, :width], 0.0, moved[cols - 8 :])
                    return jnp.concatenate([moved[: cols - 8], tail], axis=0)

                main = z_buf[slot, at, 256:512] + down(z_buf[slot, at, 0:256], 256) + up(z_buf[slot, at, 512:768], 256)
                left = z_buf[slot, at, 768:896]
                right = z_buf[slot, at, 896:1024]
                side = down(left, 128) + pltpu.roll(left, 64, 1) + up(right, 128)
                out = jnp.concatenate([main, side[:, 0:rem]], axis=1) + bias
                if index == 1:
                    out = out + lat_buf[s, r0 + r].astype(F32)
                rounded = out.astype(BF16)
                y_out[s, r0 + r] = rounded
                if index == 0:
                    back = rounded.astype(F32)
                    acc[s][0] = acc[s][0] + fold_rows(back)
                    acc[s][1] = acc[s][1] + fold_rows(back * back)
        if index == 0:
            ha_out[s] = y_out[s, row_a]
            hb_out[s] = y_out[s, rows - 1 - row_a]
        else:
            keep_new = pltpu.make_async_copy(y_out.at[s], full_out.at[n + s], sem.at[1, s])

            @pl.when(sec != 0)
            def _():
                keep_new.start()

    if index == 0:
        rows_out = []
        for s in range(n):
            rows_out += [v.sum(axis=0, keepdims=True) for v in acc[s]]
        sums = jnp.concatenate(rows_out + [jnp.zeros((8 - 2 * n, ch), F32)], axis=0)
        send_group_sums(sums, stats_out, ch // GROUPS)
    if index == 1:

        @pl.when(sec == 0)
        def _():
            keep_own.wait()
            keep_other.wait()

        @pl.when(sec != 0)
        def _():
            for s in range(n):
                pltpu.make_async_copy(y_out.at[s], full_out.at[n + s], sem.at[1, s]).wait()


def finish_kernel(full_in, second_other, full_out, sem):
    n = second_other.shape[0]
    cp = pltpu.make_async_copy(second_other, full_out.at[pl.ds(0, n)], sem)

    @pl.when(lax.axis_index("section") != 0)
    def _():
        cp.start()
        cp.wait()


def swap(array):
    return lax.ppermute(array, "section", [(0, 1), (1, 0)])


def on_device(latents, kernels, norm_gain, norm_bias, conv_bias):
    samples, rows, cols, ch = latents.shape
    n = samples // lax.axis_size("section")
    n_space = lax.axis_size("space")
    members = rows * n_space * cols * (ch // GROUPS)
    pairs_a = [(i, i ^ 1) for i in range(n_space)]
    pairs_b = [(i, (i - 1) % n_space if i % 2 == 0 else (i + 1) % n_space) for i in range(n_space)]
    shape = jax.ShapeDtypeStruct
    stats_shape = shape((n_space, 8, 128), F32)
    edge_shape = shape((n, cols, ch), BF16)
    part_shape = shape((n, rows, cols, ch), BF16)
    limit = pltpu.CompilerParams(vmem_limit_bytes=32 * 1024 * 1024)

    latents = pltpu.with_memory_space_constraint(latents, pltpu.HBM)
    kernels = pltpu.with_memory_space_constraint(kernels, pltpu.HBM)
    own_p = jnp.concatenate([norm_gain, norm_bias, conv_bias], axis=0)
    other_p = swap(own_p)
    other_k = pltpu.with_memory_space_constraint(swap(kernels), pltpu.HBM)

    stats, ha, hb = pl.pallas_call(
        stats_kernel,
        out_shape=(stats_shape, edge_shape, edge_shape),
        in_specs=[HBM],
        out_specs=(VM, VM, VM),
        scratch_shapes=[
            pltpu.VMEM((n, rows, cols, ch), BF16),
            pltpu.SemaphoreType.DMA((n,)),
        ],
        compiler_params=limit,
        name="stats",
    )(latents)
    ra = lax.ppermute(ha, "space", pairs_a)
    rb = lax.ppermute(hb, "space", pairs_b)
    stats = lax.all_to_all(stats, "space", split_axis=0, concat_axis=0, tiled=True)

    chunk_rows = 2

    def conv(index, operands, out_shape, out_specs):
        body = lambda *refs: conv_kernel(index, members, n_space, chunk_rows, *refs)
        return pl.pallas_call(
            body,
            out_shape=out_shape,
            in_specs=[HBM, VM, VM, VM, VM, VM, HBM, HBM] + [VM] * (len(operands) - 8),
            out_specs=out_specs,
            scratch_shapes=[
                pltpu.VMEM((n, rows, cols, ch), BF16),
                pltpu.VMEM(kernels.shape, BF16),
                pltpu.VMEM((1024, 256), BF16),
                pltpu.VMEM((n, (rows + 2) * cols, 256), BF16),
                pltpu.VMEM((n, rows * cols, 256), BF16),
                pltpu.VMEM((rows + 2, cols, ch - 256), F32),
                pltpu.VMEM((2, chunk_rows * cols, 1024), F32),
                pltpu.SemaphoreType.DMA((4, n)),
            ],
            compiler_params=limit,
            name="conv%d" % index,
        )(*operands)

    first, stats, ha, hb = conv(
        0,
        (latents, ra, rb, stats, own_p, other_p, kernels, other_k),
        (part_shape, stats_shape, edge_shape, edge_shape),
        (VM, VM, VM, VM),
    )
    ra = lax.ppermute(ha, "space", pairs_a)
    rb = lax.ppermute(hb, "space", pairs_b)
    first_other = swap(first)
    stats = lax.all_to_all(stats, "space", split_axis=0, concat_axis=0, tiled=True)
    full_shape = shape((samples, rows, cols, ch), BF16)
    second, full = conv(
        1,
        (latents, ra, rb, stats, own_p, other_p, kernels, other_k, first, first_other),
        (part_shape, full_shape),
        (VM, HBM),
    )
    second_other = swap(second)
    full = pl.pallas_call(
        finish_kernel,
        out_shape=full_shape,
        in_specs=[HBM, VM],
        out_specs=HBM,
        scratch_shapes=[pltpu.SemaphoreType.DMA],
        input_output_aliases={0: 0},
        compiler_params=pltpu.CompilerParams(vmem_limit_bytes=1024 * 1024),
        name="finish",
    )(full, second_other)
    return full[None]


def solution(mesh):
    return jax.shard_map(
        on_device,
        mesh=mesh,
        in_specs=(
            P("dp", "space", None, None),
            P("section", None, None, None, None),
            P("section", None),
            P("section", None),
            P("section", None),
        ),
        out_specs=P("section", "dp", "space", None, None),
        check_vma=False,
    )
```

time: 119 us -> 60.2 us (0.51)
  Pallas kernels: 77.3 us -> 20.9 us
  local copies, waits for them, and re-layouts: 9.44 us -> 1.36 us
  waiting for transfers between devices: 3.34 us -> 9.06 us
  blocking collectives: 9.5 us -> 10.9 us
  starting transfers between devices: 18.8 us -> 17.5 us
    pallas_call x4 -> x3, Pallas kernels: 75.3 us -> 18.3 us  [the longest x2 17.1 us: conv(): pl.pallas_call(body, out_shape=out_shape, in_specs=[HBM, VM, VM, VM, VM,...]
    unnamed x22 -> x8, local copies, waits for them, and re-layouts: 9.44 us -> 1.36 us
    all_to_all x1, waiting for transfers between devices: 0.01 us -> 4.9 us  [on_device(): lax.all_to_all(stats, 'space', split_axis=0, concat_axis=0, tiled=True)]
    ppermute x2, starting transfers between devices: 7.73 us -> 5.46 us  [on_device(): rb = lax.ppermute(hb, 'space', pairs_b)]
    ppermute x4, starting transfers between devices: 6.14 us -> 8.17 us  [swap(): return lax.ppermute(array, 'section', [(0, 1), (1, 0)])]
    all_to_all x1, blocking collectives: 9.5 us -> 10.9 us  [on_device(): lax.all_to_all(stats, 'space', split_axis=0, concat_axis=0, tiled=True)]
  transfers between devices with their start and end apart: 9 -> 9, of which waited for: 1 -> 3; matrix products, arithmetic and copies ran while one was open for 0% -> 0% of each run, Pallas kernels for 4% -> 4%
where the time goes in v2:
time: 60.2 us; the launch traced here: 60 us
  Pallas kernels  20.9 us (35%)
  starting transfers between devices  17.5 us (29%)
  blocking collectives  10.9 us (18%)
  waiting for transfers between devices  9.06 us (15%)
  local copies, waits for them, and re-layouts  1.36 us (2%)
    pallas_call x2, Pallas kernels, conv(): pl.pallas_call(body, out_shape=out_shape, in_specs=[HBM, VM, VM, VM, VM,...  17.1 us
    all_to_all x1, blocking collectives, on_device(): lax.all_to_all(stats, 'space', split_axis=0, concat_axis=0, tiled=True)  10.9 us
    ppermute x4, starting transfers between devices, swap(): return lax.ppermute(array, 'section', [(0, 1), (1, 0)])  8.17 us
    ppermute x2, starting transfers between devices, on_device(): rb = lax.ppermute(hb, 'space', pairs_b)  5.46 us
    all_to_all x1, waiting for transfers between devices, on_device(): lax.all_to_all(stats, 'space', split_axis=0, concat_axis=0, tiled=True)  4.9 us
    ppermute x4, waiting for transfers between devices, swap(): return lax.ppermute(array, 'section', [(0, 1), (1, 0)])  4.15 us
    all_to_all x1, starting transfers between devices, on_device(): lax.all_to_all(stats, 'space', split_axis=0, concat_axis=0, tiled=True)  3.5 us
    pallas_call x1, Pallas kernels, on_device(): pl.pallas_call(stats_kernel, out_shape=(stats_shape, edge_shape, edge_sha...  2.57 us
  transfers between devices with their start and end apart: 9, of which 3 were waited for; matrix products, arithmetic and copies ran while one was open for 0% of the time, Pallas kernels for 4%

profile of v2, /device:TPU:1, one launch (start us, length us, event | category | flops | bytes accessed | tf_op | source)
XLA Modules:
  0.0 60.0 jit_solution(4288119366535854511)
XLA Ops:
  0.0 0.0 copy-start.1
  0.0 0.0 copy-start.2
  0.0 0.0 copy-start.3
  0.0 3.2 %collective-permute-start.3 = (bf16[1,3,3,320,320]{4,3,2,1,0:T(8,128)(2,1)}, bf16[1,3,3,320,320]{4,3,2,1,0:T(8,128)(2,1)S(1)}, u32[]{:S(2)}, u32[]{:S(2)}) collective-permute-start(bf16[1,3,3,320,320]{4,3,2,1,0:T(8,128)(2,1)} %refs_6_.3), channel_id=1, source_target_pairs={{0,16},{16,0},{1,17},{17,1},{2,18},{18,2},{3,19},{19,3},{4,20},{20... | collective-permute-start | bytes 5529608 | tf_op jit(solution)/shard_map/ppermute | solution.py:258
  3.2 2.6 %stats.1 = (f32[16,8,128]{2,1,0:T(8,128)}, bf16[2,192,320]{2,1,0:T(8,128)(2,1)S(1)}, bf16[2,192,320]{2,1,0:T(8,128)(2,1)S(1)}) custom-call(bf16[4,6,192,320]{3,2,1,0:T(8,128)(2,1)} %refs_0_.3), custom_call_target="tpu_custom_call" | custom-call | tf_op jit(solution)/shard_map/stats/pallas_call | solution.py:280
  5.8 0.1 collective-permute-start
  5.9 3.8 %collective-permute-start.1 = (bf16[2,192,320]{2,1,0:T(8,128)(2,1)S(1)}, bf16[2,192,320]{2,1,0:T(8,128)(2,1)S(1)}, u32[]{:S(2)}, u32[]{:S(2)}) collective-permute-start(bf16[2,192,320]{2,1,0:T(8,128)(2,1)S(1)} %get-tuple-element.15), channel_id=1, source_target_pairs={{0,15},{1,2},{2,1},{3,4},{4,3},{5,6},{6,5},{7,8},{8,7},{9,10},{10,... | collective-permute-start | bytes 737288 | tf_op jit(solution)/shard_map/ppermute | solution.py:293
  9.7 3.5 %all-to-all-start = ((f32[16,8,128]{2,1,0:T(8,128)}), f32[16,8,128]{2,1,0:T(8,128)S(1)}, u32[]{:S(2)}, u32[]{:S(2)}) async-start(f32[16,8,128]{2,1,0:T(8,128)} %get-tuple-element.16), calls=%async_computation | async-start | bytes 131072 | tf_op jit(solution)/shard_map/all_to_all | solution.py:294
  13.2 0.0 copy-done.1
  13.3 0.0 copy-done.2
  13.3 0.0 copy-done.3
  13.3 0.7 %collective-permute-start.2 = (f32[3,320]{1,0:T(4,128)S(1)}, f32[3,320]{1,0:T(4,128)S(1)}, u32[]{:S(2)}, u32[]{:S(2)}) collective-permute-start(f32[3,320]{1,0:T(4,128)S(1)} %pad_maximum_fusion.refs_4_), channel_id=1, source_target_pairs={{0,16},{16,0},{1,17},{17,1},{2,18},{18,2},{3,19},{19,3},{4,20},{20... | collective-permute-start | bytes 11528 | tf_op jit(solution)/shard_map/ppermute | solution.py:258
  14.0 0.8 %collective-permute-done.2.refs_5_ = f32[3,320]{1,0:T(4,128)S(1)} collective-permute-done((f32[3,320]{1,0:T(4,128)S(1)}, f32[3,320]{1,0:T(4,128)S(1)}, u32[]{:S(2)}, u32[]{:S(2)}) %collective-permute-start.2) | collective-permute-done | bytes 3872 | tf_op jit(solution)/shard_map/ppermute | solution.py:258
  14.8 4.9 %all-to-all-done.refs_3_ = f32[16,8,128]{2,1,0:T(8,128)S(1)} async-done(((f32[16,8,128]{2,1,0:T(8,128)}), f32[16,8,128]{2,1,0:T(8,128)S(1)}, u32[]{:S(2)}, u32[]{:S(2)}) %all-to-all-start) | async-done | bytes 65568 | tf_op jit(solution)/shard_map/all_to_all | solution.py:294
  19.7 0.0 collective-permute-done.refs_1_
  19.7 0.0 collective-permute-done.1.refs_2_
  19.7 0.0 collective-permute-done.3.refs_7_
  19.7 0.0 copy-start
  19.7 1.4 %copy-done = bf16[1,3,3,320,320]{4,3,2,1,0:T(8,128)(2,1)} copy-done((bf16[1,3,3,320,320]{4,3,2,1,0:T(8,128)(2,1)}, bf16[1,3,3,320,320]{4,3,2,1,0:T(8,128)(2,1)S(1)}, u32[]{:S(2)}) %copy-start) | copy-done | bytes 1843224
  21.1 8.5 %conv0.1 = (bf16[2,6,192,320]{3,2,1,0:T(8,128)(2,1)S(1)}, f32[16,8,128]{2,1,0:T(8,128)S(1)}, bf16[2,192,320]{2,1,0:T(8,128)(2,1)S(1)}, bf16[2,192,320]{2,1,0:T(8,128)(2,1)S(1)}) custom-call(bf16[4,6,192,320]{3,2,1,0:T(8,128)(2,1)} %refs_0_.3, bf16[2,192,320]{2,1,0:T(8,128)(2,1)S(1)} %collective-permute-done.refs_1_, ...), custom_call_target="tpu_custom_call" | custom-call | tf_op jit(solution)/shard_map/conv0/pallas_call | solution.py:300
  29.6 1.8 %collective-permute-start.6 = (bf16[2,6,192,320]{3,2,1,0:T(8,128)(2,1)S(1)}, bf16[2,6,192,320]{3,2,1,0:T(8,128)(2,1)S(1)}, u32[]{:S(2)}, u32[]{:S(2)}) collective-permute-start(bf16[2,6,192,320]{3,2,1,0:T(8,128)(2,1)S(1)} %get-tuple-element.20.refs_8_), channel_id=1, source_target_pairs={{0,16},{16,0},{1,17},{17,1},{2,18},{18,2},{3,19},{19,3},{4,20},{20... | collective-permute-start | bytes 4423688 | tf_op jit(solution)/shard_map/ppermute | solution.py:258
  31.4 0.3 collective-permute-start.4
  31.7 1.6 %collective-permute-start.5 = (bf16[2,192,320]{2,1,0:T(8,128)(2,1)S(1)}, bf16[2,192,320]{2,1,0:T(8,128)(2,1)S(1)}, u32[]{:S(2)}, u32[]{:S(2)}) collective-permute-start(bf16[2,192,320]{2,1,0:T(8,128)(2,1)S(1)} %get-tuple-element.18), channel_id=1, source_target_pairs={{0,15},{1,2},{2,1},{3,4},{4,3},{5,6},{6,5},{7,8},{8,7},{9,10},{10,... | collective-permute-start | bytes 737288 | tf_op jit(solution)/shard_map/ppermute | solution.py:326
  33.3 10.9 %all_to_all.10.refs_3_ = f32[16,8,128]{2,1,0:T(8,128)S(1)} all-to-all(f32[16,8,128]{2,1,0:T(8,128)S(1)} %get-tuple-element.19), channel_id=1, replica_groups=mesh['dp'=8,'section'=2,'space'=16] {'space'}, dimensions={0} | all-to-all | bytes 131072 | tf_op jit(solution)/shard_map/all_to_all | solution.py:328
  44.3 0.0 collective-permute-done.4.refs_1_
  44.3 0.0 collective-permute-done.5.refs_2_
  44.3 0.0 collective-permute-done.6.refs_9_
  44.3 8.5 %conv1.1 = (bf16[2,6,192,320]{3,2,1,0:T(8,128)(2,1)S(1)}, bf16[4,6,192,320]{3,2,1,0:T(8,128)(2,1)}) custom-call(bf16[4,6,192,320]{3,2,1,0:T(8,128)(2,1)} %refs_0_.3, bf16[2,192,320]{2,1,0:T(8,128)(2,1)S(1)} %collective-permute-done.4.refs_1_, bf16[2,192,320]{2,1,0:T(8,128)(2,1)S(1)} %collective-permute-done.5.refs_2_, f32[16,8,128]{2,1,0:T(8,128)S(1)} %all_to_all.10.refs_3_, ...), custom_call_target="tpu_custom_call" | custom-call | tf_op jit(solution)/shard_map/conv1/pallas_call | solution.py:300
  52.8 2.5 %collective-permute-start.7 = (bf16[2,6,192,320]{3,2,1,0:T(8,128)(2,1)S(1)}, bf16[2,6,192,320]{3,2,1,0:T(8,128)(2,1)S(1)}, u32[]{:S(2)}, u32[]{:S(2)}) collective-permute-start(bf16[2,6,192,320]{3,2,1,0:T(8,128)(2,1)S(1)} %get-tuple-element.22), channel_id=1, source_target_pairs={{0,16},{16,0},{1,17},{17,1},{2,18},{18,2},{3,19},{19,3},{4,20},{20... | collective-permute-start | bytes 4423688 | tf_op jit(solution)/shard_map/ppermute | solution.py:258
  55.3 3.3 %collective-permute-done.7.second_other = bf16[2,6,192,320]{3,2,1,0:T(8,128)(2,1)S(1)} collective-permute-done((bf16[2,6,192,320]{3,2,1,0:T(8,128)(2,1)S(1)}, bf16[2,6,192,320]{3,2,1,0:T(8,128)(2,1)S(1)}, u32[]{:S(2)}, u32[]{:S(2)}) %collective-permute-start.7) | collective-permute-done | bytes 1474592 | tf_op jit(solution)/shard_map/ppermute | solution.py:258
  58.6 1.2 %finish.1 = bf16[4,6,192,320]{3,2,1,0:T(8,128)(2,1)} custom-call(bf16[4,6,192,320]{3,2,1,0:T(8,128)(2,1)} %get-tuple-element.21.full_in, bf16[2,6,192,320]{3,2,1,0:T(8,128)(2,1)S(1)} %collective-permute-done.7.second_other), custom_call_target="tpu_custom_call", output_to_operand_aliasing={{}: (0, {})} | custom-call | tf_op jit(solution)/shard_map/finish/pallas_call | solution.py:337
  (1 shorter events, 0.0 us)
Async XLA Ops:
  0.0 13.2 %copy-start.1 = (f32[1,320]{1,0:T(1,128)S(1)}, f32[1,320]{1,0:T(1,128)}, u32[]{:S(2)}) copy-start(f32[1,320]{1,0:T(1,128)} %param.9) | copy-start | bytes 3844
  0.0 13.3 %copy-start.2 = (f32[1,320]{1,0:T(1,128)S(1)}, f32[1,320]{1,0:T(1,128)}, u32[]{:S(2)}) copy-start(f32[1,320]{1,0:T(1,128)} %param.8) | copy-start | bytes 3844
  0.0 13.3 %copy-start.3 = (f32[1,320]{1,0:T(1,128)S(1)}, f32[1,320]{1,0:T(1,128)}, u32[]{:S(2)}) copy-start(f32[1,320]{1,0:T(1,128)} %param.7) | copy-start | bytes 3844
  0.0 19.7 %collective-permute-start.3 = (bf16[1,3,3,320,320]{4,3,2,1,0:T(8,128)(2,1)}, bf16[1,3,3,320,320]{4,3,2,1,0:T(8,128)(2,1)S(1)}, u32[]{:S(2)}, u32[]{:S(2)}) collective-permute-start(bf16[1,3,3,320,320]{4,3,2,1,0:T(8,128)(2,1)} %refs_6_.3), channel_id=1, source_target_pairs={{0,16},{16,0},{1,17},{17,1},{2,18},{18,2},{3,19},{19,3},{4,20},{20... | collective-permute-start | bytes 5529608 | tf_op jit(solution)/shard_map/ppermute | solution.py:258
  5.8 13.9 %collective-permute-start = (bf16[2,192,320]{2,1,0:T(8,128)(2,1)S(1)}, bf16[2,192,320]{2,1,0:T(8,128)(2,1)S(1)}, u32[]{:S(2)}, u32[]{:S(2)}) collective-permute-start(bf16[2,192,320]{2,1,0:T(8,128)(2,1)S(1)} %get-tuple-element.14), channel_id=1, source_target_pairs={{0,1},{1,0},{2,3},{3,2},{4,5},{5,4},{6,7},{7,6},{8,9},{9,8},{10,11... | collective-permute-start | bytes 737288 | tf_op jit(solution)/shard_map/ppermute | solution.py:292
  5.9 13.8 %collective-permute-start.1 = (bf16[2,192,320]{2,1,0:T(8,128)(2,1)S(1)}, bf16[2,192,320]{2,1,0:T(8,128)(2,1)S(1)}, u32[]{:S(2)}, u32[]{:S(2)}) collective-permute-start(bf16[2,192,320]{2,1,0:T(8,128)(2,1)S(1)} %get-tuple-element.15), channel_id=1, source_target_pairs={{0,15},{1,2},{2,1},{3,4},{4,3},{5,6},{6,5},{7,8},{8,7},{9,10},{10,... | collective-permute-start | bytes 737288 | tf_op jit(solution)/shard_map/ppermute | solution.py:293
  9.7 10.0 %all-to-all-start = ((f32[16,8,128]{2,1,0:T(8,128)}), f32[16,8,128]{2,1,0:T(8,128)S(1)}, u32[]{:S(2)}, u32[]{:S(2)}) async-start(f32[16,8,128]{2,1,0:T(8,128)} %get-tuple-element.16), calls=%async_computation | async-start | bytes 131072 | tf_op jit(solution)/shard_map/all_to_all | solution.py:294
  13.3 1.5 %collective-permute-start.2 = (f32[3,320]{1,0:T(4,128)S(1)}, f32[3,320]{1,0:T(4,128)S(1)}, u32[]{:S(2)}, u32[]{:S(2)}) collective-permute-start(f32[3,320]{1,0:T(4,128)S(1)} %pad_maximum_fusion.refs_4_), channel_id=1, source_target_pairs={{0,16},{16,0},{1,17},{17,1},{2,18},{18,2},{3,19},{19,3},{4,20},{20... | collective-permute-start | bytes 11528 | tf_op jit(solution)/shard_map/ppermute | solution.py:258
  19.7 1.4 %copy-start = (bf16[1,3,3,320,320]{4,3,2,1,0:T(8,128)(2,1)}, bf16[1,3,3,320,320]{4,3,2,1,0:T(8,128)(2,1)S(1)}, u32[]{:S(2)}) copy-start(bf16[1,3,3,320,320]{4,3,2,1,0:T(8,128)(2,1)S(1)} %collective-permute-done.3.refs_7_) | copy-start | bytes 5529604
  29.6 14.6 %collective-permute-start.6 = (bf16[2,6,192,320]{3,2,1,0:T(8,128)(2,1)S(1)}, bf16[2,6,192,320]{3,2,1,0:T(8,128)(2,1)S(1)}, u32[]{:S(2)}, u32[]{:S(2)}) collective-permute-start(bf16[2,6,192,320]{3,2,1,0:T(8,128)(2,1)S(1)} %get-tuple-element.20.refs_8_), channel_id=1, source_target_pairs={{0,16},{16,0},{1,17},{17,1},{2,18},{18,2},{3,19},{19,3},{4,20},{20... | collective-permute-start | bytes 4423688 | tf_op jit(solution)/shard_map/ppermute | solution.py:258
  31.4 12.8 %collective-permute-start.4 = (bf16[2,192,320]{2,1,0:T(8,128)(2,1)S(1)}, bf16[2,192,320]{2,1,0:T(8,128)(2,1)S(1)}, u32[]{:S(2)}, u32[]{:S(2)}) collective-permute-start(bf16[2,192,320]{2,1,0:T(8,128)(2,1)S(1)} %get-tuple-element.17), channel_id=1, source_target_pairs={{0,1},{1,0},{2,3},{3,2},{4,5},{5,4},{6,7},{7,6},{8,9},{9,8},{10,11... | collective-permute-start | bytes 737288 | tf_op jit(solution)/shard_map/ppermute | solution.py:325
  31.7 12.5 %collective-permute-start.5 = (bf16[2,192,320]{2,1,0:T(8,128)(2,1)S(1)}, bf16[2,192,320]{2,1,0:T(8,128)(2,1)S(1)}, u32[]{:S(2)}, u32[]{:S(2)}) collective-permute-start(bf16[2,192,320]{2,1,0:T(8,128)(2,1)S(1)} %get-tuple-element.18), channel_id=1, source_target_pairs={{0,15},{1,2},{2,1},{3,4},{4,3},{5,6},{6,5},{7,8},{8,7},{9,10},{10,... | collective-permute-start | bytes 737288 | tf_op jit(solution)/shard_map/ppermute | solution.py:326
  52.8 5.8 %collective-permute-start.7 = (bf16[2,6,192,320]{3,2,1,0:T(8,128)(2,1)S(1)}, bf16[2,6,192,320]{3,2,1,0:T(8,128)(2,1)S(1)}, u32[]{:S(2)}, u32[]{:S(2)}) collective-permute-start(bf16[2,6,192,320]{3,2,1,0:T(8,128)(2,1)S(1)} %get-tuple-element.22), channel_id=1, source_target_pairs={{0,16},{16,0},{1,17},{17,1},{2,18},{18,2},{3,19},{19,3},{4,20},{20... | collective-permute-start | bytes 4423688 | tf_op jit(solution)/shard_map/ppermute | solution.py:258

commit v3 on v2

v3 whole, which is shorter than its diff:
```python
import jax
import jax.numpy as jnp
from jax import lax
from jax.experimental import pallas as pl
from jax.experimental.pallas import tpu as pltpu
from jax.sharding import PartitionSpec as P

GROUPS = 32
HEAD = 5
EARLY = (2, 6)
CHUNKS = ((2, 2, 2), (2, 2, 2))
F32 = jnp.float32
BF16 = jnp.bfloat16
ANY = pl.BlockSpec(memory_space=pl.ANY)
VM = pl.BlockSpec(memory_space=pltpu.VMEM)
HBM = pl.BlockSpec(memory_space=pltpu.HBM)


def one_hot(shape, channel_dim, per_group):
    channel = lax.broadcasted_iota(jnp.int32, shape, channel_dim)
    group = lax.broadcasted_iota(jnp.int32, shape, 1 - channel_dim)
    low = group * per_group
    return jnp.where((channel >= low) & (channel < low + per_group), 1.0, 0.0).astype(BF16)


def exact_dot(values, selector):
    high = values.astype(BF16)
    rest = values - high.astype(F32)
    middle = rest.astype(BF16)
    low = (rest - middle.astype(F32)).astype(BF16)
    return (
        jnp.dot(high, selector, preferred_element_type=F32)
        + jnp.dot(middle, selector, preferred_element_type=F32)
        + jnp.dot(low, selector, preferred_element_type=F32)
    )


def send_group_sums(sums, stats_out, per_group):
    channels = sums.shape[1]
    grouped = exact_dot(sums, one_hot((channels, 128), 0, per_group))
    for i in range(stats_out.shape[0]):
        stats_out[i] = grouped


def fold_rows(block):
    return block.reshape(block.shape[0] // 8, 8, block.shape[1]).sum(axis=0)


def stats_kernel(x_any, stats_out, ha_out, hb_out, x_buf, sem):
    n, rows, cols, ch = x_buf.shape
    sec = lax.axis_index("section")
    even = lax.axis_index("space") % 2 == 0
    loads = []
    for s in range(n):
        cp = pltpu.make_async_copy(x_any.at[sec * n + s], x_buf.at[s], sem.at[s])
        cp.start()
        loads.append(cp)
    total = []
    row_a = jnp.where(even, rows - 1, 0)
    for s in range(n):
        loads[s].wait()
        ha_out[s] = x_buf[s, row_a]
        hb_out[s] = x_buf[s, rows - 1 - row_a]

        def step(r, carry):
            acc, sq = carry
            v = x_buf[s, r].astype(F32)
            return acc + fold_rows(v), sq + fold_rows(v * v)

        zero = jnp.zeros((8, ch), F32)
        acc, sq = lax.fori_loop(0, rows, step, (zero, zero))
        total += [acc.sum(axis=0, keepdims=True), sq.sum(axis=0, keepdims=True)]
    sums = jnp.concatenate(total + [jnp.zeros((8 - len(total), ch), F32)], axis=0)
    send_group_sums(sums, stats_out, ch // GROUPS)


def lay_out(src, k, dst):
    ch = src.shape[-1]
    rem = ch - 256
    for dr in range(3):
        for dc in range(3):
            dst[dr * 256 : dr * 256 + 256, dc * 256 : dc * 256 + 256] = src[k, dr, dc, 0:256, 0:256]
            dst[768 + dr * rem : 768 + dr * rem + rem, dc * 256 : dc * 256 + 256] = src[k, dr, dc, 256:ch, 0:256]
        right = [src[k, dr, dc, :, 256:ch].astype(F32) for dc in range(3)]
        right = jnp.concatenate(right + [jnp.zeros((ch, 256 - 3 * rem), F32)], axis=1).astype(BF16)
        dst[dr * 256 : dr * 256 + 256, 768:1024] = right[0:256]
        dst[768 + dr * rem : 768 + dr * rem + rem, 768:1024] = right[256:ch]
    dst[768 + 3 * rem : 1024, :] = jnp.zeros((256 - 3 * rem, 1024), BF16)


def load_kernel(index, own_k, other_k, dst, sem):
    sec = lax.axis_index("section")

    @pl.when(sec == index)
    def _():
        pltpu.make_async_copy(own_k, dst, sem).start()

    @pl.when(sec != index)
    def _():
        pltpu.make_async_copy(other_k, dst, sem).start()

    return pltpu.make_async_copy(own_k, dst, sem)


def prepare_kernel(own_k, other_k, x_hbm, head_out, w_out, src, sem):
    head = head_out.shape[0]
    kernel_load = load_kernel(0, own_k, other_k, src, sem.at[0])
    at = lax.axis_index("section") * (x_hbm.shape[0] // 2)
    load = pltpu.make_async_copy(x_hbm.at[at, pl.ds(0, head)], head_out, sem.at[1])
    load.start()
    kernel_load.wait()
    lay_out(src, 0, w_out)
    load.wait()


def conv_kernel(index, members, n_space, chunks, *refs):
    if index == 0:
        (ra_ref, rb_ref, stats_ref, own_p, other_p, head_ref, w_ref, lat_hbm,
         y_out, stats_out, ha_out, hb_out,
         xm, xr, rem_buf, z_buf, lat_buf, sem) = refs
        head = head_ref.shape[0]
        loads = []
    else:
        (ra_ref, rb_ref, stats_ref, own_p, other_p, x_ref, own_k, other_k, lat_hbm,
         send_out, keep_out,
         xm, xr, rem_buf, z_buf, lat_buf, sem, w_ref, src) = refs
        head = 0
        kernel_load = load_kernel(1, own_k, other_k, src, sem.at[2])
        loads = []
    n, rows, cols, ch = lat_buf.shape
    padded_rows = rows + 2
    rem = ch - 256
    sec = lax.axis_index("section")
    space = lax.axis_index("space")
    even = space % 2 == 0
    for s in range(n):
        low = head if s == 0 else 0
        loads.append(
            pltpu.make_async_copy(
                lat_hbm.at[sec * n + s, pl.ds(low, rows - low)], lat_buf.at[s, pl.ds(low, rows - low)], sem.at[s]
            )
        )
    for cp in loads:
        cp.start()

    def source_row(s, r):
        if index == 1:
            return x_ref[s, r]
        if s == 0 and r < head:
            return head_ref[r]
        return lat_buf[s, r]

    params = jnp.where(sec == index, own_p[...], other_p[...])
    gain, shift, bias = params[0:1], params[1:2], params[2:3]
    total = stats_ref[0]
    for i in range(1, n_space):
        total = total + stats_ref[i]
    packed = []
    for s in range(n):
        mean = total[2 * s : 2 * s + 1] * (1.0 / members)
        var = jnp.maximum(total[2 * s + 1 : 2 * s + 2] * (1.0 / members) - mean * mean, 0.0)
        packed += [mean, lax.rsqrt(var + 1e-05)]
    packed = jnp.concatenate(packed + [jnp.zeros((8 - 2 * n, 128), F32)], axis=0)
    spread = exact_dot(packed, one_hot((128, ch), 1, ch // GROUPS))
    half_a = [0.5 * (spread[2 * s + 1 : 2 * s + 2] * gain) for s in range(n)]
    half_b = [0.5 * shift - spread[2 * s : 2 * s + 1] * half_a[s] for s in range(n)]

    def normalize(s, j):
        if j == 0:
            source = jnp.where(even, rb_ref[s], ra_ref[s])
        elif j == padded_rows - 1:
            source = jnp.where(even, ra_ref[s], rb_ref[s])
        else:
            source = source_row(s, j - 1)
        half = source.astype(F32) * half_a[s] + half_b[s]
        y = half + half * jnp.tanh(half)
        if j == 0:
            y = jnp.where(space == 0, 0.0, y)
        if j == padded_rows - 1:
            y = jnp.where(space == n_space - 1, 0.0, y)
        xm[s, pl.ds(j * cols, cols), :] = y[:, 0:256].astype(BF16)
        rem_buf[s, j] = y[:, 256:ch]
        if j >= 2:
            parts = [rem_buf[s, j - 2], rem_buf[s, j - 1], rem_buf[s, j], jnp.zeros((cols, 256 - 3 * rem), F32)]
            xr[s, pl.ds((j - 2) * cols, cols), :] = jnp.concatenate(parts, axis=1).astype(BF16)

    def multiply(s, r0, count, slot):
        m = count * cols
        lhs = jnp.concatenate(
            [xm[s, pl.ds((r0 + dr) * cols, m), :] for dr in range(3)] + [xr[s, pl.ds(r0 * cols, m), :]],
            axis=1,
        )
        z_buf[slot, 0:m, :] = jnp.dot(lhs, w_ref[...], preferred_element_type=F32)

    first_slab = lax.broadcasted_iota(jnp.int32, (8, 256), 0) == 0
    last_slab = lax.broadcasted_iota(jnp.int32, (8, 256), 0) == 7

    def down(z, width):
        moved = pltpu.roll(z, 1, 0)
        head = jnp.where(first_slab[:, :width], 0.0, moved[0:8])
        return jnp.concatenate([head, moved[8:]], axis=0)

    def up(z, width):
        moved = pltpu.roll(z, cols - 1, 0)
        tail = jnp.where(last_slab[:, :width], 0.0, moved[cols - 8 :])
        return jnp.concatenate([moved[: cols - 8], tail], axis=0)

    acc = [[jnp.zeros((8, ch), F32) for _ in range(2)] for _ in range(n)]

    def finish_row(s, r, slot, at):
        at = pl.ds(at * cols, cols)
        main = z_buf[slot, at, 256:512] + down(z_buf[slot, at, 0:256], 256) + up(z_buf[slot, at, 512:768], 256)
        left = z_buf[slot, at, 768:896]
        right = z_buf[slot, at, 896:1024]
        side = down(left, 128) + pltpu.roll(left, 64, 1) + up(right, 128)
        out = jnp.concatenate([main, side[:, 0:rem]], axis=1) + bias
        if index == 1:
            out = out + lat_buf[s, r].astype(F32)
        rounded = out.astype(BF16)
        if index == 0:
            y_out[s, r] = rounded
            back = rounded.astype(F32)
            acc[s][0] = acc[s][0] + fold_rows(back)
            acc[s][1] = acc[s][1] + fold_rows(back * back)
        else:
            kept = source_row(s, r)
            send_out[s, r] = jnp.where(sec == 0, rounded, kept)
            keep_out[s, r] = jnp.where(sec == 0, kept, rounded)

    row_a = jnp.where(even, rows - 1, 0)
    tasks = []
    for s in range(n):
        r0 = 0
        for count in chunks[s]:
            tasks.append((s, r0, count))
            r0 += count
    pending = None
    done = [0] * n

    def prepare(task):
        s, r0, count = task
        while done[s] < r0 + count + 2:
            normalize(s, done[s])
            done[s] += 1

    def complete(k):
        s, r0, count = tasks[k]
        for r in range(count):
            finish_row(s, r0 + r, k % 2, r)
        if index == 0 and r0 + count == rows:
            ha_out[s] = y_out[s, row_a]
            hb_out[s] = y_out[s, rows - 1 - row_a]

    early = EARLY[index]
    if index == 0:
        for k in range(early):
            prepare(tasks[k])
            multiply(*tasks[k], k % 2)
            if k > 0:
                complete(k - 1)
    else:
        for k in range(early):
            prepare(tasks[k])
    if index == 1:
        kernel_load.wait()
        lay_out(src, 0, w_ref)
    for cp in loads:
        cp.wait()
    for k, task in enumerate(tasks):
        if index == 0 and k < early:
            continue
        prepare(task)
        multiply(*task, k % 2)
        if k + 1 < len(tasks):
            prepare(tasks[k + 1])
        if k > 0:
            complete(k - 1)
    complete(len(tasks) - 1)
    if index == 0:
        rows_out = []
        for s in range(n):
            rows_out += [v.sum(axis=0, keepdims=True) for v in acc[s]]
        sums = jnp.concatenate(rows_out + [jnp.zeros((8 - 2 * n, ch), F32)], axis=0)
        send_group_sums(sums, stats_out, ch // GROUPS)


def keep_kernel(keep, full_out, sem):
    n = keep.shape[0]
    cp = pltpu.make_async_copy(keep, full_out.at[pl.ds(n * lax.axis_index("section"), n)], sem)
    cp.start()
    cp.wait()


def finish_kernel(full_in, received, full_out, sem):
    n = received.shape[0]
    at = jnp.where(lax.axis_index("section") == 0, n, 0)
    cp = pltpu.make_async_copy(received, full_out.at[pl.ds(at, n)], sem)
    cp.start()
    cp.wait()


def swap(array):
    return lax.ppermute(array, "section", [(0, 1), (1, 0)])


def on_device(latents, kernels, norm_gain, norm_bias, conv_bias):
    samples, rows, cols, ch = latents.shape
    n = samples // lax.axis_size("section")
    n_space = lax.axis_size("space")
    members = rows * n_space * cols * (ch // GROUPS)
    pairs_a = [(i, i ^ 1) for i in range(n_space)]
    pairs_b = [(i, (i - 1) % n_space if i % 2 == 0 else (i + 1) % n_space) for i in range(n_space)]
    shape = jax.ShapeDtypeStruct
    stats_shape = pltpu.VMEM((n_space, 8, 128), F32)
    edge_shape = pltpu.VMEM((n, cols, ch), BF16)
    part_shape = shape((n, rows, cols, ch), BF16)
    limit = pltpu.CompilerParams(vmem_limit_bytes=32 * 1024 * 1024)

    latents = pltpu.with_memory_space_constraint(latents, pltpu.HBM)
    kernels = pltpu.with_memory_space_constraint(kernels, pltpu.HBM)
    own_p = jnp.concatenate([norm_gain, norm_bias, conv_bias], axis=0)
    other_p = swap(own_p)
    other_k = pltpu.with_memory_space_constraint(swap(kernels), pltpu.HBM)

    stats, ha, hb = pl.pallas_call(
        stats_kernel,
        out_shape=(stats_shape, edge_shape, edge_shape),
        in_specs=[HBM],
        out_specs=(VM, VM, VM),
        scratch_shapes=[
            pltpu.VMEM((n, rows, cols, ch), BF16),
            pltpu.SemaphoreType.DMA((n,)),
        ],
        compiler_params=limit,
        name="stats",
    )(latents)
    ra = lax.ppermute(ha, "space", pairs_a)
    rb = lax.ppermute(hb, "space", pairs_b)
    stats = lax.all_to_all(stats, "space", split_axis=0, concat_axis=0, tiled=True)

    head = HEAD
    w_type = (1024, 1024)

    head_ref, w0 = pl.pallas_call(
        prepare_kernel,
        out_shape=(pltpu.VMEM((head, cols, ch), BF16), pltpu.VMEM(w_type, BF16)),
        in_specs=[HBM, HBM, HBM],
        out_specs=(VM, VM),
        scratch_shapes=[pltpu.VMEM(kernels.shape, BF16), pltpu.SemaphoreType.DMA((2,))],
        compiler_params=pltpu.CompilerParams(vmem_limit_bytes=16 * 1024 * 1024),
        name="prepare",
    )(kernels, other_k, latents)

    chunks = CHUNKS
    most = max(max(c) for c in chunks)

    def conv(index, operands, out_shape):
        body = lambda *refs: conv_kernel(index, members, n_space, chunks, *refs)
        return pl.pallas_call(
            body,
            out_shape=out_shape,
            in_specs=[VM] * 6 + [HBM, HBM, HBM] if index else [VM] * 7 + [HBM],
            out_specs=(VM,) * len(out_shape),
            scratch_shapes=[
                pltpu.VMEM((n, (rows + 2) * cols, 256), BF16),
                pltpu.VMEM((n, rows * cols, 256), BF16),
                pltpu.VMEM((n, rows + 2, cols, ch - 256), F32),
                pltpu.VMEM((2, most * cols, 1024), F32),
                pltpu.VMEM((n, rows, cols, ch), BF16),
                pltpu.SemaphoreType.DMA((n + 1,)),
                *([pltpu.VMEM(w_type, BF16), pltpu.VMEM(kernels.shape, BF16)] if index else []),
            ],
            compiler_params=limit,
            name="conv%d" % index,
        )(*operands)

    first, stats, ha, hb = conv(
        0,
        (ra, rb, stats, own_p, other_p, head_ref, w0, latents),
        (pltpu.VMEM(part_shape.shape, BF16), stats_shape, edge_shape, edge_shape),
    )
    ra = lax.ppermute(ha, "space", pairs_a)
    rb = lax.ppermute(hb, "space", pairs_b)
    stats = lax.all_to_all(stats, "space", split_axis=0, concat_axis=0, tiled=True)
    full_shape = shape((samples, rows, cols, ch), BF16)
    send, keep = conv(1, (ra, rb, stats, own_p, other_p, first, kernels, other_k, latents), (part_shape, part_shape))
    received = swap(send)
    small = pltpu.CompilerParams(vmem_limit_bytes=1024 * 1024)
    full = pl.pallas_call(
        keep_kernel,
        out_shape=full_shape,
        in_specs=[VM],
        out_specs=HBM,
        scratch_shapes=[pltpu.SemaphoreType.DMA],
        compiler_params=small,
        name="keep",
    )(keep)
    full = pl.pallas_call(
        finish_kernel,
        out_shape=full_shape,
        in_specs=[HBM, VM],
        out_specs=HBM,
        scratch_shapes=[pltpu.SemaphoreType.DMA],
        input_output_aliases={0: 0},
        compiler_params=small,
        name="finish",
    )(full, received)
    return full[None]


def solution(mesh):
    return jax.shard_map(
        on_device,
        mesh=mesh,
        in_specs=(
            P("dp", "space", None, None),
            P("section", None, None, None, None),
            P("section", None),
            P("section", None),
            P("section", None),
        ),
        out_specs=P("section", "dp", "space", None, None),
        check_vma=False,
    )
```

time: 60.2 us -> 56.3 us (0.935)
  waiting for transfers between devices: 9.06 us -> 5.83 us
  local copies, waits for them, and re-layouts: 1.36 us -> 0.01 us
  Pallas kernels: 20.9 us -> 21.9 us
  blocking collectives: 10.9 us -> 10.1 us
    ppermute x4 -> x3, waiting for transfers between devices: 4.15 us -> 2.1 us  [swap(): return lax.ppermute(array, 'section', [(0, 1), (1, 0)])]
    unnamed x8 -> x6, local copies, waits for them, and re-layouts: 1.36 us -> 0.01 us
    all_to_all x1, waiting for transfers between devices: 4.9 us -> 3.72 us  [on_device(): lax.all_to_all(stats, 'space', split_axis=0, concat_axis=0, tiled=True)]
    pallas_call x2 -> x4, Pallas kernels: 17.1 us -> 18.2 us  [the longest x2 15 us: conv(): pl.pallas_call(body, out_shape=out_shape, in_specs=[VM] * 6 + [HBM, HBM,...]
    all_to_all x1, blocking collectives: 10.9 us -> 10.1 us  [on_device(): lax.all_to_all(stats, 'space', split_axis=0, concat_axis=0, tiled=True)]
    ppermute x2, starting transfers between devices: 5.46 us -> 6.19 us  [on_device(): rb = lax.ppermute(hb, 'space', pairs_b)]
    ppermute x4 -> x3, starting transfers between devices: 8.17 us -> 7.69 us  [swap(): return lax.ppermute(array, 'section', [(0, 1), (1, 0)])]
  transfers between devices with their start and end apart: 9 -> 8, of which waited for: 3 -> 2; matrix products, arithmetic and copies ran while one was open for 0% -> 0% of each run, Pallas kernels for 4% -> 10%
where the time goes in v3:
time: 56.3 us; the launch traced here: 56 us
  Pallas kernels  21.9 us (39%)
  starting transfers between devices  17.8 us (32%)
  blocking collectives  10.1 us (18%)
  waiting for transfers between devices  5.83 us (10%)
    pallas_call x2, Pallas kernels, conv(): pl.pallas_call(body, out_shape=out_shape, in_specs=[VM] * 6 + [HBM, HBM,...  15 us
    all_to_all x1, blocking collectives, on_device(): lax.all_to_all(stats, 'space', split_axis=0, concat_axis=0, tiled=True)  10.1 us
    ppermute x3, starting transfers between devices, swap(): return lax.ppermute(array, 'section', [(0, 1), (1, 0)])  7.69 us
    ppermute x2, starting transfers between devices, on_device(): rb = lax.ppermute(hb, 'space', pairs_b)  6.19 us
    all_to_all x1, waiting for transfers between devices, on_device(): lax.all_to_all(stats, 'space', split_axis=0, concat_axis=0, tiled=True)  3.72 us
    all_to_all x1, starting transfers between devices, on_device(): lax.all_to_all(stats, 'space', split_axis=0, concat_axis=0, tiled=True)  3.49 us
    pallas_call x1, Pallas kernels, on_device(): pl.pallas_call(stats_kernel, out_shape=(stats_shape, edge_shape, edge_sha...  2.57 us
    ppermute x3, waiting for transfers between devices, swap(): return lax.ppermute(array, 'section', [(0, 1), (1, 0)])  2.1 us
  transfers between devices with their start and end apart: 8, of which 2 were waited for; matrix products, arithmetic and copies ran while one was open for 0% of the time, Pallas kernels for 10%

profile of v3, /device:TPU:1, one launch (start us, length us, event | category | flops | bytes accessed | tf_op | source)
XLA Modules:
  0.0 56.0 jit_solution(5565358944460814001)
XLA Ops:
  0.0 0.0 copy-start
  0.0 0.0 copy-start.1
  0.0 0.0 copy-start.2
  0.0 3.2 %collective-permute-start.3 = (bf16[1,3,3,320,320]{4,3,2,1,0:T(8,128)(2,1)}, bf16[1,3,3,320,320]{4,3,2,1,0:T(8,128)(2,1)}, u32[]{:S(2)}, u32[]{:S(2)}) collective-permute-start(bf16[1,3,3,320,320]{4,3,2,1,0:T(8,128)(2,1)} %refs_6_.1), channel_id=1, source_target_pairs={{0,16},{16,0},{1,17},{17,1},{2,18},{18,2},{3,19},{19,3},{4,20},{20... | collective-permute-start | bytes 5529608 | tf_op jit(solution)/shard_map/ppermute | solution.py:303
  3.2 2.6 %stats.1 = (f32[16,8,128]{2,1,0:T(8,128)}, bf16[2,192,320]{2,1,0:T(8,128)(2,1)}, bf16[2,192,320]{2,1,0:T(8,128)(2,1)}) custom-call(bf16[4,6,192,320]{3,2,1,0:T(8,128)(2,1)} %refs_8_.1), custom_call_target="tpu_custom_call" | custom-call | tf_op jit(solution)/shard_map/stats/pallas_call | solution.py:325
  5.8 0.1 collective-permute-start
  5.9 3.8 %collective-permute-start.1 = (bf16[2,192,320]{2,1,0:T(8,128)(2,1)}, bf16[2,192,320]{2,1,0:T(8,128)(2,1)S(1)}, u32[]{:S(2)}, u32[]{:S(2)}) collective-permute-start(bf16[2,192,320]{2,1,0:T(8,128)(2,1)} %get-tuple-element.17), channel_id=1, source_target_pairs={{0,15},{1,2},{2,1},{3,4},{4,3},{5,6},{6,5},{7,8},{8,7},{9,10},{10,... | collective-permute-start | bytes 737288 | tf_op jit(solution)/shard_map/ppermute | solution.py:338
  9.7 3.5 %all-to-all-start = ((f32[16,8,128]{2,1,0:T(8,128)}), f32[16,8,128]{2,1,0:T(8,128)S(1)}, u32[]{:S(2)}, u32[]{:S(2)}) async-start(f32[16,8,128]{2,1,0:T(8,128)} %get-tuple-element.18), calls=%async_computation | async-start | bytes 131072 | tf_op jit(solution)/shard_map/all_to_all | solution.py:339
  13.2 0.0 copy-done
  13.2 0.0 copy-done.1
  13.3 0.0 copy-done.2
  13.3 0.7 %collective-permute-start.2 = (f32[3,320]{1,0:T(4,128)S(1)}, f32[3,320]{1,0:T(4,128)S(1)}, u32[]{:S(2)}, u32[]{:S(2)}) collective-permute-start(f32[3,320]{1,0:T(4,128)S(1)} %pad_maximum_fusion.refs_3_), channel_id=1, source_target_pairs={{0,16},{16,0},{1,17},{17,1},{2,18},{18,2},{3,19},{19,3},{4,20},{20... | collective-permute-start | bytes 11528 | tf_op jit(solution)/shard_map/ppermute | solution.py:303
  14.0 0.0 collective-permute-done.3.other_k.refs_7_
  14.0 2.0 %prepare.1 = (bf16[5,192,320]{2,1,0:T(8,128)(2,1)S(1)}, bf16[1024,1024]{1,0:T(8,128)(2,1)S(1)}) custom-call(bf16[1,3,3,320,320]{4,3,2,1,0:T(8,128)(2,1)} %refs_6_.1, bf16[1,3,3,320,320]{4,3,2,1,0:T(8,128)(2,1)} %collective-permute-done.3.other_k.refs_7_, bf16[4,6,192,320]{3,2,1,0:T(8,128)(2,1)} %refs_8_.1), custom_call_target="tpu_custom_call" | custom-call | tf_op jit(solution)/shard_map/prepare/pallas_call | solution.py:344
  16.0 0.0 collective-permute-done.2.refs_4_
  16.0 3.7 %all-to-all-done.refs_2_ = f32[16,8,128]{2,1,0:T(8,128)S(1)} async-done(((f32[16,8,128]{2,1,0:T(8,128)}), f32[16,8,128]{2,1,0:T(8,128)S(1)}, u32[]{:S(2)}, u32[]{:S(2)}) %all-to-all-start) | async-done | bytes 65568 | tf_op jit(solution)/shard_map/all_to_all | solution.py:339
  19.7 0.0 collective-permute-done.refs_0_
  19.7 0.0 collective-permute-done.1.refs_1_
  19.7 6.9 %conv0.1 = (bf16[2,6,192,320]{3,2,1,0:T(8,128)(2,1)S(1)}, f32[16,8,128]{2,1,0:T(8,128)S(1)}, bf16[2,192,320]{2,1,0:T(8,128)(2,1)S(1)}, bf16[2,192,320]{2,1,0:T(8,128)(2,1)S(1)}) custom-call(bf16[2,192,320]{2,1,0:T(8,128)(2,1)S(1)} %collective-permute-done.refs_0_, bf16[2,192,320]{2,1,0:T(8,128)(2,1)S(1)} %collective-permute-done.1.refs_1_, ...), custom_call_target="tpu_custom_call" | custom-call | tf_op jit(solution)/shard_map/conv0/pallas_call | solution.py:359
  26.6 0.4 collective-permute-start.4
  26.9 2.3 %collective-permute-start.5 = (bf16[2,192,320]{2,1,0:T(8,128)(2,1)S(1)}, bf16[2,192,320]{2,1,0:T(8,128)(2,1)S(1)}, u32[]{:S(2)}, u32[]{:S(2)}) collective-permute-start(bf16[2,192,320]{2,1,0:T(8,128)(2,1)S(1)} %get-tuple-element.22), channel_id=1, source_target_pairs={{0,15},{1,2},{2,1},{3,4},{4,3},{5,6},{6,5},{7,8},{8,7},{9,10},{10,... | collective-permute-start | bytes 737288 | tf_op jit(solution)/shard_map/ppermute | solution.py:383
  29.3 10.1 %all_to_all.10.refs_2_ = f32[16,8,128]{2,1,0:T(8,128)S(1)} all-to-all(f32[16,8,128]{2,1,0:T(8,128)S(1)} %get-tuple-element.23), channel_id=1, replica_groups=mesh['dp'=8,'section'=2,'space'=16] {'space'}, dimensions={0} | all-to-all | bytes 131072 | tf_op jit(solution)/shard_map/all_to_all | solution.py:384
  39.4 0.0 collective-permute-done.4.refs_0_
  39.4 0.0 collective-permute-done.5.refs_1_
  39.4 8.1 %conv1.1 = (bf16[2,6,192,320]{3,2,1,0:T(8,128)(2,1)S(1)}, bf16[2,6,192,320]{3,2,1,0:T(8,128)(2,1)S(1)}) custom-call(bf16[2,192,320]{2,1,0:T(8,128)(2,1)S(1)} %collective-permute-done.4.refs_0_, bf16[2,192,320]{2,1,0:T(8,128)(2,1)S(1)} %collective-permute-done.5.refs_1_, f32[16,8,128]{2,1,0:T(8,128)S(1)} %all_to_all.10.refs_2_, ...), custom_call_target="tpu_custom_call" | custom-call | tf_op jit(solution)/shard_map/conv1/pallas_call | solution.py:359
  47.5 3.8 %collective-permute-start.6 = (bf16[2,6,192,320]{3,2,1,0:T(8,128)(2,1)S(1)}, bf16[2,6,192,320]{3,2,1,0:T(8,128)(2,1)S(1)}, u32[]{:S(2)}, u32[]{:S(2)}) collective-permute-start(bf16[2,6,192,320]{3,2,1,0:T(8,128)(2,1)S(1)} %get-tuple-element.26), channel_id=1, source_target_pairs={{0,16},{16,0},{1,17},{17,1},{2,18},{18,2},{3,19},{19,3},{4,20},{20... | collective-permute-start | bytes 4423688 | tf_op jit(solution)/shard_map/ppermute | solution.py:303
  51.3 1.2 %keep.1.full_in = bf16[4,6,192,320]{3,2,1,0:T(8,128)(2,1)} custom-call(bf16[2,6,192,320]{3,2,1,0:T(8,128)(2,1)S(1)} %get-tuple-element.25.keep), custom_call_target="tpu_custom_call" | custom-call | tf_op jit(solution)/shard_map/keep/pallas_call | solution.py:389
  52.5 2.1 %collective-permute-done.6.received = bf16[2,6,192,320]{3,2,1,0:T(8,128)(2,1)S(1)} collective-permute-done((bf16[2,6,192,320]{3,2,1,0:T(8,128)(2,1)S(1)}, bf16[2,6,192,320]{3,2,1,0:T(8,128)(2,1)S(1)}, u32[]{:S(2)}, u32[]{:S(2)}) %collective-permute-start.6) | collective-permute-done | bytes 1474592 | tf_op jit(solution)/shard_map/ppermute | solution.py:303
  54.6 1.2 %finish.1 = bf16[4,6,192,320]{3,2,1,0:T(8,128)(2,1)} custom-call(bf16[4,6,192,320]{3,2,1,0:T(8,128)(2,1)} %keep.1.full_in, bf16[2,6,192,320]{3,2,1,0:T(8,128)(2,1)S(1)} %collective-permute-done.6.received), custom_call_target="tpu_custom_call", output_to_operand_aliasing={{}: (0, {})} | custom-call | tf_op jit(solution)/shard_map/finish/pallas_call | solution.py:398
  (1 shorter events, 0.0 us)
Async XLA Ops:
  0.0 13.2 %copy-start = (f32[1,320]{1,0:T(1,128)S(1)}, f32[1,320]{1,0:T(1,128)}, u32[]{:S(2)}) copy-start(f32[1,320]{1,0:T(1,128)} %param.9) | copy-start | bytes 3844
  0.0 13.2 %copy-start.1 = (f32[1,320]{1,0:T(1,128)S(1)}, f32[1,320]{1,0:T(1,128)}, u32[]{:S(2)}) copy-start(f32[1,320]{1,0:T(1,128)} %param.8) | copy-start | bytes 3844
  0.0 13.3 %copy-start.2 = (f32[1,320]{1,0:T(1,128)S(1)}, f32[1,320]{1,0:T(1,128)}, u32[]{:S(2)}) copy-start(f32[1,320]{1,0:T(1,128)} %param.7) | copy-start | bytes 3844
  0.0 14.0 %collective-permute-start.3 = (bf16[1,3,3,320,320]{4,3,2,1,0:T(8,128)(2,1)}, bf16[1,3,3,320,320]{4,3,2,1,0:T(8,128)(2,1)}, u32[]{:S(2)}, u32[]{:S(2)}) collective-permute-start(bf16[1,3,3,320,320]{4,3,2,1,0:T(8,128)(2,1)} %refs_6_.1), channel_id=1, source_target_pairs={{0,16},{16,0},{1,17},{17,1},{2,18},{18,2},{3,19},{19,3},{4,20},{20... | collective-permute-start | bytes 5529608 | tf_op jit(solution)/shard_map/ppermute | solution.py:303
  5.8 13.9 %collective-permute-start = (bf16[2,192,320]{2,1,0:T(8,128)(2,1)}, bf16[2,192,320]{2,1,0:T(8,128)(2,1)S(1)}, u32[]{:S(2)}, u32[]{:S(2)}) collective-permute-start(bf16[2,192,320]{2,1,0:T(8,128)(2,1)} %get-tuple-element.16), channel_id=1, source_target_pairs={{0,1},{1,0},{2,3},{3,2},{4,5},{5,4},{6,7},{7,6},{8,9},{9,8},{10,11... | collective-permute-start | bytes 737288 | tf_op jit(solution)/shard_map/ppermute | solution.py:337
  5.9 13.8 %collective-permute-start.1 = (bf16[2,192,320]{2,1,0:T(8,128)(2,1)}, bf16[2,192,320]{2,1,0:T(8,128)(2,1)S(1)}, u32[]{:S(2)}, u32[]{:S(2)}) collective-permute-start(bf16[2,192,320]{2,1,0:T(8,128)(2,1)} %get-tuple-element.17), channel_id=1, source_target_pairs={{0,15},{1,2},{2,1},{3,4},{4,3},{5,6},{6,5},{7,8},{8,7},{9,10},{10,... | collective-permute-start | bytes 737288 | tf_op jit(solution)/shard_map/ppermute | solution.py:338
  9.7 10.0 %all-to-all-start = ((f32[16,8,128]{2,1,0:T(8,128)}), f32[16,8,128]{2,1,0:T(8,128)S(1)}, u32[]{:S(2)}, u32[]{:S(2)}) async-start(f32[16,8,128]{2,1,0:T(8,128)} %get-tuple-element.18), calls=%async_computation | async-start | bytes 131072 | tf_op jit(solution)/shard_map/all_to_all | solution.py:339
  13.3 2.7 %collective-permute-start.2 = (f32[3,320]{1,0:T(4,128)S(1)}, f32[3,320]{1,0:T(4,128)S(1)}, u32[]{:S(2)}, u32[]{:S(2)}) collective-permute-start(f32[3,320]{1,0:T(4,128)S(1)} %pad_maximum_fusion.refs_3_), channel_id=1, source_target_pairs={{0,16},{16,0},{1,17},{17,1},{2,18},{18,2},{3,19},{19,3},{4,20},{20... | collective-permute-start | bytes 11528 | tf_op jit(solution)/shard_map/ppermute | solution.py:303
  26.6 12.8 %collective-permute-start.4 = (bf16[2,192,320]{2,1,0:T(8,128)(2,1)S(1)}, bf16[2,192,320]{2,1,0:T(8,128)(2,1)S(1)}, u32[]{:S(2)}, u32[]{:S(2)}) collective-permute-start(bf16[2,192,320]{2,1,0:T(8,128)(2,1)S(1)} %get-tuple-element.21), channel_id=1, source_target_pairs={{0,1},{1,0},{2,3},{3,2},{4,5},{5,4},{6,7},{7,6},{8,9},{9,8},{10,11... | collective-permute-start | bytes 737288 | tf_op jit(solution)/shard_map/ppermute | solution.py:382
  26.9 12.5 %collective-permute-start.5 = (bf16[2,192,320]{2,1,0:T(8,128)(2,1)S(1)}, bf16[2,192,320]{2,1,0:T(8,128)(2,1)S(1)}, u32[]{:S(2)}, u32[]{:S(2)}) collective-permute-start(bf16[2,192,320]{2,1,0:T(8,128)(2,1)S(1)} %get-tuple-element.22), channel_id=1, source_target_pairs={{0,15},{1,2},{2,1},{3,4},{4,3},{5,6},{6,5},{7,8},{8,7},{9,10},{10,... | collective-permute-start | bytes 737288 | tf_op jit(solution)/shard_map/ppermute | solution.py:383
  47.5 7.1 %collective-permute-start.6 = (bf16[2,6,192,320]{3,2,1,0:T(8,128)(2,1)S(1)}, bf16[2,6,192,320]{3,2,1,0:T(8,128)(2,1)S(1)}, u32[]{:S(2)}, u32[]{:S(2)}) collective-permute-start(bf16[2,6,192,320]{3,2,1,0:T(8,128)(2,1)S(1)} %get-tuple-element.26), channel_id=1, source_target_pairs={{0,16},{16,0},{1,17},{17,1},{2,18},{18,2},{3,19},{19,3},{4,20},{20... | collective-permute-start | bytes 4423688 | tf_op jit(solution)/shard_map/ppermute | solution.py:303

commit v4 on v3

--- a/solution.py
+++ b/solution.py
@@ -7,7 +7,7 @@
 
 GROUPS = 32
 HEAD = 5
-EARLY = (2, 6)
+EARLY = (2, 3, 1)
 CHUNKS = ((2, 2, 2), (2, 2, 2))
 F32 = jnp.float32
 BF16 = jnp.bfloat16
@@ -113,35 +113,47 @@
     load.wait()
 
 
-def conv_kernel(index, members, n_space, chunks, *refs):
+def conv_kernel(index, which, members, n_space, chunks, *refs):
     if index == 0:
         (ra_ref, rb_ref, stats_ref, own_p, other_p, head_ref, w_ref, lat_hbm,
          y_out, stats_out, ha_out, hb_out,
          xm, xr, rem_buf, z_buf, lat_buf, sem) = refs
         head = head_ref.shape[0]
         loads = []
-    else:
+    elif which == 0:
         (ra_ref, rb_ref, stats_ref, own_p, other_p, x_ref, own_k, other_k, lat_hbm,
-         send_out, keep_out,
-         xm, xr, rem_buf, z_buf, lat_buf, sem, w_ref, src) = refs
+         send_out, keep_out, w_ref, lat_next,
+         xm, xr, rem_buf, z_buf, lat_buf, sem, src) = refs
         head = 0
         kernel_load = load_kernel(1, own_k, other_k, src, sem.at[2])
         loads = []
-    n, rows, cols, ch = lat_buf.shape
+    else:
+        (ra_ref, rb_ref, stats_ref, own_p, other_p, x_ref, w_ref, lat_next,
+         send_out, keep_out,
+         xm, xr, rem_buf, z_buf) = refs
+        loads = []
+    n, rows, cols, ch = lat_buf.shape if index == 0 else x_ref.shape
+    chosen = range(n) if index == 0 else (which,)
     padded_rows = rows + 2
     rem = ch - 256
     sec = lax.axis_index("section")
     space = lax.axis_index("space")
     even = space % 2 == 0
-    for s in range(n):
-        low = head if s == 0 else 0
-        loads.append(
-            pltpu.make_async_copy(
-                lat_hbm.at[sec * n + s, pl.ds(low, rows - low)], lat_buf.at[s, pl.ds(low, rows - low)], sem.at[s]
+    if index == 0:
+        for s in range(n):
+            low = head if s == 0 else 0
+            loads.append(
+                pltpu.make_async_copy(
+                    lat_hbm.at[sec * n + s, pl.ds(low, rows - low)], lat_buf.at[s, pl.ds(low, rows - low)], sem.at[s]
+                )
             )
-        )
+    elif which == 0:
+        loads.append(pltpu.make_async_copy(lat_hbm.at[sec * n], lat_buf.at[0], sem.at[0]))
+        next_load = pltpu.make_async_copy(lat_hbm.at[sec * n + 1], lat_next, sem.at[1])
     for cp in loads:
         cp.start()
+    if index == 1 and which == 0:
+        next_load.start()
 
     def source_row(s, r):
         if index == 1:
@@ -215,7 +227,7 @@
         side = down(left, 128) + pltpu.roll(left, 64, 1) + up(right, 128)
         out = jnp.concatenate([main, side[:, 0:rem]], axis=1) + bias
         if index == 1:
-            out = out + lat_buf[s, r].astype(F32)
+            out = out + (lat_buf[0, r] if which == 0 else lat_next[r]).astype(F32)
         rounded = out.astype(BF16)
         if index == 0:
             y_out[s, r] = rounded
@@ -224,12 +236,12 @@
             acc[s][1] = acc[s][1] + fold_rows(back * back)
         else:
             kept = source_row(s, r)
-            send_out[s, r] = jnp.where(sec == 0, rounded, kept)
-            keep_out[s, r] = jnp.where(sec == 0, kept, rounded)
+            send_out[r] = jnp.where(sec == 0, rounded, kept)
+            keep_out[r] = jnp.where(sec == 0, kept, rounded)
 
     row_a = jnp.where(even, rows - 1, 0)
     tasks = []
-    for s in range(n):
+    for s in chosen:
         r0 = 0
         for count in chunks[s]:
             tasks.append((s, r0, count))
@@ -251,7 +263,7 @@
             ha_out[s] = y_out[s, row_a]
             hb_out[s] = y_out[s, rows - 1 - row_a]
 
-    early = EARLY[index]
+    early = EARLY[index + which]
     if index == 0:
         for k in range(early):
             prepare(tasks[k])
@@ -261,7 +273,7 @@
     else:
         for k in range(early):
             prepare(tasks[k])
-    if index == 1:
+    if index == 1 and which == 0:
         kernel_load.wait()
         lay_out(src, 0, w_ref)
     for cp in loads:
@@ -276,6 +288,8 @@
         if k > 0:
             complete(k - 1)
     complete(len(tasks) - 1)
+    if index == 1 and which == 0:
+        next_load.wait()
     if index == 0:
         rows_out = []
         for s in range(n):
@@ -284,17 +298,21 @@
         send_group_sums(sums, stats_out, ch // GROUPS)
 
 
-def keep_kernel(keep, full_out, sem):
-    n = keep.shape[0]
-    cp = pltpu.make_async_copy(keep, full_out.at[pl.ds(n * lax.axis_index("section"), n)], sem)
-    cp.start()
-    cp.wait()
+def keep_kernel(keep_0, keep_1, received, full_out, sem):
+    sec = lax.axis_index("section")
+    copies = [
+        pltpu.make_async_copy(keep_0, full_out.at[2 * sec], sem.at[0]),
+        pltpu.make_async_copy(keep_1, full_out.at[2 * sec + 1], sem.at[1]),
+        pltpu.make_async_copy(received, full_out.at[2 - 2 * sec], sem.at[2]),
+    ]
+    for cp in copies:
+        cp.start()
+    for cp in copies:
+        cp.wait()
 
 
 def finish_kernel(full_in, received, full_out, sem):
-    n = received.shape[0]
-    at = jnp.where(lax.axis_index("section") == 0, n, 0)
-    cp = pltpu.make_async_copy(received, full_out.at[pl.ds(at, n)], sem)
+    cp = pltpu.make_async_copy(received, full_out.at[3 - 2 * lax.axis_index("section")], sem)
     cp.start()
     cp.wait()
 
@@ -354,27 +372,37 @@
     chunks = CHUNKS
     most = max(max(c) for c in chunks)
 
-    def conv(index, operands, out_shape):
-        body = lambda *refs: conv_kernel(index, members, n_space, chunks, *refs)
+    def conv(index, which, operands, out_shape):
+        body = lambda *refs: conv_kernel(index, which, members, n_space, chunks, *refs)
+        in_hbm = (1, 3, 0)[index + which]
+        if index == 0:
+            extra = [pltpu.VMEM((n, rows, cols, ch), BF16), pltpu.SemaphoreType.DMA((n,))]
+        elif which == 0:
+            extra = [
+                pltpu.VMEM((1, rows, cols, ch), BF16),
+                pltpu.SemaphoreType.DMA((3,)),
+                pltpu.VMEM(kernels.shape, BF16),
+            ]
+        else:
+            extra = []
         return pl.pallas_call(
             body,
             out_shape=out_shape,
-            in_specs=[VM] * 6 + [HBM, HBM, HBM] if index else [VM] * 7 + [HBM],
+            in_specs=[VM] * (len(operands) - in_hbm) + [HBM] * in_hbm,
             out_specs=(VM,) * len(out_shape),
             scratch_shapes=[
                 pltpu.VMEM((n, (rows + 2) * cols, 256), BF16),
                 pltpu.VMEM((n, rows * cols, 256), BF16),
                 pltpu.VMEM((n, rows + 2, cols, ch - 256), F32),
                 pltpu.VMEM((2, most * cols, 1024), F32),
-                pltpu.VMEM((n, rows, cols, ch), BF16),
-                pltpu.SemaphoreType.DMA((n + 1,)),
-                *([pltpu.VMEM(w_type, BF16), pltpu.VMEM(kernels.shape, BF16)] if index else []),
+                *extra,
             ],
             compiler_params=limit,
-            name="conv%d" % index,
+            name="conv%d%d" % (index, which),
         )(*operands)
 
     first, stats, ha, hb = conv(
+        0,
         0,
         (ra, rb, stats, own_p, other_p, head_ref, w0, latents),
         (pltpu.VMEM(part_shape.shape, BF16), stats_shape, edge_shape, edge_shape),
@@ -383,18 +411,24 @@
     rb = lax.ppermute(hb, "space", pairs_b)
     stats = lax.all_to_all(stats, "space", split_axis=0, concat_axis=0, tiled=True)
     full_shape = shape((samples, rows, cols, ch), BF16)
-    send, keep = conv(1, (ra, rb, stats, own_p, other_p, first, kernels, other_k, latents), (part_shape, part_shape))
-    received = swap(send)
+    common = (ra, rb, stats, own_p, other_p, first)
+    sample_shape = pltpu.VMEM((rows, cols, ch), BF16)
+    send_0, keep_0, w1, lat_next = conv(
+        1, 0, (*common, kernels, other_k, latents), (sample_shape, sample_shape, pltpu.VMEM(w_type, BF16), sample_shape)
+    )
+    received_0 = swap(send_0)
+    send_1, keep_1 = conv(1, 1, (*common, w1, lat_next), (sample_shape, sample_shape))
+    received_1 = swap(send_1)
     small = pltpu.CompilerParams(vmem_limit_bytes=1024 * 1024)
     full = pl.pallas_call(
         keep_kernel,
         out_shape=full_shape,
-        in_specs=[VM],
+        in_specs=[VM, VM, VM],
         out_specs=HBM,
-        scratch_shapes=[pltpu.SemaphoreType.DMA],
+        scratch_shapes=[pltpu.SemaphoreType.DMA((3,))],
         compiler_params=small,
         name="keep",
-    )(keep)
+    )(keep_0, keep_1, received_0)
     full = pl.pallas_call(
         finish_kernel,
         out_shape=full_shape,
@@ -404,7 +438,7 @@
         input_output_aliases={0: 0},
         compiler_params=small,
         name="finish",
-    )(full, received)
+    )(full, received_1)
     return full[None]
 
 

time: 56.3 us -> 55.4 us (0.984)
  waiting for transfers between devices: 5.83 us -> 4.6 us
    ppermute x3 -> x4, waiting for transfers between devices: 2.1 us -> 0.87 us  [swap(): return lax.ppermute(array, 'section', [(0, 1), (1, 0)])]
    pallas_call x3 -> x4, Pallas kernels: 16.2 us -> 16.7 us  [the longest x3 15.1 us: conv(): pl.pallas_call(body, out_shape=out_shape, in_specs=[VM] * (len(operands)...]
    ppermute x3 -> x4, starting transfers between devices: 7.69 us -> 7.79 us  [swap(): return lax.ppermute(array, 'section', [(0, 1), (1, 0)])]
  transfers between devices with their start and end apart: 8 -> 9, of which waited for: 2 -> 2; matrix products, arithmetic and copies ran while one was open for 0% -> 0% of each run, Pallas kernels for 10% -> 17%
where the time goes in v4:
time: 55.4 us; the launch traced here: 55.1 us
  Pallas kernels  22.2 us (40%)
  starting transfers between devices  17.9 us (32%)
  blocking collectives  10.1 us (18%)
  waiting for transfers between devices  4.6 us (8%)
    pallas_call x3, Pallas kernels, conv(): pl.pallas_call(body, out_shape=out_shape, in_specs=[VM] * (len(operands)...  15.1 us
    all_to_all x1, blocking collectives, on_device(): lax.all_to_all(stats, 'space', split_axis=0, concat_axis=0, tiled=True)  10.1 us
    ppermute x4, starting transfers between devices, swap(): return lax.ppermute(array, 'section', [(0, 1), (1, 0)])  7.79 us
    ppermute x2, starting transfers between devices, on_device(): rb = lax.ppermute(hb, 'space', pairs_b)  6.19 us
    all_to_all x1, waiting for transfers between devices, on_device(): lax.all_to_all(stats, 'space', split_axis=0, concat_axis=0, tiled=True)  3.72 us
    all_to_all x1, starting transfers between devices, on_device(): lax.all_to_all(stats, 'space', split_axis=0, concat_axis=0, tiled=True)  3.49 us
    pallas_call x1, Pallas kernels, on_device(): pl.pallas_call(stats_kernel, out_shape=(stats_shape, edge_shape, edge_sha...  2.58 us
    pallas_call x1, Pallas kernels, on_device(): pl.pallas_call(prepare_kernel, out_shape=(pltpu.VMEM((head, cols, ch), BF...  1.99 us
  transfers between devices with their start and end apart: 9, of which 2 were waited for; matrix products, arithmetic and copies ran while one was open for 0% of the time, Pallas kernels for 17%

profile of v4, /device:TPU:1, one launch (start us, length us, event | category | flops | bytes accessed | tf_op | source)
XLA Modules:
  0.0 55.1 jit_solution(12542449850148444861)
XLA Ops:
  0.0 0.0 copy-start
  0.0 0.0 copy-start.1
  0.0 0.0 copy-start.2
  0.0 3.2 %collective-permute-start.3 = (bf16[1,3,3,320,320]{4,3,2,1,0:T(8,128)(2,1)}, bf16[1,3,3,320,320]{4,3,2,1,0:T(8,128)(2,1)}, u32[]{:S(2)}, u32[]{:S(2)}) collective-permute-start(bf16[1,3,3,320,320]{4,3,2,1,0:T(8,128)(2,1)} %refs_6_.1), channel_id=1, source_target_pairs={{0,16},{16,0},{1,17},{17,1},{2,18},{18,2},{3,19},{19,3},{4,20},{20... | collective-permute-start | bytes 5529608 | tf_op jit(solution)/shard_map/ppermute | solution.py:321
  3.2 2.6 %stats.1 = (f32[16,8,128]{2,1,0:T(8,128)}, bf16[2,192,320]{2,1,0:T(8,128)(2,1)}, bf16[2,192,320]{2,1,0:T(8,128)(2,1)}) custom-call(bf16[4,6,192,320]{3,2,1,0:T(8,128)(2,1)} %refs_8_.1), custom_call_target="tpu_custom_call" | custom-call | tf_op jit(solution)/shard_map/stats/pallas_call | solution.py:343
  5.8 0.1 collective-permute-start
  5.9 3.8 %collective-permute-start.1 = (bf16[2,192,320]{2,1,0:T(8,128)(2,1)}, bf16[2,192,320]{2,1,0:T(8,128)(2,1)S(1)}, u32[]{:S(2)}, u32[]{:S(2)}) collective-permute-start(bf16[2,192,320]{2,1,0:T(8,128)(2,1)} %get-tuple-element.21), channel_id=1, source_target_pairs={{0,15},{1,2},{2,1},{3,4},{4,3},{5,6},{6,5},{7,8},{8,7},{9,10},{10,... | collective-permute-start | bytes 737288 | tf_op jit(solution)/shard_map/ppermute | solution.py:356
  9.7 3.5 %all-to-all-start = ((f32[16,8,128]{2,1,0:T(8,128)}), f32[16,8,128]{2,1,0:T(8,128)S(1)}, u32[]{:S(2)}, u32[]{:S(2)}) async-start(f32[16,8,128]{2,1,0:T(8,128)} %get-tuple-element.22), calls=%async_computation | async-start | bytes 131072 | tf_op jit(solution)/shard_map/all_to_all | solution.py:357
  13.2 0.0 copy-done
  13.2 0.0 copy-done.1
  13.3 0.0 copy-done.2
  13.3 0.7 %collective-permute-start.2 = (f32[3,320]{1,0:T(4,128)S(1)}, f32[3,320]{1,0:T(4,128)S(1)}, u32[]{:S(2)}, u32[]{:S(2)}) collective-permute-start(f32[3,320]{1,0:T(4,128)S(1)} %pad_maximum_fusion.refs_3_), channel_id=1, source_target_pairs={{0,16},{16,0},{1,17},{17,1},{2,18},{18,2},{3,19},{19,3},{4,20},{20... | collective-permute-start | bytes 11528 | tf_op jit(solution)/shard_map/ppermute | solution.py:321
  14.0 0.0 collective-permute-done.3.other_k.refs_7_
  14.0 2.0 %prepare.1 = (bf16[5,192,320]{2,1,0:T(8,128)(2,1)S(1)}, bf16[1024,1024]{1,0:T(8,128)(2,1)S(1)}) custom-call(bf16[1,3,3,320,320]{4,3,2,1,0:T(8,128)(2,1)} %refs_6_.1, bf16[1,3,3,320,320]{4,3,2,1,0:T(8,128)(2,1)} %collective-permute-done.3.other_k.refs_7_, bf16[4,6,192,320]{3,2,1,0:T(8,128)(2,1)} %refs_8_.1), custom_call_target="tpu_custom_call" | custom-call | tf_op jit(solution)/shard_map/prepare/pallas_call | solution.py:362
  16.0 0.0 collective-permute-done.2.refs_4_
  16.0 3.7 %all-to-all-done.refs_2_ = f32[16,8,128]{2,1,0:T(8,128)S(1)} async-done(((f32[16,8,128]{2,1,0:T(8,128)}), f32[16,8,128]{2,1,0:T(8,128)S(1)}, u32[]{:S(2)}, u32[]{:S(2)}) %all-to-all-start) | async-done | bytes 65568 | tf_op jit(solution)/shard_map/all_to_all | solution.py:357
  19.7 0.0 collective-permute-done.refs_0_
  19.7 0.0 collective-permute-done.1.refs_1_
  19.7 6.9 %conv00.1 = (bf16[2,6,192,320]{3,2,1,0:T(8,128)(2,1)S(1)}, f32[16,8,128]{2,1,0:T(8,128)S(1)}, bf16[2,192,320]{2,1,0:T(8,128)(2,1)S(1)}, bf16[2,192,320]{2,1,0:T(8,128)(2,1)S(1)}) custom-call(bf16[2,192,320]{2,1,0:T(8,128)(2,1)S(1)} %collective-permute-done.refs_0_, bf16[2,192,320]{2,1,0:T(8,128)(2,1)S(1)} %collective-permute-done.1.refs_1_, ...), custom_call_target="tpu_custom_call" | custom-call | tf_op jit(solution)/shard_map/conv00/pallas_call | solution.py:388
  26.6 0.4 collective-permute-start.4
  26.9 2.3 %collective-permute-start.5 = (bf16[2,192,320]{2,1,0:T(8,128)(2,1)S(1)}, bf16[2,192,320]{2,1,0:T(8,128)(2,1)S(1)}, u32[]{:S(2)}, u32[]{:S(2)}) collective-permute-start(bf16[2,192,320]{2,1,0:T(8,128)(2,1)S(1)} %get-tuple-element.26), channel_id=1, source_target_pairs={{0,15},{1,2},{2,1},{3,4},{4,3},{5,6},{6,5},{7,8},{8,7},{9,10},{10,... | collective-permute-start | bytes 737288 | tf_op jit(solution)/shard_map/ppermute | solution.py:411
  29.3 10.1 %all_to_all.10.refs_2_ = f32[16,8,128]{2,1,0:T(8,128)S(1)} all-to-all(f32[16,8,128]{2,1,0:T(8,128)S(1)} %get-tuple-element.27), channel_id=1, replica_groups=mesh['dp'=8,'section'=2,'space'=16] {'space'}, dimensions={0} | all-to-all | bytes 131072 | tf_op jit(solution)/shard_map/all_to_all | solution.py:412
  39.4 0.0 collective-permute-done.4.refs_0_
  39.4 0.0 collective-permute-done.5.refs_1_
  39.4 5.0 %conv10.1 = (bf16[6,192,320]{2,1,0:T(8,128)(2,1)S(1)}, bf16[6,192,320]{2,1,0:T(8,128)(2,1)S(1)}, bf16[1024,1024]{1,0:T(8,128)(2,1)S(1)}, bf16[6,192,320]{2,1,0:T(8,128)(2,1)S(1)}) custom-call(bf16[2,192,320]{2,1,0:T(8,128)(2,1)S(1)} %collective-permute-done.4.refs_0_, bf16[2,192,320]{2,1,0:T(8,128)(2,1)S(1)} %collective-permute-done.5.refs_1_, ...), custom_call_target="tpu_custom_call" | custom-call | tf_op jit(solution)/shard_map/conv10/pallas_call | solution.py:388
  44.4 3.8 %collective-permute-start.6 = (bf16[6,192,320]{2,1,0:T(8,128)(2,1)S(1)}, bf16[6,192,320]{2,1,0:T(8,128)(2,1)S(1)}, u32[]{:S(2)}, u32[]{:S(2)}) collective-permute-start(bf16[6,192,320]{2,1,0:T(8,128)(2,1)S(1)} %get-tuple-element.33), channel_id=1, source_target_pairs={{0,16},{16,0},{1,17},{17,1},{2,18},{18,2},{3,19},{19,3},{4,20},{20... | collective-permute-start | bytes 2211848 | tf_op jit(solution)/shard_map/ppermute | solution.py:321
  48.2 3.3 %conv11.1 = (bf16[6,192,320]{2,1,0:T(8,128)(2,1)S(1)}, bf16[6,192,320]{2,1,0:T(8,128)(2,1)S(1)}) custom-call(bf16[2,192,320]{2,1,0:T(8,128)(2,1)S(1)} %collective-permute-done.4.refs_0_, bf16[2,192,320]{2,1,0:T(8,128)(2,1)S(1)} %collective-permute-done.5.refs_1_, f32[16,8,128]{2,1,0:T(8,128)S(1)} %all_to_all.10.refs_2_, ...), custom_call_target="tpu_custom_call" | custom-call | tf_op jit(solution)/shard_map/conv11/pallas_call | solution.py:388
  51.5 0.1 collective-permute-start.7
  51.6 0.0 collective-permute-done.6.received
  51.6 1.5 %keep.1.full_in = bf16[4,6,192,320]{3,2,1,0:T(8,128)(2,1)} custom-call(bf16[6,192,320]{2,1,0:T(8,128)(2,1)S(1)} %get-tuple-element.29.keep_0, bf16[6,192,320]{2,1,0:T(8,128)(2,1)S(1)} %get-tuple-element.32.keep_1, bf16[6,192,320]{2,1,0:T(8,128)(2,1)S(1)} %collective-permute-done.6.received), custom_call_target="tpu_custom_call" | custom-call | tf_op jit(solution)/shard_map/keep/pallas_call | solution.py:423
  53.2 0.9 %collective-permute-done.7.received = bf16[6,192,320]{2,1,0:T(8,128)(2,1)S(1)} collective-permute-done((bf16[6,192,320]{2,1,0:T(8,128)(2,1)S(1)}, bf16[6,192,320]{2,1,0:T(8,128)(2,1)S(1)}, u32[]{:S(2)}, u32[]{:S(2)}) %collective-permute-start.7) | collective-permute-done | bytes 737312 | tf_op jit(solution)/shard_map/ppermute | solution.py:321
  54.0 0.9 %finish.1 = bf16[4,6,192,320]{3,2,1,0:T(8,128)(2,1)} custom-call(bf16[4,6,192,320]{3,2,1,0:T(8,128)(2,1)} %keep.1.full_in, bf16[6,192,320]{2,1,0:T(8,128)(2,1)S(1)} %collective-permute-done.7.received), custom_call_target="tpu_custom_call", output_to_operand_aliasing={{}: (0, {})} | custom-call | tf_op jit(solution)/shard_map/finish/pallas_call | solution.py:432
  (1 shorter events, 0.0 us)
Async XLA Ops:
  0.0 13.2 %copy-start = (f32[1,320]{1,0:T(1,128)S(1)}, f32[1,320]{1,0:T(1,128)}, u32[]{:S(2)}) copy-start(f32[1,320]{1,0:T(1,128)} %param.9) | copy-start | bytes 3844
  0.0 13.2 %copy-start.1 = (f32[1,320]{1,0:T(1,128)S(1)}, f32[1,320]{1,0:T(1,128)}, u32[]{:S(2)}) copy-start(f32[1,320]{1,0:T(1,128)} %param.8) | copy-start | bytes 3844
  0.0 13.3 %copy-start.2 = (f32[1,320]{1,0:T(1,128)S(1)}, f32[1,320]{1,0:T(1,128)}, u32[]{:S(2)}) copy-start(f32[1,320]{1,0:T(1,128)} %param.7) | copy-start | bytes 3844
  0.0 14.0 %collective-permute-start.3 = (bf16[1,3,3,320,320]{4,3,2,1,0:T(8,128)(2,1)}, bf16[1,3,3,320,320]{4,3,2,1,0:T(8,128)(2,1)}, u32[]{:S(2)}, u32[]{:S(2)}) collective-permute-start(bf16[1,3,3,320,320]{4,3,2,1,0:T(8,128)(2,1)} %refs_6_.1), channel_id=1, source_target_pairs={{0,16},{16,0},{1,17},{17,1},{2,18},{18,2},{3,19},{19,3},{4,20},{20... | collective-permute-start | bytes 5529608 | tf_op jit(solution)/shard_map/ppermute | solution.py:321
  5.8 13.9 %collective-permute-start = (bf16[2,192,320]{2,1,0:T(8,128)(2,1)}, bf16[2,192,320]{2,1,0:T(8,128)(2,1)S(1)}, u32[]{:S(2)}, u32[]{:S(2)}) collective-permute-start(bf16[2,192,320]{2,1,0:T(8,128)(2,1)} %get-tuple-element.20), channel_id=1, source_target_pairs={{0,1},{1,0},{2,3},{3,2},{4,5},{5,4},{6,7},{7,6},{8,9},{9,8},{10,11... | collective-permute-start | bytes 737288 | tf_op jit(solution)/shard_map/ppermute | solution.py:355
  5.9 13.8 %collective-permute-start.1 = (bf16[2,192,320]{2,1,0:T(8,128)(2,1)}, bf16[2,192,320]{2,1,0:T(8,128)(2,1)S(1)}, u32[]{:S(2)}, u32[]{:S(2)}) collective-permute-start(bf16[2,192,320]{2,1,0:T(8,128)(2,1)} %get-tuple-element.21), channel_id=1, source_target_pairs={{0,15},{1,2},{2,1},{3,4},{4,3},{5,6},{6,5},{7,8},{8,7},{9,10},{10,... | collective-permute-start | bytes 737288 | tf_op jit(solution)/shard_map/ppermute | solution.py:356
  9.7 9.9 %all-to-all-start = ((f32[16,8,128]{2,1,0:T(8,128)}), f32[16,8,128]{2,1,0:T(8,128)S(1)}, u32[]{:S(2)}, u32[]{:S(2)}) async-start(f32[16,8,128]{2,1,0:T(8,128)} %get-tuple-element.22), calls=%async_computation | async-start | bytes 131072 | tf_op jit(solution)/shard_map/all_to_all | solution.py:357
  13.3 2.7 %collective-permute-start.2 = (f32[3,320]{1,0:T(4,128)S(1)}, f32[3,320]{1,0:T(4,128)S(1)}, u32[]{:S(2)}, u32[]{:S(2)}) collective-permute-start(f32[3,320]{1,0:T(4,128)S(1)} %pad_maximum_fusion.refs_3_), channel_id=1, source_target_pairs={{0,16},{16,0},{1,17},{17,1},{2,18},{18,2},{3,19},{19,3},{4,20},{20... | collective-permute-start | bytes 11528 | tf_op jit(solution)/shard_map/ppermute | solution.py:321
  26.6 12.8 %collective-permute-start.4 = (bf16[2,192,320]{2,1,0:T(8,128)(2,1)S(1)}, bf16[2,192,320]{2,1,0:T(8,128)(2,1)S(1)}, u32[]{:S(2)}, u32[]{:S(2)}) collective-permute-start(bf16[2,192,320]{2,1,0:T(8,128)(2,1)S(1)} %get-tuple-element.25), channel_id=1, source_target_pairs={{0,1},{1,0},{2,3},{3,2},{4,5},{5,4},{6,7},{7,6},{8,9},{9,8},{10,11... | collective-permute-start | bytes 737288 | tf_op jit(solution)/shard_map/ppermute | solution.py:410
  26.9 12.5 %collective-permute-start.5 = (bf16[2,192,320]{2,1,0:T(8,128)(2,1)S(1)}, bf16[2,192,320]{2,1,0:T(8,128)(2,1)S(1)}, u32[]{:S(2)}, u32[]{:S(2)}) collective-permute-start(bf16[2,192,320]{2,1,0:T(8,128)(2,1)S(1)} %get-tuple-element.26), channel_id=1, source_target_pairs={{0,15},{1,2},{2,1},{3,4},{4,3},{5,6},{6,5},{7,8},{8,7},{9,10},{10,... | collective-permute-start | bytes 737288 | tf_op jit(solution)/shard_map/ppermute | solution.py:411
  44.4 7.2 %collective-permute-start.6 = (bf16[6,192,320]{2,1,0:T(8,128)(2,1)S(1)}, bf16[6,192,320]{2,1,0:T(8,128)(2,1)S(1)}, u32[]{:S(2)}, u32[]{:S(2)}) collective-permute-start(bf16[6,192,320]{2,1,0:T(8,128)(2,1)S(1)} %get-tuple-element.33), channel_id=1, source_target_pairs={{0,16},{16,0},{1,17},{17,1},{2,18},{18,2},{3,19},{19,3},{4,20},{20... | collective-permute-start | bytes 2211848 | tf_op jit(solution)/shard_map/ppermute | solution.py:321
  51.5 2.5 %collective-permute-start.7 = (bf16[6,192,320]{2,1,0:T(8,128)(2,1)S(1)}, bf16[6,192,320]{2,1,0:T(8,128)(2,1)S(1)}, u32[]{:S(2)}, u32[]{:S(2)}) collective-permute-start(bf16[6,192,320]{2,1,0:T(8,128)(2,1)S(1)} %get-tuple-element.34), channel_id=1, source_target_pairs={{0,16},{16,0},{1,17},{17,1},{2,18},{18,2},{3,19},{19,3},{4,20},{20... | collective-permute-start | bytes 2211848 | tf_op jit(solution)/shard_map/ppermute | solution.py:321

commit v5 on v4

--- a/solution.py
+++ b/solution.py
@@ -8,7 +8,7 @@
 GROUPS = 32
 HEAD = 5
 EARLY = (2, 3, 1)
-CHUNKS = ((2, 2, 2), (2, 2, 2))
+CHUNKS = ((2, 2, 2), (3, 3))
 F32 = jnp.float32
 BF16 = jnp.bfloat16
 ANY = pl.BlockSpec(memory_space=pl.ANY)
@@ -88,29 +88,30 @@
     dst[768 + 3 * rem : 1024, :] = jnp.zeros((256 - 3 * rem, 1024), BF16)
 
 
-def load_kernel(index, own_k, other_k, dst, sem):
+def prepare_kernel(x_hbm, own_k, other_k, head_out, w0_out, w1_hbm, src, w1_buf, sem):
+    head = head_out.shape[0]
     sec = lax.axis_index("section")
 
-    @pl.when(sec == index)
+    @pl.when(sec == 0)
     def _():
-        pltpu.make_async_copy(own_k, dst, sem).start()
-
-    @pl.when(sec != index)
+        pltpu.make_async_copy(other_k.at[0], src.at[1], sem.at[1]).start()
+        pltpu.make_async_copy(own_k.at[0], src.at[0], sem.at[0]).start()
+
+    @pl.when(sec != 0)
     def _():
-        pltpu.make_async_copy(other_k, dst, sem).start()
-
-    return pltpu.make_async_copy(own_k, dst, sem)
-
-
-def prepare_kernel(own_k, other_k, x_hbm, head_out, w_out, src, sem):
-    head = head_out.shape[0]
-    kernel_load = load_kernel(0, own_k, other_k, src, sem.at[0])
-    at = lax.axis_index("section") * (x_hbm.shape[0] // 2)
-    load = pltpu.make_async_copy(x_hbm.at[at, pl.ds(0, head)], head_out, sem.at[1])
+        pltpu.make_async_copy(own_k.at[0], src.at[1], sem.at[1]).start()
+        pltpu.make_async_copy(other_k.at[0], src.at[0], sem.at[0]).start()
+
+    load = pltpu.make_async_copy(x_hbm.at[sec * (x_hbm.shape[0] // 2), pl.ds(0, head)], head_out, sem.at[2])
     load.start()
-    kernel_load.wait()
-    lay_out(src, 0, w_out)
+    pltpu.make_async_copy(own_k.at[0], src.at[1], sem.at[1]).wait()
+    lay_out(src, 1, w1_buf)
+    store = pltpu.make_async_copy(w1_buf, w1_hbm, sem.at[3])
+    store.start()
+    pltpu.make_async_copy(own_k.at[0], src.at[0], sem.at[0]).wait()
+    lay_out(src, 0, w0_out)
     load.wait()
+    store.wait()
 
 
 def conv_kernel(index, which, members, n_space, chunks, *refs):
@@ -120,18 +121,20 @@
          xm, xr, rem_buf, z_buf, lat_buf, sem) = refs
         head = head_ref.shape[0]
         loads = []
+        planes = [(xm.at[s], xr.at[s]) for s in range(2)]
     elif which == 0:
-        (ra_ref, rb_ref, stats_ref, own_p, other_p, x_ref, own_k, other_k, lat_hbm,
-         send_out, keep_out, w_ref, lat_next,
-         xm, xr, rem_buf, z_buf, lat_buf, sem, src) = refs
+        (ra_ref, rb_ref, stats_ref, own_p, other_p, x_ref, w_hbm, lat_hbm,
+         send_out, keep_out, w_ref, lat_next, xm_next, xr_next,
+         xm, xr, rem_buf, z_buf, lat_buf, sem) = refs
         head = 0
-        kernel_load = load_kernel(1, own_k, other_k, src, sem.at[2])
+        loads = [pltpu.make_async_copy(w_hbm, w_ref, sem.at[2])]
+        planes = [(xm.at[0], xr.at[0]), (xm_next, xr_next)]
+    else:
+        (own_p, other_p, x_ref, w_ref, lat_next, xm_next, xr_next,
+         send_out, keep_out,
+         z_buf) = refs
         loads = []
-    else:
-        (ra_ref, rb_ref, stats_ref, own_p, other_p, x_ref, w_ref, lat_next,
-         send_out, keep_out,
-         xm, xr, rem_buf, z_buf) = refs
-        loads = []
+        planes = [None, (xm_next, xr_next)]
     n, rows, cols, ch = lat_buf.shape if index == 0 else x_ref.shape
     chosen = range(n) if index == 0 else (which,)
     padded_rows = rows + 2
@@ -164,18 +167,19 @@
 
     params = jnp.where(sec == index, own_p[...], other_p[...])
     gain, shift, bias = params[0:1], params[1:2], params[2:3]
-    total = stats_ref[0]
-    for i in range(1, n_space):
-        total = total + stats_ref[i]
-    packed = []
-    for s in range(n):
-        mean = total[2 * s : 2 * s + 1] * (1.0 / members)
-        var = jnp.maximum(total[2 * s + 1 : 2 * s + 2] * (1.0 / members) - mean * mean, 0.0)
-        packed += [mean, lax.rsqrt(var + 1e-05)]
-    packed = jnp.concatenate(packed + [jnp.zeros((8 - 2 * n, 128), F32)], axis=0)
-    spread = exact_dot(packed, one_hot((128, ch), 1, ch // GROUPS))
-    half_a = [0.5 * (spread[2 * s + 1 : 2 * s + 2] * gain) for s in range(n)]
-    half_b = [0.5 * shift - spread[2 * s : 2 * s + 1] * half_a[s] for s in range(n)]
+    if index + which < 2:
+        total = stats_ref[0]
+        for i in range(1, n_space):
+            total = total + stats_ref[i]
+        packed = []
+        for s in range(n):
+            mean = total[2 * s : 2 * s + 1] * (1.0 / members)
+            var = jnp.maximum(total[2 * s + 1 : 2 * s + 2] * (1.0 / members) - mean * mean, 0.0)
+            packed += [mean, lax.rsqrt(var + 1e-05)]
+        packed = jnp.concatenate(packed + [jnp.zeros((8 - 2 * n, 128), F32)], axis=0)
+        spread = exact_dot(packed, one_hot((128, ch), 1, ch // GROUPS))
+        half_a = [0.5 * (spread[2 * s + 1 : 2 * s + 2] * gain) for s in range(n)]
+        half_b = [0.5 * shift - spread[2 * s : 2 * s + 1] * half_a[s] for s in range(n)]
 
     def normalize(s, j):
         if j == 0:
@@ -190,16 +194,16 @@
             y = jnp.where(space == 0, 0.0, y)
         if j == padded_rows - 1:
             y = jnp.where(space == n_space - 1, 0.0, y)
-        xm[s, pl.ds(j * cols, cols), :] = y[:, 0:256].astype(BF16)
+        planes[s][0][pl.ds(j * cols, cols), :] = y[:, 0:256].astype(BF16)
         rem_buf[s, j] = y[:, 256:ch]
         if j >= 2:
             parts = [rem_buf[s, j - 2], rem_buf[s, j - 1], rem_buf[s, j], jnp.zeros((cols, 256 - 3 * rem), F32)]
-            xr[s, pl.ds((j - 2) * cols, cols), :] = jnp.concatenate(parts, axis=1).astype(BF16)
+            planes[s][1][pl.ds((j - 2) * cols, cols), :] = jnp.concatenate(parts, axis=1).astype(BF16)
 
     def multiply(s, r0, count, slot):
         m = count * cols
         lhs = jnp.concatenate(
-            [xm[s, pl.ds((r0 + dr) * cols, m), :] for dr in range(3)] + [xr[s, pl.ds(r0 * cols, m), :]],
+            [planes[s][0][pl.ds((r0 + dr) * cols, m), :] for dr in range(3)] + [planes[s][1][pl.ds(r0 * cols, m), :]],
             axis=1,
         )
         z_buf[slot, 0:m, :] = jnp.dot(lhs, w_ref[...], preferred_element_type=F32)
@@ -251,6 +255,8 @@
 
     def prepare(task):
         s, r0, count = task
+        if index + which == 2:
+            return
         while done[s] < r0 + count + 2:
             normalize(s, done[s])
             done[s] += 1
@@ -271,11 +277,10 @@
             if k > 0:
                 complete(k - 1)
     else:
-        for k in range(early):
-            prepare(tasks[k])
-    if index == 1 and which == 0:
-        kernel_load.wait()
-        lay_out(src, 0, w_ref)
+        for s in range(n) if which == 0 else ():
+            for j in range(padded_rows):
+                normalize(s, j)
+            done[s] = padded_rows
     for cp in loads:
         cp.wait()
     for k, task in enumerate(tasks):
@@ -327,7 +332,10 @@
     n_space = lax.axis_size("space")
     members = rows * n_space * cols * (ch // GROUPS)
     pairs_a = [(i, i ^ 1) for i in range(n_space)]
-    pairs_b = [(i, (i - 1) % n_space if i % 2 == 0 else (i + 1) % n_space) for i in range(n_space)]
+    pairs_b = []
+    for c in range(lax.axis_size("section")):
+        pairs_b += [(c * n_space + e, (1 - c) * n_space + e) for e in (0, n_space - 1)]
+        pairs_b += [(c * n_space + i, c * n_space + (i - 1 if i % 2 == 0 else i + 1)) for i in range(1, n_space - 1)]
     shape = jax.ShapeDtypeStruct
     stats_shape = pltpu.VMEM((n_space, 8, 128), F32)
     edge_shape = pltpu.VMEM((n, cols, ch), BF16)
@@ -353,50 +361,52 @@
         name="stats",
     )(latents)
     ra = lax.ppermute(ha, "space", pairs_a)
-    rb = lax.ppermute(hb, "space", pairs_b)
+    rb = lax.ppermute(hb, ("section", "space"), pairs_b)
     stats = lax.all_to_all(stats, "space", split_axis=0, concat_axis=0, tiled=True)
 
     head = HEAD
     w_type = (1024, 1024)
 
-    head_ref, w0 = pl.pallas_call(
+    head_ref, w0, w1 = pl.pallas_call(
         prepare_kernel,
-        out_shape=(pltpu.VMEM((head, cols, ch), BF16), pltpu.VMEM(w_type, BF16)),
+        out_shape=(pltpu.VMEM((head, cols, ch), BF16), pltpu.VMEM(w_type, BF16), pltpu.HBM(w_type, BF16)),
         in_specs=[HBM, HBM, HBM],
-        out_specs=(VM, VM),
-        scratch_shapes=[pltpu.VMEM(kernels.shape, BF16), pltpu.SemaphoreType.DMA((2,))],
+        out_specs=(VM, VM, HBM),
+        scratch_shapes=[
+            pltpu.VMEM((2, *kernels.shape[1:]), BF16),
+            pltpu.VMEM(w_type, BF16),
+            pltpu.SemaphoreType.DMA((4,)),
+        ],
         compiler_params=pltpu.CompilerParams(vmem_limit_bytes=16 * 1024 * 1024),
         name="prepare",
-    )(kernels, other_k, latents)
+    )(latents, kernels, other_k)
+    w1 = pltpu.with_memory_space_constraint(w1, pltpu.HBM)
 
     chunks = CHUNKS
     most = max(max(c) for c in chunks)
 
     def conv(index, which, operands, out_shape):
         body = lambda *refs: conv_kernel(index, which, members, n_space, chunks, *refs)
-        in_hbm = (1, 3, 0)[index + which]
-        if index == 0:
-            extra = [pltpu.VMEM((n, rows, cols, ch), BF16), pltpu.SemaphoreType.DMA((n,))]
-        elif which == 0:
-            extra = [
-                pltpu.VMEM((1, rows, cols, ch), BF16),
+        in_hbm = (1, 2, 0)[index + which]
+        z_type = pltpu.VMEM((2, most * cols, 1024), F32)
+        if index + which < 2:
+            held = n if index == 0 else 1
+            scratch = [
+                pltpu.VMEM((held, (rows + 2) * cols, 256), BF16),
+                pltpu.VMEM((held, rows * cols, 256), BF16),
+                pltpu.VMEM((n, rows + 2, cols, ch - 256), F32),
+                z_type,
+                pltpu.VMEM((held, rows, cols, ch), BF16),
                 pltpu.SemaphoreType.DMA((3,)),
-                pltpu.VMEM(kernels.shape, BF16),
             ]
         else:
-            extra = []
+            scratch = [z_type]
         return pl.pallas_call(
             body,
             out_shape=out_shape,
             in_specs=[VM] * (len(operands) - in_hbm) + [HBM] * in_hbm,
             out_specs=(VM,) * len(out_shape),
-            scratch_shapes=[
-                pltpu.VMEM((n, (rows + 2) * cols, 256), BF16),
-                pltpu.VMEM((n, rows * cols, 256), BF16),
-                pltpu.VMEM((n, rows + 2, cols, ch - 256), F32),
-                pltpu.VMEM((2, most * cols, 1024), F32),
-                *extra,
-            ],
+            scratch_shapes=scratch,
             compiler_params=limit,
             name="conv%d%d" % (index, which),
         )(*operands)
@@ -408,16 +418,20 @@
         (pltpu.VMEM(part_shape.shape, BF16), stats_shape, edge_shape, edge_shape),
     )
     ra = lax.ppermute(ha, "space", pairs_a)
-    rb = lax.ppermute(hb, "space", pairs_b)
+    rb = lax.ppermute(hb, ("section", "space"), pairs_b)
     stats = lax.all_to_all(stats, "space", split_axis=0, concat_axis=0, tiled=True)
     full_shape = shape((samples, rows, cols, ch), BF16)
     common = (ra, rb, stats, own_p, other_p, first)
     sample_shape = pltpu.VMEM((rows, cols, ch), BF16)
-    send_0, keep_0, w1, lat_next = conv(
-        1, 0, (*common, kernels, other_k, latents), (sample_shape, sample_shape, pltpu.VMEM(w_type, BF16), sample_shape)
+    plane_shapes = (pltpu.VMEM(((rows + 2) * cols, 256), BF16), pltpu.VMEM((rows * cols, 256), BF16))
+    send_0, keep_0, *rest = conv(
+        1,
+        0,
+        (*common, w1, latents),
+        (sample_shape, sample_shape, pltpu.VMEM(w_type, BF16), sample_shape, *plane_shapes),
     )
     received_0 = swap(send_0)
-    send_1, keep_1 = conv(1, 1, (*common, w1, lat_next), (sample_shape, sample_shape))
+    send_1, keep_1 = conv(1, 1, (own_p, other_p, first, *rest), (sample_shape, sample_shape))
     received_1 = swap(send_1)
     small = pltpu.CompilerParams(vmem_limit_bytes=1024 * 1024)
     full = pl.pallas_call(

time: 55.4 us -> 54.3 us (0.980)
  waiting for transfers between devices: 4.6 us -> 3.15 us
  Pallas kernels: 22.2 us -> 23 us
  starting transfers between devices: 17.9 us -> 17.3 us
    ppermute x2, starting transfers between devices: 6.19 us -> 2.16 us  [on_device(): rb = lax.ppermute(hb, ('section', 'space'), pairs_b)]
    all_to_all x1, starting transfers between devices: 3.49 us -> 6.86 us  [on_device(): lax.all_to_all(stats, 'space', split_axis=0, concat_axis=0, tiled=True)]
    all_to_all x1, waiting for transfers between devices: 3.72 us -> 2.27 us  [on_device(): lax.all_to_all(stats, 'space', split_axis=0, concat_axis=0, tiled=True)]
    pallas_call x1, Pallas kernels: 1.99 us -> 3.27 us  [on_device(): pl.pallas_call(prepare_kernel, out_shape=(pltpu.VMEM((head, cols, ch), BF...]
  transfers between devices with their start and end apart: 9 -> 9, of which waited for: 2 -> 2; matrix products, arithmetic and copies ran while one was open for 0% -> 0% of each run, Pallas kernels for 17% -> 19%
where the time goes in v5:
time: 54.3 us; the launch traced here: 54 us
  Pallas kernels  23 us (42%)
  starting transfers between devices  17.3 us (32%)
  blocking collectives  10.2 us (19%)
  waiting for transfers between devices  3.15 us (6%)
    pallas_call x3, Pallas kernels, conv(): pl.pallas_call(body, out_shape=out_shape, in_specs=[VM] * (len(operands)...  14.7 us
    all_to_all x1, blocking collectives, on_device(): lax.all_to_all(stats, 'space', split_axis=0, concat_axis=0, tiled=True)  10.2 us
    ppermute x4, starting transfers between devices, swap(): return lax.ppermute(array, 'section', [(0, 1), (1, 0)])  7.64 us
    all_to_all x1, starting transfers between devices, on_device(): lax.all_to_all(stats, 'space', split_axis=0, concat_axis=0, tiled=True)  6.86 us
    pallas_call x1, Pallas kernels, on_device(): pl.pallas_call(prepare_kernel, out_shape=(pltpu.VMEM((head, cols, ch), BF...  3.27 us
    pallas_call x1, Pallas kernels, on_device(): pl.pallas_call(stats_kernel, out_shape=(stats_shape, edge_shape, edge_sha...  2.58 us
    all_to_all x1, waiting for transfers between devices, on_device(): lax.all_to_all(stats, 'space', split_axis=0, concat_axis=0, tiled=True)  2.27 us
    ppermute x2, starting transfers between devices, on_device(): rb = lax.ppermute(hb, ('section', 'space'), pairs_b)  2.16 us
  transfers between devices with their start and end apart: 9, of which 2 were waited for; matrix products, arithmetic and copies ran while one was open for 0% of the time, Pallas kernels for 19%

profile of v5, /device:TPU:1, one launch (start us, length us, event | category | flops | bytes accessed | tf_op | source)
XLA Modules:
  0.0 54.0 jit_solution(11097275038644179143)
XLA Ops:
  0.0 0.0 copy-start
  0.0 0.0 copy-start.1
  0.0 0.0 copy-start.2
  0.0 3.2 %collective-permute-start.3 = (bf16[1,3,3,320,320]{4,3,2,1,0:T(8,128)(2,1)}, bf16[1,3,3,320,320]{4,3,2,1,0:T(8,128)(2,1)}, u32[]{:S(2)}, u32[]{:S(2)}) collective-permute-start(bf16[1,3,3,320,320]{4,3,2,1,0:T(8,128)(2,1)} %own_k.1), channel_id=1, source_target_pairs={{0,16},{16,0},{1,17},{17,1},{2,18},{18,2},{3,19},{19,3},{4,20},{20... | collective-permute-start | bytes 5529608 | tf_op jit(solution)/shard_map/ppermute | solution.py:326
  3.2 2.6 %stats.1 = (f32[16,8,128]{2,1,0:T(8,128)}, bf16[2,192,320]{2,1,0:T(8,128)(2,1)}, bf16[2,192,320]{2,1,0:T(8,128)(2,1)}) custom-call(bf16[4,6,192,320]{3,2,1,0:T(8,128)(2,1)} %refs_7_.3), custom_call_target="tpu_custom_call" | custom-call | tf_op jit(solution)/shard_map/stats/pallas_call | solution.py:351
  5.8 0.1 collective-permute-start
  5.9 0.1 collective-permute-start.1
  6.0 6.9 %all-to-all-start = ((f32[16,8,128]{2,1,0:T(8,128)}), f32[16,8,128]{2,1,0:T(8,128)S(1)}, u32[]{:S(2)}, u32[]{:S(2)}) async-start(f32[16,8,128]{2,1,0:T(8,128)} %get-tuple-element.25), calls=%async_computation | async-start | bytes 131072 | tf_op jit(solution)/shard_map/all_to_all | solution.py:365
  12.9 0.0 copy-done
  12.9 0.0 copy-done.1
  12.9 0.0 copy-done.2
  12.9 1.0 %collective-permute-start.2 = (f32[3,320]{1,0:T(4,128)S(1)}, f32[3,320]{1,0:T(4,128)S(1)}, u32[]{:S(2)}, u32[]{:S(2)}) collective-permute-start(f32[3,320]{1,0:T(4,128)S(1)} %pad_maximum_fusion.refs_3_.refs_0_), channel_id=1, source_target_pairs={{0,16},{16,0},{1,17},{17,1},{2,18},{18,2},{3,19},{19,3},{4,20},{20... | collective-permute-start | bytes 11528 | tf_op jit(solution)/shard_map/ppermute | solution.py:326
  13.9 0.0 collective-permute-done.3.other_k
  13.9 3.3 %prepare.1 = (bf16[5,192,320]{2,1,0:T(8,128)(2,1)S(1)}, bf16[1024,1024]{1,0:T(8,128)(2,1)S(1)}, bf16[1024,1024]{1,0:T(8,128)(2,1)}) custom-call(bf16[4,6,192,320]{3,2,1,0:T(8,128)(2,1)} %refs_7_.3, bf16[1,3,3,320,320]{4,3,2,1,0:T(8,128)(2,1)} %own_k.1, bf16[1,3,3,320,320]{4,3,2,1,0:T(8,128)(2,1)} %collective-permute-done.3.other_k), custom_call_target="tpu_custom_call" | custom-call | tf_op jit(solution)/shard_map/prepare/pallas_call | solution.py:370
  17.2 0.0 collective-permute-done.2.refs_4_.refs_1_
  17.2 2.3 %all-to-all-done.refs_2_ = f32[16,8,128]{2,1,0:T(8,128)S(1)} async-done(((f32[16,8,128]{2,1,0:T(8,128)}), f32[16,8,128]{2,1,0:T(8,128)S(1)}, u32[]{:S(2)}, u32[]{:S(2)}) %all-to-all-start) | async-done | bytes 65568 | tf_op jit(solution)/shard_map/all_to_all | solution.py:365
  19.5 0.0 collective-permute-done.refs_0_
  19.5 0.0 collective-permute-done.1.refs_1_
  19.5 6.9 %conv00.1 = (bf16[2,6,192,320]{3,2,1,0:T(8,128)(2,1)S(1)}, f32[16,8,128]{2,1,0:T(8,128)S(1)}, bf16[2,192,320]{2,1,0:T(8,128)(2,1)S(1)}, bf16[2,192,320]{2,1,0:T(8,128)(2,1)S(1)}) custom-call(bf16[2,192,320]{2,1,0:T(8,128)(2,1)S(1)} %collective-permute-done.refs_0_, bf16[2,192,320]{2,1,0:T(8,128)(2,1)S(1)} %collective-permute-done.1.refs_1_, ...), custom_call_target="tpu_custom_call" | custom-call | tf_op jit(solution)/shard_map/conv00/pallas_call | solution.py:404
  26.3 0.6 %collective-permute-start.4 = (bf16[2,192,320]{2,1,0:T(8,128)(2,1)S(1)}, bf16[2,192,320]{2,1,0:T(8,128)(2,1)S(1)}, u32[]{:S(2)}, u32[]{:S(2)}) collective-permute-start(bf16[2,192,320]{2,1,0:T(8,128)(2,1)S(1)} %get-tuple-element.28), channel_id=1, source_target_pairs={{0,1},{1,0},{2,3},{3,2},{4,5},{5,4},{6,7},{7,6},{8,9},{9,8},{10,11... | collective-permute-start | bytes 737288 | tf_op jit(solution)/shard_map/ppermute | solution.py:420
  26.9 2.0 %collective-permute-start.5 = (bf16[2,192,320]{2,1,0:T(8,128)(2,1)S(1)}, bf16[2,192,320]{2,1,0:T(8,128)(2,1)S(1)}, u32[]{:S(2)}, u32[]{:S(2)}) collective-permute-start(bf16[2,192,320]{2,1,0:T(8,128)(2,1)S(1)} %get-tuple-element.29), channel_id=1, source_target_pairs={{0,16},{15,31},{1,2},{2,1},{3,4},{4,3},{5,6},{6,5},{7,8},{8,7},{9,... | collective-permute-start | bytes 737288 | tf_op jit(solution)/shard_map/ppermute | solution.py:421
  28.9 10.2 %all_to_all.10.refs_2_ = f32[16,8,128]{2,1,0:T(8,128)S(1)} all-to-all(f32[16,8,128]{2,1,0:T(8,128)S(1)} %get-tuple-element.30), channel_id=1, replica_groups=mesh['dp'=8,'section'=2,'space'=16] {'space'}, dimensions={0} | all-to-all | bytes 131072 | tf_op jit(solution)/shard_map/all_to_all | solution.py:422
  39.2 0.0 collective-permute-done.4.refs_0_
  39.2 0.0 collective-permute-done.5.refs_1_
  39.2 4.9 %conv10.1 = (bf16[6,192,320]{2,1,0:T(8,128)(2,1)S(1)}, bf16[6,192,320]{2,1,0:T(8,128)(2,1)S(1)}, bf16[1024,1024]{1,0:T(8,128)(2,1)S(1)}, bf16[6,192,320]{2,1,0:T...) custom-call(bf16[2,192,320]{2,1,0:T(8,128)(2,1)S(1)} %collective-permute-done.4.refs_0_, ...), custom_call_target="tpu_custom_call" | custom-call | tf_op jit(solution)/shard_map/conv10/pallas_call | solution.py:404
  44.1 3.4 %collective-permute-start.6 = (bf16[6,192,320]{2,1,0:T(8,128)(2,1)S(1)}, bf16[6,192,320]{2,1,0:T(8,128)(2,1)S(1)}, u32[]{:S(2)}, u32[]{:S(2)}) collective-permute-start(bf16[6,192,320]{2,1,0:T(8,128)(2,1)S(1)} %get-tuple-element.39), channel_id=1, source_target_pairs={{0,16},{16,0},{1,17},{17,1},{2,18},{18,2},{3,19},{19,3},{4,20},{20... | collective-permute-start | bytes 2211848 | tf_op jit(solution)/shard_map/ppermute | solution.py:326
  47.5 2.9 %conv11.1 = (bf16[6,192,320]{2,1,0:T(8,128)(2,1)S(1)}, bf16[6,192,320]{2,1,0:T(8,128)(2,1)S(1)}) custom-call(f32[3,320]{1,0:T(4,128)S(1)} %pad_maximum_fusion.refs_3_.refs_0_, f32[3,320]{1,0:T(4,128)S(1)} %collective-permute-done.2.refs_4_.refs_1_, bf16[2,6,192,320]{3,2,1,0:T(8,128)(2,1)S(1)} %get-tuple-element.31.refs_5_.refs_2_, ...), custom_call_target="tpu_custom_call" | custom-call | tf_op jit(solution)/shard_map/conv11/pallas_call | solution.py:404
  50.4 0.1 collective-permute-start.7
  50.5 0.0 collective-permute-done.6.received
  50.6 1.5 %keep.1.full_in = bf16[4,6,192,320]{3,2,1,0:T(8,128)(2,1)} custom-call(bf16[6,192,320]{2,1,0:T(8,128)(2,1)S(1)} %get-tuple-element.33.keep_0, bf16[6,192,320]{2,1,0:T(8,128)(2,1)S(1)} %get-tuple-element.38.keep_1, bf16[6,192,320]{2,1,0:T(8,128)(2,1)S(1)} %collective-permute-done.6.received), custom_call_target="tpu_custom_call" | custom-call | tf_op jit(solution)/shard_map/keep/pallas_call | solution.py:437
  52.1 0.9 %collective-permute-done.7.received = bf16[6,192,320]{2,1,0:T(8,128)(2,1)S(1)} collective-permute-done((bf16[6,192,320]{2,1,0:T(8,128)(2,1)S(1)}, bf16[6,192,320]{2,1,0:T(8,128)(2,1)S(1)}, u32[]{:S(2)}, u32[]{:S(2)}) %collective-permute-start.7) | collective-permute-done | bytes 737312 | tf_op jit(solution)/shard_map/ppermute | solution.py:326
  53.0 0.9 %finish.1 = bf16[4,6,192,320]{3,2,1,0:T(8,128)(2,1)} custom-call(bf16[4,6,192,320]{3,2,1,0:T(8,128)(2,1)} %keep.1.full_in, bf16[6,192,320]{2,1,0:T(8,128)(2,1)S(1)} %collective-permute-done.7.received), custom_call_target="tpu_custom_call", output_to_operand_aliasing={{}: (0, {})} | custom-call | tf_op jit(solution)/shard_map/finish/pallas_call | solution.py:446
  (1 shorter events, 0.0 us)
Async XLA Ops:
  0.0 12.9 %copy-start = (f32[1,320]{1,0:T(1,128)S(1)}, f32[1,320]{1,0:T(1,128)}, u32[]{:S(2)}) copy-start(f32[1,320]{1,0:T(1,128)} %param.9) | copy-start | bytes 3844
  0.0 12.9 %copy-start.1 = (f32[1,320]{1,0:T(1,128)S(1)}, f32[1,320]{1,0:T(1,128)}, u32[]{:S(2)}) copy-start(f32[1,320]{1,0:T(1,128)} %param.8) | copy-start | bytes 3844
  0.0 12.9 %copy-start.2 = (f32[1,320]{1,0:T(1,128)S(1)}, f32[1,320]{1,0:T(1,128)}, u32[]{:S(2)}) copy-start(f32[1,320]{1,0:T(1,128)} %param.7) | copy-start | bytes 3844
  0.0 13.9 %collective-permute-start.3 = (bf16[1,3,3,320,320]{4,3,2,1,0:T(8,128)(2,1)}, bf16[1,3,3,320,320]{4,3,2,1,0:T(8,128)(2,1)}, u32[]{:S(2)}, u32[]{:S(2)}) collective-permute-start(bf16[1,3,3,320,320]{4,3,2,1,0:T(8,128)(2,1)} %own_k.1), channel_id=1, source_target_pairs={{0,16},{16,0},{1,17},{17,1},{2,18},{18,2},{3,19},{19,3},{4,20},{20... | collective-permute-start | bytes 5529608 | tf_op jit(solution)/shard_map/ppermute | solution.py:326
  5.8 13.7 %collective-permute-start = (bf16[2,192,320]{2,1,0:T(8,128)(2,1)}, bf16[2,192,320]{2,1,0:T(8,128)(2,1)S(1)}, u32[]{:S(2)}, u32[]{:S(2)}) collective-permute-start(bf16[2,192,320]{2,1,0:T(8,128)(2,1)} %get-tuple-element.23), channel_id=1, source_target_pairs={{0,1},{1,0},{2,3},{3,2},{4,5},{5,4},{6,7},{7,6},{8,9},{9,8},{10,11... | collective-permute-start | bytes 737288 | tf_op jit(solution)/shard_map/ppermute | solution.py:363
  5.9 13.6 %collective-permute-start.1 = (bf16[2,192,320]{2,1,0:T(8,128)(2,1)}, bf16[2,192,320]{2,1,0:T(8,128)(2,1)S(1)}, u32[]{:S(2)}, u32[]{:S(2)}) collective-permute-start(bf16[2,192,320]{2,1,0:T(8,128)(2,1)} %get-tuple-element.24), channel_id=1, source_target_pairs={{0,16},{15,31},{1,2},{2,1},{3,4},{4,3},{5,6},{6,5},{7,8},{8,7},{9,... | collective-permute-start | bytes 737288 | tf_op jit(solution)/shard_map/ppermute | solution.py:364
  6.0 13.4 %all-to-all-start = ((f32[16,8,128]{2,1,0:T(8,128)}), f32[16,8,128]{2,1,0:T(8,128)S(1)}, u32[]{:S(2)}, u32[]{:S(2)}) async-start(f32[16,8,128]{2,1,0:T(8,128)} %get-tuple-element.25), calls=%async_computation | async-start | bytes 131072 | tf_op jit(solution)/shard_map/all_to_all | solution.py:365
  12.9 4.2 %collective-permute-start.2 = (f32[3,320]{1,0:T(4,128)S(1)}, f32[3,320]{1,0:T(4,128)S(1)}, u32[]{:S(2)}, u32[]{:S(2)}) collective-permute-start(f32[3,320]{1,0:T(4,128)S(1)} %pad_maximum_fusion.refs_3_.refs_0_), channel_id=1, source_target_pairs={{0,16},{16,0},{1,17},{17,1},{2,18},{18,2},{3,19},{19,3},{4,20},{20... | collective-permute-start | bytes 11528 | tf_op jit(solution)/shard_map/ppermute | solution.py:326
  26.3 12.8 %collective-permute-start.4 = (bf16[2,192,320]{2,1,0:T(8,128)(2,1)S(1)}, bf16[2,192,320]{2,1,0:T(8,128)(2,1)S(1)}, u32[]{:S(2)}, u32[]{:S(2)}) collective-permute-start(bf16[2,192,320]{2,1,0:T(8,128)(2,1)S(1)} %get-tuple-element.28), channel_id=1, source_target_pairs={{0,1},{1,0},{2,3},{3,2},{4,5},{5,4},{6,7},{7,6},{8,9},{9,8},{10,11... | collective-permute-start | bytes 737288 | tf_op jit(solution)/shard_map/ppermute | solution.py:420
  26.9 12.3 %collective-permute-start.5 = (bf16[2,192,320]{2,1,0:T(8,128)(2,1)S(1)}, bf16[2,192,320]{2,1,0:T(8,128)(2,1)S(1)}, u32[]{:S(2)}, u32[]{:S(2)}) collective-permute-start(bf16[2,192,320]{2,1,0:T(8,128)(2,1)S(1)} %get-tuple-element.29), channel_id=1, source_target_pairs={{0,16},{15,31},{1,2},{2,1},{3,4},{4,3},{5,6},{6,5},{7,8},{8,7},{9,... | collective-permute-start | bytes 737288 | tf_op jit(solution)/shard_map/ppermute | solution.py:421
  44.1 6.4 %collective-permute-start.6 = (bf16[6,192,320]{2,1,0:T(8,128)(2,1)S(1)}, bf16[6,192,320]{2,1,0:T(8,128)(2,1)S(1)}, u32[]{:S(2)}, u32[]{:S(2)}) collective-permute-start(bf16[6,192,320]{2,1,0:T(8,128)(2,1)S(1)} %get-tuple-element.39), channel_id=1, source_target_pairs={{0,16},{16,0},{1,17},{17,1},{2,18},{18,2},{3,19},{19,3},{4,20},{20... | collective-permute-start | bytes 2211848 | tf_op jit(solution)/shard_map/ppermute | solution.py:326
  50.4 2.5 %collective-permute-start.7 = (bf16[6,192,320]{2,1,0:T(8,128)(2,1)S(1)}, bf16[6,192,320]{2,1,0:T(8,128)(2,1)S(1)}, u32[]{:S(2)}, u32[]{:S(2)}) collective-permute-start(bf16[6,192,320]{2,1,0:T(8,128)(2,1)S(1)} %get-tuple-element.40), channel_id=1, source_target_pairs={{0,16},{16,0},{1,17},{17,1},{2,18},{18,2},{3,19},{19,3},{4,20},{20... | collective-permute-start | bytes 2211848 | tf_op jit(solution)/shard_map/ppermute | solution.py:326

commit v6 on v5

--- a/solution.py
+++ b/solution.py
@@ -6,9 +6,10 @@
 from jax.sharding import PartitionSpec as P
 
 GROUPS = 32
+MORE = 2
 HEAD = 5
 EARLY = (2, 3, 1)
-CHUNKS = ((2, 2, 2), (3, 3))
+CHUNKS = ((2, 2, 2), (2, 2, 2))
 F32 = jnp.float32
 BF16 = jnp.bfloat16
 ANY = pl.BlockSpec(memory_space=pl.ANY)
@@ -136,7 +137,7 @@
         loads = []
         planes = [None, (xm_next, xr_next)]
     n, rows, cols, ch = lat_buf.shape if index == 0 else x_ref.shape
-    chosen = range(n) if index == 0 else (which,)
+    chosen = range(n)
     padded_rows = rows + 2
     rem = ch - 256
     sec = lax.axis_index("section")
@@ -152,6 +153,8 @@
             )
     elif which == 0:
         loads.append(pltpu.make_async_copy(lat_hbm.at[sec * n], lat_buf.at[0], sem.at[0]))
+        more = pl.ds(0, MORE)
+        loads.append(pltpu.make_async_copy(lat_hbm.at[sec * n + 1, more], lat_buf.at[1, more], sem.at[3]))
         next_load = pltpu.make_async_copy(lat_hbm.at[sec * n + 1], lat_next, sem.at[1])
     for cp in loads:
         cp.start()
@@ -231,7 +234,7 @@
         side = down(left, 128) + pltpu.roll(left, 64, 1) + up(right, 128)
         out = jnp.concatenate([main, side[:, 0:rem]], axis=1) + bias
         if index == 1:
-            out = out + (lat_buf[0, r] if which == 0 else lat_next[r]).astype(F32)
+            out = out + (lat_buf[s, r] if which == 0 else lat_next[r]).astype(F32)
         rounded = out.astype(BF16)
         if index == 0:
             y_out[s, r] = rounded
@@ -240,17 +243,18 @@
             acc[s][1] = acc[s][1] + fold_rows(back * back)
         else:
             kept = source_row(s, r)
-            send_out[r] = jnp.where(sec == 0, rounded, kept)
-            keep_out[r] = jnp.where(sec == 0, kept, rounded)
+            place = s * rows + r if which == 0 else r - MORE
+            send_out[place] = jnp.where(sec == 0, rounded, kept)
+            keep_out[place] = jnp.where(sec == 0, kept, rounded)
 
     row_a = jnp.where(even, rows - 1, 0)
     tasks = []
     for s in chosen:
         r0 = 0
         for count in chunks[s]:
-            tasks.append((s, r0, count))
+            if index == 0 or (s == 0 or r0 < MORE) == (which == 0):
+                tasks.append((s, r0, count))
             r0 += count
-    pending = None
     done = [0] * n
 
     def prepare(task):
@@ -304,11 +308,16 @@
 
 
 def keep_kernel(keep_0, keep_1, received, full_out, sem):
-    sec = lax.axis_index("section")
+    rows = full_out.shape[1]
+    own = 2 * lax.axis_index("section")
+    head, more, rest = pl.ds(0, rows), pl.ds(rows, MORE), pl.ds(MORE, rows - MORE)
+    top = pl.ds(0, MORE)
     copies = [
-        pltpu.make_async_copy(keep_0, full_out.at[2 * sec], sem.at[0]),
-        pltpu.make_async_copy(keep_1, full_out.at[2 * sec + 1], sem.at[1]),
-        pltpu.make_async_copy(received, full_out.at[2 - 2 * sec], sem.at[2]),
+        pltpu.make_async_copy(keep_0.at[head], full_out.at[own], sem.at[0]),
+        pltpu.make_async_copy(keep_0.at[more], full_out.at[own + 1, top], sem.at[1]),
+        pltpu.make_async_copy(keep_1, full_out.at[own + 1, rest], sem.at[2]),
+        pltpu.make_async_copy(received.at[head], full_out.at[2 - own], sem.at[3]),
+        pltpu.make_async_copy(received.at[more], full_out.at[3 - own, top], sem.at[4]),
     ]
     for cp in copies:
         cp.start()
@@ -317,7 +326,8 @@
 
 
 def finish_kernel(full_in, received, full_out, sem):
-    cp = pltpu.make_async_copy(received, full_out.at[3 - 2 * lax.axis_index("section")], sem)
+    rest = pl.ds(MORE, full_out.shape[1] - MORE)
+    cp = pltpu.make_async_copy(received, full_out.at[3 - 2 * lax.axis_index("section"), rest], sem)
     cp.start()
     cp.wait()
 
@@ -396,8 +406,8 @@
                 pltpu.VMEM((held, rows * cols, 256), BF16),
                 pltpu.VMEM((n, rows + 2, cols, ch - 256), F32),
                 z_type,
-                pltpu.VMEM((held, rows, cols, ch), BF16),
-                pltpu.SemaphoreType.DMA((3,)),
+                pltpu.VMEM((n, rows, cols, ch), BF16),
+                pltpu.SemaphoreType.DMA((4,)),
             ]
         else:
             scratch = [z_type]
@@ -423,15 +433,17 @@
     full_shape = shape((samples, rows, cols, ch), BF16)
     common = (ra, rb, stats, own_p, other_p, first)
     sample_shape = pltpu.VMEM((rows, cols, ch), BF16)
+    large = pltpu.VMEM((rows + MORE, cols, ch), BF16)
+    little = pltpu.VMEM((rows - MORE, cols, ch), BF16)
     plane_shapes = (pltpu.VMEM(((rows + 2) * cols, 256), BF16), pltpu.VMEM((rows * cols, 256), BF16))
     send_0, keep_0, *rest = conv(
         1,
         0,
         (*common, w1, latents),
-        (sample_shape, sample_shape, pltpu.VMEM(w_type, BF16), sample_shape, *plane_shapes),
+        (large, large, pltpu.VMEM(w_type, BF16), sample_shape, *plane_shapes),
     )
     received_0 = swap(send_0)
-    send_1, keep_1 = conv(1, 1, (own_p, other_p, first, *rest), (sample_shape, sample_shape))
+    send_1, keep_1 = conv(1, 1, (own_p, other_p, first, *rest), (little, little))
     received_1 = swap(send_1)
     small = pltpu.CompilerParams(vmem_limit_bytes=1024 * 1024)
     full = pl.pallas_call(
@@ -439,7 +451,7 @@
         out_shape=full_shape,
         in_specs=[VM, VM, VM],
         out_specs=HBM,
-        scratch_shapes=[pltpu.SemaphoreType.DMA((3,))],
+        scratch_shapes=[pltpu.SemaphoreType.DMA((5,))],
         compiler_params=small,
         name="keep",
     )(keep_0, keep_1, received_0)

time: 54.3 us -> 53.8 us (level)
  transfers between devices with their start and end apart: 9 -> 9, of which waited for: 2 -> 2; matrix products, arithmetic and copies ran while one was open for 0% -> 0% of each run, Pallas kernels for 19% -> 18%
where the time goes in v6:
time: 53.8 us; the launch traced here: 53.6 us
  Pallas kernels  23.1 us (43%)
  starting transfers between devices  17.3 us (32%)
  blocking collectives  10.2 us (19%)
  waiting for transfers between devices  2.63 us (5%)
    pallas_call x3, Pallas kernels, conv(): pl.pallas_call(body, out_shape=out_shape, in_specs=[VM] * (len(operands)...  14.8 us
    all_to_all x1, blocking collectives, on_device(): lax.all_to_all(stats, 'space', split_axis=0, concat_axis=0, tiled=True)  10.2 us
    ppermute x4, starting transfers between devices, swap(): return lax.ppermute(array, 'section', [(0, 1), (1, 0)])  7.64 us
    all_to_all x1, starting transfers between devices, on_device(): lax.all_to_all(stats, 'space', split_axis=0, concat_axis=0, tiled=True)  6.86 us
    pallas_call x1, Pallas kernels, on_device(): pl.pallas_call(prepare_kernel, out_shape=(pltpu.VMEM((head, cols, ch), BF...  3.27 us
    pallas_call x1, Pallas kernels, on_device(): pl.pallas_call(stats_kernel, out_shape=(stats_shape, edge_shape, edge_sha...  2.58 us
    all_to_all x1, waiting for transfers between devices, on_device(): lax.all_to_all(stats, 'space', split_axis=0, concat_axis=0, tiled=True)  2.27 us
    ppermute x2, starting transfers between devices, on_device(): rb = lax.ppermute(hb, ('section', 'space'), pairs_b)  2.16 us
  transfers between devices with their start and end apart: 9, of which 2 were waited for; matrix products, arithmetic and copies ran while one was open for 0% of the time, Pallas kernels for 18%

profile of v6, /device:TPU:1, one launch (start us, length us, event | category | flops | bytes accessed | tf_op | source)
XLA Modules:
  0.0 53.6 jit_solution(11834640908815911211)
XLA Ops:
  0.0 0.0 copy-start
  0.0 0.0 copy-start.1
  0.0 0.0 copy-start.2
  0.0 3.2 %collective-permute-start.3 = (bf16[1,3,3,320,320]{4,3,2,1,0:T(8,128)(2,1)}, bf16[1,3,3,320,320]{4,3,2,1,0:T(8,128)(2,1)}, u32[]{:S(2)}, u32[]{:S(2)}) collective-permute-start(bf16[1,3,3,320,320]{4,3,2,1,0:T(8,128)(2,1)} %own_k.1), channel_id=1, source_target_pairs={{0,16},{16,0},{1,17},{17,1},{2,18},{18,2},{3,19},{19,3},{4,20},{20... | collective-permute-start | bytes 5529608 | tf_op jit(solution)/shard_map/ppermute | solution.py:336
  3.2 2.6 %stats.1 = (f32[16,8,128]{2,1,0:T(8,128)}, bf16[2,192,320]{2,1,0:T(8,128)(2,1)}, bf16[2,192,320]{2,1,0:T(8,128)(2,1)}) custom-call(bf16[4,6,192,320]{3,2,1,0:T(8,128)(2,1)} %refs_7_.3), custom_call_target="tpu_custom_call" | custom-call | tf_op jit(solution)/shard_map/stats/pallas_call | solution.py:361
  5.8 0.1 collective-permute-start
  5.9 0.1 collective-permute-start.1
  6.0 6.9 %all-to-all-start = ((f32[16,8,128]{2,1,0:T(8,128)}), f32[16,8,128]{2,1,0:T(8,128)S(1)}, u32[]{:S(2)}, u32[]{:S(2)}) async-start(f32[16,8,128]{2,1,0:T(8,128)} %get-tuple-element.25), calls=%async_computation | async-start | bytes 131072 | tf_op jit(solution)/shard_map/all_to_all | solution.py:375
  12.9 0.0 copy-done
  12.9 0.0 copy-done.1
  12.9 0.0 copy-done.2
  12.9 1.0 %collective-permute-start.2 = (f32[3,320]{1,0:T(4,128)S(1)}, f32[3,320]{1,0:T(4,128)S(1)}, u32[]{:S(2)}, u32[]{:S(2)}) collective-permute-start(f32[3,320]{1,0:T(4,128)S(1)} %pad_maximum_fusion.refs_3_.refs_0_), channel_id=1, source_target_pairs={{0,16},{16,0},{1,17},{17,1},{2,18},{18,2},{3,19},{19,3},{4,20},{20... | collective-permute-start | bytes 11528 | tf_op jit(solution)/shard_map/ppermute | solution.py:336
  13.9 0.0 collective-permute-done.3.other_k
  13.9 3.3 %prepare.1 = (bf16[5,192,320]{2,1,0:T(8,128)(2,1)S(1)}, bf16[1024,1024]{1,0:T(8,128)(2,1)S(1)}, bf16[1024,1024]{1,0:T(8,128)(2,1)}) custom-call(bf16[4,6,192,320]{3,2,1,0:T(8,128)(2,1)} %refs_7_.3, bf16[1,3,3,320,320]{4,3,2,1,0:T(8,128)(2,1)} %own_k.1, bf16[1,3,3,320,320]{4,3,2,1,0:T(8,128)(2,1)} %collective-permute-done.3.other_k), custom_call_target="tpu_custom_call" | custom-call | tf_op jit(solution)/shard_map/prepare/pallas_call | solution.py:380
  17.2 0.0 collective-permute-done.2.refs_4_.refs_1_
  17.2 2.3 %all-to-all-done.refs_2_ = f32[16,8,128]{2,1,0:T(8,128)S(1)} async-done(((f32[16,8,128]{2,1,0:T(8,128)}), f32[16,8,128]{2,1,0:T(8,128)S(1)}, u32[]{:S(2)}, u32[]{:S(2)}) %all-to-all-start) | async-done | bytes 65568 | tf_op jit(solution)/shard_map/all_to_all | solution.py:375
  19.5 0.0 collective-permute-done.refs_0_
  19.5 0.0 collective-permute-done.1.refs_1_
  19.5 6.9 %conv00.1 = (bf16[2,6,192,320]{3,2,1,0:T(8,128)(2,1)S(1)}, f32[16,8,128]{2,1,0:T(8,128)S(1)}, bf16[2,192,320]{2,1,0:T(8,128)(2,1)S(1)}, bf16[2,192,320]{2,1,0:T(8,128)(2,1)S(1)}) custom-call(bf16[2,192,320]{2,1,0:T(8,128)(2,1)S(1)} %collective-permute-done.refs_0_, bf16[2,192,320]{2,1,0:T(8,128)(2,1)S(1)} %collective-permute-done.1.refs_1_, ...), custom_call_target="tpu_custom_call" | custom-call | tf_op jit(solution)/shard_map/conv00/pallas_call | solution.py:414
  26.3 0.6 %collective-permute-start.4 = (bf16[2,192,320]{2,1,0:T(8,128)(2,1)S(1)}, bf16[2,192,320]{2,1,0:T(8,128)(2,1)S(1)}, u32[]{:S(2)}, u32[]{:S(2)}) collective-permute-start(bf16[2,192,320]{2,1,0:T(8,128)(2,1)S(1)} %get-tuple-element.28), channel_id=1, source_target_pairs={{0,1},{1,0},{2,3},{3,2},{4,5},{5,4},{6,7},{7,6},{8,9},{9,8},{10,11... | collective-permute-start | bytes 737288 | tf_op jit(solution)/shard_map/ppermute | solution.py:430
  26.9 2.0 %collective-permute-start.5 = (bf16[2,192,320]{2,1,0:T(8,128)(2,1)S(1)}, bf16[2,192,320]{2,1,0:T(8,128)(2,1)S(1)}, u32[]{:S(2)}, u32[]{:S(2)}) collective-permute-start(bf16[2,192,320]{2,1,0:T(8,128)(2,1)S(1)} %get-tuple-element.29), channel_id=1, source_target_pairs={{0,16},{15,31},{1,2},{2,1},{3,4},{4,3},{5,6},{6,5},{7,8},{8,7},{9,... | collective-permute-start | bytes 737288 | tf_op jit(solution)/shard_map/ppermute | solution.py:431
  28.9 10.2 %all_to_all.10.refs_2_ = f32[16,8,128]{2,1,0:T(8,128)S(1)} all-to-all(f32[16,8,128]{2,1,0:T(8,128)S(1)} %get-tuple-element.30), channel_id=1, replica_groups=mesh['dp'=8,'section'=2,'space'=16] {'space'}, dimensions={0} | all-to-all | bytes 131072 | tf_op jit(solution)/shard_map/all_to_all | solution.py:432
  39.2 0.0 collective-permute-done.4.refs_0_
  39.2 0.0 collective-permute-done.5.refs_1_
  39.2 5.9 %conv10.1 = (bf16[8,192,320]{2,1,0:T(8,128)(2,1)S(1)}, bf16[8,192,320]{2,1,0:T(8,128)(2,1)S(1)}, bf16[1024,1024]{1,0:T(8,128)(2,1)S(1)}, bf16[6,192,320]{2,1,0:T...) custom-call(bf16[2,192,320]{2,1,0:T(8,128)(2,1)S(1)} %collective-permute-done.4.refs_0_, ...), custom_call_target="tpu_custom_call" | custom-call | tf_op jit(solution)/shard_map/conv10/pallas_call | solution.py:414
  45.1 3.4 %collective-permute-start.6 = (bf16[8,192,320]{2,1,0:T(8,128)(2,1)S(1)}, bf16[8,192,320]{2,1,0:T(8,128)(2,1)S(1)}, u32[]{:S(2)}, u32[]{:S(2)}) collective-permute-start(bf16[8,192,320]{2,1,0:T(8,128)(2,1)S(1)} %get-tuple-element.39), channel_id=1, source_target_pairs={{0,16},{16,0},{1,17},{17,1},{2,18},{18,2},{3,19},{19,3},{4,20},{20... | collective-permute-start | bytes 2949128 | tf_op jit(solution)/shard_map/ppermute | solution.py:336
  48.5 2.0 %conv11.1 = (bf16[4,192,320]{2,1,0:T(8,128)(2,1)S(1)}, bf16[4,192,320]{2,1,0:T(8,128)(2,1)S(1)}) custom-call(f32[3,320]{1,0:T(4,128)S(1)} %pad_maximum_fusion.refs_3_.refs_0_, f32[3,320]{1,0:T(4,128)S(1)} %collective-permute-done.2.refs_4_.refs_1_, bf16[2,6,192,320]{3,2,1,0:T(8,128)(2,1)S(1)} %get-tuple-element.31.refs_5_.refs_2_, ...), custom_call_target="tpu_custom_call" | custom-call | tf_op jit(solution)/shard_map/conv11/pallas_call | solution.py:414
  50.5 0.1 collective-permute-start.7
  50.6 0.3 collective-permute-done.6.received
  50.9 1.6 %keep.1.full_in = bf16[4,6,192,320]{3,2,1,0:T(8,128)(2,1)} custom-call(bf16[8,192,320]{2,1,0:T(8,128)(2,1)S(1)} %get-tuple-element.33.keep_0, bf16[4,192,320]{2,1,0:T(8,128)(2,1)S(1)} %get-tuple-element.38.keep_1, bf16[8,192,320]{2,1,0:T(8,128)(2,1)S(1)} %collective-permute-done.6.received), custom_call_target="tpu_custom_call" | custom-call | tf_op jit(solution)/shard_map/keep/pallas_call | solution.py:449
  52.6 0.0 collective-permute-done.7.received
  52.6 0.8 %finish.1 = bf16[4,6,192,320]{3,2,1,0:T(8,128)(2,1)} custom-call(bf16[4,6,192,320]{3,2,1,0:T(8,128)(2,1)} %keep.1.full_in, bf16[4,192,320]{2,1,0:T(8,128)(2,1)S(1)} %collective-permute-done.7.received), custom_call_target="tpu_custom_call", output_to_operand_aliasing={{}: (0, {})} | custom-call | tf_op jit(solution)/shard_map/finish/pallas_call | solution.py:458
  (1 shorter events, 0.0 us)
Async XLA Ops:
  0.0 12.9 %copy-start = (f32[1,320]{1,0:T(1,128)S(1)}, f32[1,320]{1,0:T(1,128)}, u32[]{:S(2)}) copy-start(f32[1,320]{1,0:T(1,128)} %param.9) | copy-start | bytes 3844
  0.0 12.9 %copy-start.1 = (f32[1,320]{1,0:T(1,128)S(1)}, f32[1,320]{1,0:T(1,128)}, u32[]{:S(2)}) copy-start(f32[1,320]{1,0:T(1,128)} %param.8) | copy-start | bytes 3844
  0.0 12.9 %copy-start.2 = (f32[1,320]{1,0:T(1,128)S(1)}, f32[1,320]{1,0:T(1,128)}, u32[]{:S(2)}) copy-start(f32[1,320]{1,0:T(1,128)} %param.7) | copy-start | bytes 3844
  0.0 13.9 %collective-permute-start.3 = (bf16[1,3,3,320,320]{4,3,2,1,0:T(8,128)(2,1)}, bf16[1,3,3,320,320]{4,3,2,1,0:T(8,128)(2,1)}, u32[]{:S(2)}, u32[]{:S(2)}) collective-permute-start(bf16[1,3,3,320,320]{4,3,2,1,0:T(8,128)(2,1)} %own_k.1), channel_id=1, source_target_pairs={{0,16},{16,0},{1,17},{17,1},{2,18},{18,2},{3,19},{19,3},{4,20},{20... | collective-permute-start | bytes 5529608 | tf_op jit(solution)/shard_map/ppermute | solution.py:336
  5.8 13.7 %collective-permute-start = (bf16[2,192,320]{2,1,0:T(8,128)(2,1)}, bf16[2,192,320]{2,1,0:T(8,128)(2,1)S(1)}, u32[]{:S(2)}, u32[]{:S(2)}) collective-permute-start(bf16[2,192,320]{2,1,0:T(8,128)(2,1)} %get-tuple-element.23), channel_id=1, source_target_pairs={{0,1},{1,0},{2,3},{3,2},{4,5},{5,4},{6,7},{7,6},{8,9},{9,8},{10,11... | collective-permute-start | bytes 737288 | tf_op jit(solution)/shard_map/ppermute | solution.py:373
  5.9 13.6 %collective-permute-start.1 = (bf16[2,192,320]{2,1,0:T(8,128)(2,1)}, bf16[2,192,320]{2,1,0:T(8,128)(2,1)S(1)}, u32[]{:S(2)}, u32[]{:S(2)}) collective-permute-start(bf16[2,192,320]{2,1,0:T(8,128)(2,1)} %get-tuple-element.24), channel_id=1, source_target_pairs={{0,16},{15,31},{1,2},{2,1},{3,4},{4,3},{5,6},{6,5},{7,8},{8,7},{9,... | collective-permute-start | bytes 737288 | tf_op jit(solution)/shard_map/ppermute | solution.py:374
  6.0 13.4 %all-to-all-start = ((f32[16,8,128]{2,1,0:T(8,128)}), f32[16,8,128]{2,1,0:T(8,128)S(1)}, u32[]{:S(2)}, u32[]{:S(2)}) async-start(f32[16,8,128]{2,1,0:T(8,128)} %get-tuple-element.25), calls=%async_computation | async-start | bytes 131072 | tf_op jit(solution)/shard_map/all_to_all | solution.py:375
  12.9 4.2 %collective-permute-start.2 = (f32[3,320]{1,0:T(4,128)S(1)}, f32[3,320]{1,0:T(4,128)S(1)}, u32[]{:S(2)}, u32[]{:S(2)}) collective-permute-start(f32[3,320]{1,0:T(4,128)S(1)} %pad_maximum_fusion.refs_3_.refs_0_), channel_id=1, source_target_pairs={{0,16},{16,0},{1,17},{17,1},{2,18},{18,2},{3,19},{19,3},{4,20},{20... | collective-permute-start | bytes 11528 | tf_op jit(solution)/shard_map/ppermute | solution.py:336
  26.3 12.8 %collective-permute-start.4 = (bf16[2,192,320]{2,1,0:T(8,128)(2,1)S(1)}, bf16[2,192,320]{2,1,0:T(8,128)(2,1)S(1)}, u32[]{:S(2)}, u32[]{:S(2)}) collective-permute-start(bf16[2,192,320]{2,1,0:T(8,128)(2,1)S(1)} %get-tuple-element.28), channel_id=1, source_target_pairs={{0,1},{1,0},{2,3},{3,2},{4,5},{5,4},{6,7},{7,6},{8,9},{9,8},{10,11... | collective-permute-start | bytes 737288 | tf_op jit(solution)/shard_map/ppermute | solution.py:430
  26.9 12.3 %collective-permute-start.5 = (bf16[2,192,320]{2,1,0:T(8,128)(2,1)S(1)}, bf16[2,192,320]{2,1,0:T(8,128)(2,1)S(1)}, u32[]{:S(2)}, u32[]{:S(2)}) collective-permute-start(bf16[2,192,320]{2,1,0:T(8,128)(2,1)S(1)} %get-tuple-element.29), channel_id=1, source_target_pairs={{0,16},{15,31},{1,2},{2,1},{3,4},{4,3},{5,6},{6,5},{7,8},{8,7},{9,... | collective-permute-start | bytes 737288 | tf_op jit(solution)/shard_map/ppermute | solution.py:431
  45.1 5.9 %collective-permute-start.6 = (bf16[8,192,320]{2,1,0:T(8,128)(2,1)S(1)}, bf16[8,192,320]{2,1,0:T(8,128)(2,1)S(1)}, u32[]{:S(2)}, u32[]{:S(2)}) collective-permute-start(bf16[8,192,320]{2,1,0:T(8,128)(2,1)S(1)} %get-tuple-element.39), channel_id=1, source_target_pairs={{0,16},{16,0},{1,17},{17,1},{2,18},{18,2},{3,19},{19,3},{4,20},{20... | collective-permute-start | bytes 2949128 | tf_op jit(solution)/shard_map/ppermute | solution.py:336
  50.5 2.1 %collective-permute-start.7 = (bf16[4,192,320]{2,1,0:T(8,128)(2,1)S(1)}, bf16[4,192,320]{2,1,0:T(8,128)(2,1)S(1)}, u32[]{:S(2)}, u32[]{:S(2)}) collective-permute-start(bf16[4,192,320]{2,1,0:T(8,128)(2,1)S(1)} %get-tuple-element.40), channel_id=1, source_target_pairs={{0,16},{16,0},{1,17},{17,1},{2,18},{18,2},{3,19},{19,3},{4,20},{20... | collective-permute-start | bytes 1474568 | tf_op jit(solution)/shard_map/ppermute | solution.py:336
